TPU v7x, 32 devices: a whole 2x2x4 slice. The times are simulated.
32 devices in a mesh: gx: 2 (over y), gy: 4 (over x, core), gz: 4 (over z).
Axes of the slice: x: 2, y: 2, z: 4, core: 2. Of those that a mesh axis runs over, the one named last changes fastest.
Arguments:
- rhs_velocity: float32 [3, 8, 32, 512], P(None, 'gx', 'gy', 'gz'), may hold values from -6 to 6
- rhs_pressure: float32 [8, 32, 512], P('gx', 'gy', 'gz'), may hold values from -6 to 6
- layer_ids: int32 [8, 32, 512], P('gx', 'gy', 'gz'), may hold values from 0 to 7
- visc_table: float32 [8], replicated, may hold values from 0.5 to 8
- stencil: float32 [27, 3, 3], replicated, as said below
Outputs:
- velocity_out: float32 [3, 8, 32, 512], P(None, 'gx', 'gy', 'gz')
- pressure_out: float32 [8, 32, 512], P('gx', 'gy', 'gz')
Inputs may be any that keep to these rules, and one draw needn't show every extreme that they name: The block stencil[13] has a positive diagonal that dominates its row together with all other blocks' entries.
All inputs are finite; a program needn't handle non-finite values.
Results may differ from a plain program's by a relative error of at most 0.00015.
Values sent between devices are 32-bit elements; how exact they have to be, the bound alone decides.
No kernel may reach another device: no remote copies, remote signals or barrier semaphores. Data moves between devices by JAX's collectives and lax.ppermute only.
A program may use at most 64 MiB of HBM per device.

v0:
```python
import jax
import jax.numpy as jnp
from jax import lax
from jax.sharding import PartitionSpec as P

LOW_BOUND = 0.2
HIGH_BOUND = 1.8
OMEGA = 2.0 / 3.0


def padded_2(block, sides, width):
    for axis, dim in sides:
        count = lax.axis_size(axis)
        forward = [(i, i + 1) for i in range(count - 1)]
        backward = [(target, source) for source, target in forward]
        low = lax.ppermute(
            lax.slice_in_dim(block, block.shape[dim] - width, None, axis=dim), axis, forward
        )
        high = lax.ppermute(lax.slice_in_dim(block, 0, width, axis=dim), axis, backward)
        block = jnp.concatenate([low, block, high], axis=dim)
    return block


def cheb_consts():
    theta = (HIGH_BOUND + LOW_BOUND) / 2.0
    delta = (HIGH_BOUND - LOW_BOUND) / 2.0
    sigma = theta / delta
    rho_zero = 1.0 / sigma
    rho_one = 1.0 / (2.0 * sigma - rho_zero)
    return (theta, delta, rho_zero, rho_one)


def stencil_sum(padded, stencil):
    sizes = (padded.shape[1] - 2, padded.shape[2] - 2, padded.shape[3] - 2)
    total = jnp.zeros((3,) + sizes, jnp.float32)
    for first in range(3):
        for second in range(3):
            for third in range(3):
                slab = padded[
                    :,
                    first : first + sizes[0],
                    second : second + sizes[1],
                    third : third + sizes[2],
                ]
                block = stencil[first * 9 + second * 3 + third]
                total = total + jnp.einsum(
                    "ij,jxyz->ixyz", block, slab, precision=lax.Precision.HIGHEST
                )
    return total


def lookup(layer_ids, visc_table):
    eta = jnp.zeros(layer_ids.shape, jnp.float32)
    for layer in range(visc_table.shape[0]):
        eta = eta + jnp.where(layer_ids == layer, visc_table[layer], 0.0)
    return eta


def face_sum(padded):
    beside = padded[2:, 1:-1, 1:-1] + padded[:-2, 1:-1, 1:-1]
    beside = beside + padded[1:-1, 2:, 1:-1] + padded[1:-1, :-2, 1:-1]
    beside = beside + padded[1:-1, 1:-1, 2:] + padded[1:-1, 1:-1, :-2]
    return beside


def coarsen(field):
    shape = field.shape
    blocks = field.reshape(shape[:-3] + (shape[-3] // 2, 2, shape[-2] // 2, 2, shape[-1] // 2, 2))
    count = len(shape)
    return jnp.mean(blocks, axis=(count - 2, count, count + 2))


def refine(field):
    return jnp.repeat(jnp.repeat(jnp.repeat(field, 2, axis=1), 2, axis=2), 2, axis=3)


def fine_apply(field, eta, stencil):
    padded = padded_2(field, (("gx", 1), ("gy", 2), ("gz", 3)), 1)
    return eta[None] * stencil_sum(padded, stencil)


def on_device(rhs_velocity, rhs_pressure, layer_ids, visc_table, stencil):
    theta, delta, rho_zero, rho_one = cheb_consts()
    eta = lookup(layer_ids, visc_table)
    kc = (stencil[13, 0, 0] + stencil[13, 1, 1] + stencil[13, 2, 2]) / 3.0
    dinv = 1.0 / (eta * kc)
    weight_cheb = 2.0 * rho_one / delta
    weight = 1.0 / eta
    pinv = 1.0 / (6.0 * weight)
    first = dinv[None] * rhs_velocity / theta
    resid = rhs_velocity - fine_apply(first, eta, stencil)
    second = rho_one * rho_zero * first + weight_cheb * dinv[None] * resid
    smoothed = first + second
    residual = rhs_velocity - fine_apply(smoothed, eta, stencil)
    coarse_res = coarsen(residual)
    scale_coarse = 0.25 * coarsen(eta)
    dinv_coarse = 1.0 / (scale_coarse * kc)
    coarse_first = dinv_coarse[None] * coarse_res / theta
    coarse_pad = padded_2(coarse_first, (("gx", 1), ("gy", 2), ("gz", 3)), 1)
    coarse_resid = coarse_res - scale_coarse[None] * stencil_sum(coarse_pad, stencil)
    coarse_second = (
        rho_one * rho_zero * coarse_first + weight_cheb * dinv_coarse[None] * coarse_resid
    )
    correction = coarse_first + coarse_second
    start = smoothed + refine(correction)
    resid = rhs_velocity - fine_apply(start, eta, stencil)
    first = dinv[None] * resid / theta
    middle = start + first
    resid = rhs_velocity - fine_apply(middle, eta, stencil)
    second = rho_one * rho_zero * first + weight_cheb * dinv[None] * resid
    velocity_out = middle + second
    pressure = OMEGA * pinv * rhs_pressure
    for sweep in range(2):
        padded = padded_2(pressure, (("gx", 0), ("gy", 1), ("gz", 2)), 1)
        applied = weight * (6.0 * pressure - face_sum(padded))
        pressure = pressure + OMEGA * pinv * (rhs_pressure - applied)
    return (velocity_out, pressure)


def solution(mesh):
    placed = (P(None, "gx", "gy", "gz"), P("gx", "gy", "gz"), P("gx", "gy", "gz"), P(), P())
    return jax.shard_map(
        on_device,
        mesh=mesh,
        in_specs=placed,
        out_specs=(P(None, "gx", "gy", "gz"), P("gx", "gy", "gz")),
        check_vma=False,
    )
```

profile of v0, /device:TPU:1, one launch (start us, length us, event | category | flops | bytes accessed | tf_op | source)
XLA Modules:
  0.0 207.5 jit_solution(17718716511729512360)
XLA Ops:
  0.7 1.6 fusion.519
  2.3 5.8 %fusion.333 = (f32[4,8,128]{2,1,0:T(8,128)S(1)}, f32[4,8,128]{2,1,0:T(8,128)S(1)}) fusion(f32[4,8,128]{2,1,0:T(8,128)} %param.6, f32[]{:T(128)} %bitcast.7, s32[4,8,128]{2,1,0:T(8,128)} %param.7, f32[]{:T(128)} %bitcast.6, f32[]{:T(128)} %bitcast.5, f32[]{:T(128)} %bitcast.4, f32[]{:T(128)} %bitcast.3, f32[]{:T(128)} %bitcast.2, f32[]{:T(128)} %bitcast.1, ...), kind=kLoop, calls=%fused_computation.475 | loop fusion | flops 114688 | bytes 65568 | tf_op jit(solution)/shard_map/mul | solution.py:112
  8.1 1.3 collective-permute-start.30
  9.4 4.0 %collective-permute-start.31 = (f32[1,8,128]{2,1,0:T(8,128)S(1)}, f32[1,8,128]{2,1,0:T(8,128)S(1)}, u32[]{:S(2)}, u32[]{:S(2)}) collective-permute-start(f32[1,8,128]{2,1,0:T(8,128)S(1)} %get-tuple-element.89), channel_id=1, source_target_pairs={{0,16},{1,17},{2,18},{3,19},{4,20},{5,21},{6,22},{7,23},{8,24},{9,... | collective-permute-start | bytes 12296 | tf_op jit(solution)/shard_map/ppermute | solution.py:16
  13.4 1.4 fusion.518
  17.6 1.3 collective-permute-start
  18.9 1.3 collective-permute-start.1
  20.2 1.6 slice_reduce_fusion.1
  21.9 2.8 %collective-permute-start.32 = (f32[6,1,128]{2,1,0:T(1,128)S(1)}, f32[6,1,128]{2,1,0:T(1,128)S(1)}, u32[]{:S(2)}, u32[]{:S(2)}) collective-permute-start(f32[6,1,128]{2,1,0:T(1,128)S(1)} %get-tuple-element.86), channel_id=1, source_target_pairs={{4,0},{8,4},{12,8},{5,1},{9,5},{13,9},{6,2},{10,6},{14,10},{7,3},{... | collective-permute-start | bytes 9224 | tf_op jit(solution)/shard_map/ppermute | solution.py:19
  24.8 4.1 %collective-permute-start.33 = (f32[6,1,128]{2,1,0:T(1,128)S(1)}, f32[6,1,128]{2,1,0:T(1,128)S(1)}, u32[]{:S(2)}, u32[]{:S(2)}) collective-permute-start(f32[6,1,128]{2,1,0:T(1,128)S(1)} %get-tuple-element.85), channel_id=1, source_target_pairs={{0,4},{4,8},{8,12},{1,5},{5,9},{9,13},{2,6},{6,10},{10,14},{3,7},{... | collective-permute-start | bytes 9224 | tf_op jit(solution)/shard_map/ppermute | solution.py:16
  28.9 1.1 fusion.412
  30.0 1.0 reshape.41
  31.3 1.3 collective-permute-start.34
  32.6 4.0 %collective-permute-start.35 = (f32[6,10,1]{2,1,0:T(8,128)S(1)}, f32[6,10,1]{2,1,0:T(8,128)S(1)}, u32[]{:S(2)}, u32[]{:S(2)}) collective-permute-start(f32[6,10,1]{2,1,0:T(8,128)S(1)} %get-tuple-element.76), channel_id=1, source_target_pairs={{0,1},{1,2},{2,3},{4,5},{5,6},{6,7},{8,9},{9,10},{10,11},{12,13},{... | collective-permute-start | bytes 728 | tf_op jit(solution)/shard_map/ppermute | solution.py:16
  36.6 1.2 collective-permute-done.35
  37.9 1.3 collective-permute-start.36
  39.2 4.3 %collective-permute-start.37 = (f32[1,8,128]{2,1,0:T(8,128)S(1)}, f32[1,8,128]{2,1,0:T(8,128)S(1)}, u32[]{:S(2)}, u32[]{:S(2)}) collective-permute-start(f32[1,8,128]{2,1,0:T(8,128)S(1)} %get-tuple-element.87), channel_id=1, source_target_pairs={{0,16},{1,17},{2,18},{3,19},{4,20},{5,21},{6,22},{7,23},{8,24},{9,... | collective-permute-start | bytes 12296 | tf_op jit(solution)/shard_map/ppermute | solution.py:16
  44.2 2.8 %collective-permute-start.38 = (f32[6,1,128]{2,1,0:T(1,128)S(1)}, f32[6,1,128]{2,1,0:T(1,128)S(1)}, u32[]{:S(2)}, u32[]{:S(2)}) collective-permute-start(f32[6,1,128]{2,1,0:T(1,128)S(1)} %get-tuple-element.84), channel_id=1, source_target_pairs={{4,0},{8,4},{12,8},{5,1},{9,5},{13,9},{6,2},{10,6},{14,10},{7,3},{... | collective-permute-start | bytes 9224 | tf_op jit(solution)/shard_map/ppermute | solution.py:19
  47.1 3.6 %collective-permute-start.39 = (f32[6,1,128]{2,1,0:T(1,128)S(1)}, f32[6,1,128]{2,1,0:T(1,128)S(1)}, u32[]{:S(2)}, u32[]{:S(2)}) collective-permute-start(f32[6,1,128]{2,1,0:T(1,128)S(1)} %get-tuple-element.83), channel_id=1, source_target_pairs={{0,4},{4,8},{8,12},{1,5},{5,9},{9,13},{2,6},{6,10},{10,14},{3,7},{... | collective-permute-start | bytes 9224 | tf_op jit(solution)/shard_map/ppermute | solution.py:16
  50.7 2.4 %collective-permute-start.2 = (f32[3,6,1,128]{3,0,2,1:T(4,128)S(1)}, f32[3,6,1,128]{3,0,2,1:T(4,128)S(1)}, u32[]{:S(2)}, u32[]{:S(2)}) collective-permute-start(f32[3,6,1,128]{3,0,2,1:T(4,128)S(1)} %get-tuple-element.63), channel_id=1, source_target_pairs={{0,4},{4,8},{8,12},{1,5},{5,9},{9,13},{2,6},{6,10},{10,14},{3,7},{... | collective-permute-start | bytes 27656 | tf_op jit(solution)/shard_map/ppermute | solution.py:16
  53.1 1.9 collective-permute-start.3
  55.2 1.3 collective-permute-start.40
  56.5 4.6 %collective-permute-start.41 = (f32[6,10,1]{2,1,0:T(8,128)S(1)}, f32[6,10,1]{2,1,0:T(8,128)S(1)}, u32[]{:S(2)}, u32[]{:S(2)}) collective-permute-start(f32[6,10,1]{2,1,0:T(8,128)S(1)} %get-tuple-element.74), channel_id=1, source_target_pairs={{0,1},{1,2},{2,3},{4,5},{5,6},{6,7},{8,9},{9,10},{10,11},{12,13},{... | collective-permute-start | bytes 728 | tf_op jit(solution)/shard_map/ppermute | solution.py:16
  61.4 1.2 collective-permute-done.41
  63.4 3.9 %collective-permute-start.4 = (f32[3,6,10,1]{3,0,2,1:T(4,128)S(1)}, f32[3,6,10,1]{3,0,2,1:T(4,128)S(1)}, u32[]{:S(2)}, u32[]{:S(2)}) collective-permute-start(f32[3,6,10,1]{3,0,2,1:T(4,128)S(1)} %get-tuple-element.55), channel_id=1, source_target_pairs={{0,1},{1,2},{2,3},{4,5},{5,6},{6,7},{8,9},{9,10},{10,11},{12,13},{... | collective-permute-start | bytes 2168 | tf_op jit(solution)/shard_map/ppermute | solution.py:16
  67.3 1.3 collective-permute-start.5
  69.7 4.1 %collective-permute-done.5 = f32[3,6,10,1]{3,0,2,1:T(4,128)S(1)} collective-permute-done((f32[3,6,10,1]{3,0,2,1:T(4,128)S(1)}, f32[3,6,10,1]{3,0,2,1:T(4,128)S(1)}, u32[]{:S(2)}, u32[]{:S(2)}) %collective-permute-start.5) | collective-permute-done | bytes 752 | tf_op jit(solution)/shard_map/ppermute | solution.py:19
  80.1 3.9 %collective-permute-start.6 = (f32[3,1,8,128]{3,0,2,1:T(4,128)S(1)}, f32[3,1,8,128]{3,0,2,1:T(4,128)S(1)}, u32[]{:S(2)}, u32[]{:S(2)}) collective-permute-start(f32[3,1,8,128]{3,0,2,1:T(4,128)S(1)} %get-tuple-element.69), channel_id=1, source_target_pairs={{0,16},{1,17},{2,18},{3,19},{4,20},{5,21},{6,22},{7,23},{8,24},{9,... | collective-permute-start | bytes 36872 | tf_op jit(solution)/shard_map/ppermute | solution.py:16
  84.0 1.3 collective-permute-start.7
  85.5 2.9 %collective-permute-done.7 = f32[3,1,8,128]{3,0,2,1:T(4,128)S(1)} collective-permute-done((f32[3,1,8,128]{3,0,2,1:T(4,128)S(1)}, f32[3,1,8,128]{3,0,2,1:T(4,128)S(1)}, u32[]{:S(2)}, u32[]{:S(2)}) %collective-permute-start.7) | collective-permute-done | bytes 12320 | tf_op jit(solution)/shard_map/ppermute | solution.py:19
  88.5 6.3 %collective-permute-start.8 = (f32[3,6,1,128]{3,0,2,1:T(4,128)S(1)}, f32[3,6,1,128]{3,0,2,1:T(4,128)S(1)}, u32[]{:S(2)}, u32[]{:S(2)}) collective-permute-start(f32[3,6,1,128]{3,0,2,1:T(4,128)S(1)} %get-tuple-element.61), channel_id=1, source_target_pairs={{0,4},{4,8},{8,12},{1,5},{5,9},{9,13},{2,6},{6,10},{10,14},{3,7},{... | collective-permute-start | bytes 27656 | tf_op jit(solution)/shard_map/ppermute | solution.py:16
  94.8 1.9 collective-permute-start.9
  97.0 2.8 %collective-permute-done.9 = f32[3,6,1,128]{3,0,2,1:T(4,128)S(1)} collective-permute-done((f32[3,6,1,128]{3,0,2,1:T(4,128)S(1)}, f32[3,6,1,128]{3,0,2,1:T(4,128)S(1)}, u32[]{:S(2)}, u32[]{:S(2)}) %collective-permute-start.9) | collective-permute-done | bytes 9248 | tf_op jit(solution)/shard_map/ppermute | solution.py:19
  100.0 3.6 %collective-permute-start.10 = (f32[3,6,10,1]{3,0,2,1:T(4,128)S(1)}, f32[3,6,10,1]{3,0,2,1:T(4,128)S(1)}, u32[]{:S(2)}, u32[]{:S(2)}) collective-permute-start(f32[3,6,10,1]{3,0,2,1:T(4,128)S(1)} %get-tuple-element.51), channel_id=1, source_target_pairs={{0,1},{1,2},{2,3},{4,5},{5,6},{6,7},{8,9},{9,10},{10,11},{12,13},{... | collective-permute-start | bytes 2168 | tf_op jit(solution)/shard_map/ppermute | solution.py:16
  103.6 1.5 collective-permute-start.11
  106.2 3.2 %collective-permute-done.11 = f32[3,6,10,1]{3,0,2,1:T(4,128)S(1)} collective-permute-done((f32[3,6,10,1]{3,0,2,1:T(4,128)S(1)}, f32[3,6,10,1]{3,0,2,1:T(4,128)S(1)}, u32[]{:S(2)}, u32[]{:S(2)}) %collective-permute-start.11) | collective-permute-done | bytes 752 | tf_op jit(solution)/shard_map/ppermute | solution.py:19
  115.7 3.2 %reshape.40 = f32[3,2,2,4,2,64,2]{6,5,4,3,2,1,0:T(8,128)S(1)} reshape(f32[3,4,8,128]{3,2,1,0:T(8,128)S(1)} %copy.35) | data formatting | bytes 98304 | tf_op jit(solution)/shard_map/reshape | solution.py:68
  119.2 1.3 collective-permute-start.12
  120.5 1.3 collective-permute-start.13
  122.0 2.9 %collective-permute-done.13 = f32[3,1,4,64]{3,0,2,1:T(4,128)S(1)} collective-permute-done((f32[3,1,4,64]{3,0,2,1:T(4,128)S(1)}, f32[3,1,4,64]{3,0,2,1:T(4,128)S(1)}, u32[]{:S(2)}, u32[]{:S(2)}) %collective-permute-start.13) | collective-permute-done | bytes 3104 | tf_op jit(solution)/shard_map/ppermute | solution.py:19
  124.9 4.7 %collective-permute-start.14 = (f32[3,4,1,64]{3,0,2,1:T(4,128)S(1)}, f32[3,4,1,64]{3,0,2,1:T(4,128)S(1)}, u32[]{:S(2)}, u32[]{:S(2)}) collective-permute-start(f32[3,4,1,64]{3,0,2,1:T(4,128)S(1)} %get-tuple-element.81), channel_id=1, source_target_pairs={{0,4},{4,8},{8,12},{1,5},{5,9},{9,13},{2,6},{6,10},{10,14},{3,7},{... | collective-permute-start | bytes 9224 | tf_op jit(solution)/shard_map/ppermute | solution.py:16
  129.6 1.9 collective-permute-start.15
  131.7 2.9 %collective-permute-done.15 = f32[3,4,1,64]{3,0,2,1:T(4,128)S(1)} collective-permute-done((f32[3,4,1,64]{3,0,2,1:T(4,128)S(1)}, f32[3,4,1,64]{3,0,2,1:T(4,128)S(1)}, u32[]{:S(2)}, u32[]{:S(2)}) %collective-permute-start.15) | collective-permute-done | bytes 3104 | tf_op jit(solution)/shard_map/ppermute | solution.py:19
  134.7 3.2 %collective-permute-start.16 = (f32[3,4,6,1]{3,0,2,1:T(4,128)S(1)}, f32[3,4,6,1]{3,0,2,1:T(4,128)S(1)}, u32[]{:S(2)}, u32[]{:S(2)}) collective-permute-start(f32[3,4,6,1]{3,0,2,1:T(4,128)S(1)} %get-tuple-element.79), channel_id=1, source_target_pairs={{0,1},{1,2},{2,3},{4,5},{5,6},{6,7},{8,9},{9,10},{10,11},{12,13},{... | collective-permute-start | bytes 872 | tf_op jit(solution)/shard_map/ppermute | solution.py:16
  137.9 1.3 collective-permute-start.17
  139.9 2.8 %collective-permute-done.17 = f32[3,4,6,1]{3,0,2,1:T(4,128)S(1)} collective-permute-done((f32[3,4,6,1]{3,0,2,1:T(4,128)S(1)}, f32[3,4,6,1]{3,0,2,1:T(4,128)S(1)}, u32[]{:S(2)}, u32[]{:S(2)}) %collective-permute-start.17) | collective-permute-done | bytes 320 | tf_op jit(solution)/shard_map/ppermute | solution.py:19
  147.9 1.4 collective-permute-start.18
  149.2 1.3 collective-permute-start.19
  150.8 2.9 %collective-permute-done.19 = f32[3,1,8,128]{3,0,2,1:T(4,128)S(1)} collective-permute-done((f32[3,1,8,128]{3,0,2,1:T(4,128)S(1)}, f32[3,1,8,128]{3,0,2,1:T(4,128)S(1)}, u32[]{:S(2)}, u32[]{:S(2)}) %collective-permute-start.19) | collective-permute-done | bytes 12320 | tf_op jit(solution)/shard_map/ppermute | solution.py:19
  153.7 4.8 %collective-permute-start.20 = (f32[3,6,1,128]{3,0,2,1:T(4,128)S(1)}, f32[3,6,1,128]{3,0,2,1:T(4,128)S(1)}, u32[]{:S(2)}, u32[]{:S(2)}) collective-permute-start(f32[3,6,1,128]{3,0,2,1:T(4,128)S(1)} %get-tuple-element.59), channel_id=1, source_target_pairs={{0,4},{4,8},{8,12},{1,5},{5,9},{9,13},{2,6},{6,10},{10,14},{3,7},{... | collective-permute-start | bytes 27656 | tf_op jit(solution)/shard_map/ppermute | solution.py:16
  158.5 1.9 collective-permute-start.21
  160.7 2.8 %collective-permute-done.21 = f32[3,6,1,128]{3,0,2,1:T(4,128)S(1)} collective-permute-done((f32[3,6,1,128]{3,0,2,1:T(4,128)S(1)}, f32[3,6,1,128]{3,0,2,1:T(4,128)S(1)}, u32[]{:S(2)}, u32[]{:S(2)}) %collective-permute-start.21) | collective-permute-done | bytes 9248 | tf_op jit(solution)/shard_map/ppermute | solution.py:19
  163.7 1.6 collective-permute-start.22
  165.4 1.5 collective-permute-start.23
  167.9 3.2 %collective-permute-done.23 = f32[3,6,10,1]{3,0,2,1:T(4,128)S(1)} collective-permute-done((f32[3,6,10,1]{3,0,2,1:T(4,128)S(1)}, f32[3,6,10,1]{3,0,2,1:T(4,128)S(1)}, u32[]{:S(2)}, u32[]{:S(2)}) %collective-permute-start.23) | collective-permute-done | bytes 752 | tf_op jit(solution)/shard_map/ppermute | solution.py:19
  177.4 1.3 collective-permute-start.24
  178.8 1.3 collective-permute-start.25
  180.3 2.9 %collective-permute-done.25 = f32[3,1,8,128]{3,0,2,1:T(4,128)S(1)} collective-permute-done((f32[3,1,8,128]{3,0,2,1:T(4,128)S(1)}, f32[3,1,8,128]{3,0,2,1:T(4,128)S(1)}, u32[]{:S(2)}, u32[]{:S(2)}) %collective-permute-start.25) | collective-permute-done | bytes 12320 | tf_op jit(solution)/shard_map/ppermute | solution.py:19
  183.3 4.7 %collective-permute-start.26 = (f32[3,6,1,128]{3,0,2,1:T(4,128)S(1)}, f32[3,6,1,128]{3,0,2,1:T(4,128)S(1)}, u32[]{:S(2)}, u32[]{:S(2)}) collective-permute-start(f32[3,6,1,128]{3,0,2,1:T(4,128)S(1)} %get-tuple-element.57), channel_id=1, source_target_pairs={{0,4},{4,8},{8,12},{1,5},{5,9},{9,13},{2,6},{6,10},{10,14},{3,7},{... | collective-permute-start | bytes 27656 | tf_op jit(solution)/shard_map/ppermute | solution.py:16
  187.9 1.9 collective-permute-start.27
  190.1 2.8 %collective-permute-done.27 = f32[3,6,1,128]{3,0,2,1:T(4,128)S(1)} collective-permute-done((f32[3,6,1,128]{3,0,2,1:T(4,128)S(1)}, f32[3,6,1,128]{3,0,2,1:T(4,128)S(1)}, u32[]{:S(2)}, u32[]{:S(2)}) %collective-permute-start.27) | collective-permute-done | bytes 9248 | tf_op jit(solution)/shard_map/ppermute | solution.py:19
  193.1 1.6 collective-permute-start.28
  194.8 1.3 collective-permute-start.29
  197.1 3.4 %collective-permute-done.29 = f32[3,6,10,1]{3,0,2,1:T(4,128)S(1)} collective-permute-done((f32[3,6,10,1]{3,0,2,1:T(4,128)S(1)}, f32[3,6,10,1]{3,0,2,1:T(4,128)S(1)}, u32[]{:S(2)}, u32[]{:S(2)}) %collective-permute-start.29) | collective-permute-done | bytes 752 | tf_op jit(solution)/shard_map/ppermute | solution.py:19
  (218 shorter events, 40.8 us)
Async XLA Ops:
  0.6 37.2 %copy-start.2 = (f32[4,8,128]{2,1,0:T(8,128)S(1)}, f32[4,8,128]{2,1,0:T(8,128)}, u32[]{:S(2)}) copy-start(f32[4,8,128]{2,1,0:T(8,128)} %param.6) | copy-start | bytes 49156
  0.6 42.8 %copy-start = (f32[27,3,3]{0,2,1:T(4,128)S(1)}, f32[27,3,3]{0,2,1:T(4,128)}, u32[]{:S(2)}) copy-start(f32[27,3,3]{0,2,1:T(4,128)} %param.9) | copy-start | bytes 2920
  8.1 13.8 %collective-permute-start.30 = (f32[1,8,128]{2,1,0:T(8,128)S(1)}, f32[1,8,128]{2,1,0:T(8,128)S(1)}, u32[]{:S(2)}, u32[]{:S(2)}) collective-permute-start(f32[1,8,128]{2,1,0:T(8,128)S(1)} %get-tuple-element.90), channel_id=1, source_target_pairs={{16,0},{17,1},{18,2},{19,3},{20,4},{21,5},{22,6},{23,7},{24,8},{25... | collective-permute-start | bytes 12296 | tf_op jit(solution)/shard_map/ppermute | solution.py:19
  9.4 12.5 %collective-permute-start.31 = (f32[1,8,128]{2,1,0:T(8,128)S(1)}, f32[1,8,128]{2,1,0:T(8,128)S(1)}, u32[]{:S(2)}, u32[]{:S(2)}) collective-permute-start(f32[1,8,128]{2,1,0:T(8,128)S(1)} %get-tuple-element.89), channel_id=1, source_target_pairs={{0,16},{1,17},{2,18},{3,19},{4,20},{5,21},{6,22},{7,23},{8,24},{9,... | collective-permute-start | bytes 12296 | tf_op jit(solution)/shard_map/ppermute | solution.py:16
  17.6 33.1 %collective-permute-start = (f32[3,1,8,128]{3,0,2,1:T(4,128)S(1)}, f32[3,1,8,128]{3,0,2,1:T(4,128)S(1)}, u32[]{:S(2)}, u32[]{:S(2)}) collective-permute-start(f32[3,1,8,128]{3,0,2,1:T(4,128)S(1)} %get-tuple-element.71), channel_id=1, source_target_pairs={{0,16},{1,17},{2,18},{3,19},{4,20},{5,21},{6,22},{7,23},{8,24},{9,... | collective-permute-start | bytes 36872 | tf_op jit(solution)/shard_map/ppermute | solution.py:16
  18.9 31.8 %collective-permute-start.1 = (f32[3,1,8,128]{3,0,2,1:T(4,128)S(1)}, f32[3,1,8,128]{3,0,2,1:T(4,128)S(1)}, u32[]{:S(2)}, u32[]{:S(2)}) collective-permute-start(f32[3,1,8,128]{3,0,2,1:T(4,128)S(1)} %get-tuple-element.72), channel_id=1, source_target_pairs={{16,0},{17,1},{18,2},{19,3},{20,4},{21,5},{22,6},{23,7},{24,8},{25... | collective-permute-start | bytes 36872 | tf_op jit(solution)/shard_map/ppermute | solution.py:19
  21.9 9.2 %collective-permute-start.32 = (f32[6,1,128]{2,1,0:T(1,128)S(1)}, f32[6,1,128]{2,1,0:T(1,128)S(1)}, u32[]{:S(2)}, u32[]{:S(2)}) collective-permute-start(f32[6,1,128]{2,1,0:T(1,128)S(1)} %get-tuple-element.86), channel_id=1, source_target_pairs={{4,0},{8,4},{12,8},{5,1},{9,5},{13,9},{6,2},{10,6},{14,10},{7,3},{... | collective-permute-start | bytes 9224 | tf_op jit(solution)/shard_map/ppermute | solution.py:19
  24.8 6.4 %collective-permute-start.33 = (f32[6,1,128]{2,1,0:T(1,128)S(1)}, f32[6,1,128]{2,1,0:T(1,128)S(1)}, u32[]{:S(2)}, u32[]{:S(2)}) collective-permute-start(f32[6,1,128]{2,1,0:T(1,128)S(1)} %get-tuple-element.85), channel_id=1, source_target_pairs={{0,4},{4,8},{8,12},{1,5},{5,9},{9,13},{2,6},{6,10},{10,14},{3,7},{... | collective-permute-start | bytes 9224 | tf_op jit(solution)/shard_map/ppermute | solution.py:16
  31.3 5.3 %collective-permute-start.34 = (f32[6,10,1]{2,1,0:T(8,128)S(1)}, f32[6,10,1]{2,1,0:T(8,128)S(1)}, u32[]{:S(2)}, u32[]{:S(2)}) collective-permute-start(f32[6,10,1]{2,1,0:T(8,128)S(1)} %get-tuple-element.75), channel_id=1, source_target_pairs={{1,0},{2,1},{3,2},{5,4},{6,5},{7,6},{9,8},{10,9},{11,10},{13,12},{... | collective-permute-start | bytes 728 | tf_op jit(solution)/shard_map/ppermute | solution.py:19
  32.6 5.2 %collective-permute-start.35 = (f32[6,10,1]{2,1,0:T(8,128)S(1)}, f32[6,10,1]{2,1,0:T(8,128)S(1)}, u32[]{:S(2)}, u32[]{:S(2)}) collective-permute-start(f32[6,10,1]{2,1,0:T(8,128)S(1)} %get-tuple-element.76), channel_id=1, source_target_pairs={{0,1},{1,2},{2,3},{4,5},{5,6},{6,7},{8,9},{9,10},{10,11},{12,13},{... | collective-permute-start | bytes 728 | tf_op jit(solution)/shard_map/ppermute | solution.py:16
  37.9 5.8 %collective-permute-start.36 = (f32[1,8,128]{2,1,0:T(8,128)S(1)}, f32[1,8,128]{2,1,0:T(8,128)S(1)}, u32[]{:S(2)}, u32[]{:S(2)}) collective-permute-start(f32[1,8,128]{2,1,0:T(8,128)S(1)} %get-tuple-element.88), channel_id=1, source_target_pairs={{16,0},{17,1},{18,2},{19,3},{20,4},{21,5},{22,6},{23,7},{24,8},{25... | collective-permute-start | bytes 12296 | tf_op jit(solution)/shard_map/ppermute | solution.py:19
  39.2 5.0 %collective-permute-start.37 = (f32[1,8,128]{2,1,0:T(8,128)S(1)}, f32[1,8,128]{2,1,0:T(8,128)S(1)}, u32[]{:S(2)}, u32[]{:S(2)}) collective-permute-start(f32[1,8,128]{2,1,0:T(8,128)S(1)} %get-tuple-element.87), channel_id=1, source_target_pairs={{0,16},{1,17},{2,18},{3,19},{4,20},{5,21},{6,22},{7,23},{8,24},{9,... | collective-permute-start | bytes 12296 | tf_op jit(solution)/shard_map/ppermute | solution.py:16
  44.2 10.9 %collective-permute-start.38 = (f32[6,1,128]{2,1,0:T(1,128)S(1)}, f32[6,1,128]{2,1,0:T(1,128)S(1)}, u32[]{:S(2)}, u32[]{:S(2)}) collective-permute-start(f32[6,1,128]{2,1,0:T(1,128)S(1)} %get-tuple-element.84), channel_id=1, source_target_pairs={{4,0},{8,4},{12,8},{5,1},{9,5},{13,9},{6,2},{10,6},{14,10},{7,3},{... | collective-permute-start | bytes 9224 | tf_op jit(solution)/shard_map/ppermute | solution.py:19
  47.1 8.0 %collective-permute-start.39 = (f32[6,1,128]{2,1,0:T(1,128)S(1)}, f32[6,1,128]{2,1,0:T(1,128)S(1)}, u32[]{:S(2)}, u32[]{:S(2)}) collective-permute-start(f32[6,1,128]{2,1,0:T(1,128)S(1)} %get-tuple-element.83), channel_id=1, source_target_pairs={{0,4},{4,8},{8,12},{1,5},{5,9},{9,13},{2,6},{6,10},{10,14},{3,7},{... | collective-permute-start | bytes 9224 | tf_op jit(solution)/shard_map/ppermute | solution.py:16
  50.7 12.5 %collective-permute-start.2 = (f32[3,6,1,128]{3,0,2,1:T(4,128)S(1)}, f32[3,6,1,128]{3,0,2,1:T(4,128)S(1)}, u32[]{:S(2)}, u32[]{:S(2)}) collective-permute-start(f32[3,6,1,128]{3,0,2,1:T(4,128)S(1)} %get-tuple-element.63), channel_id=1, source_target_pairs={{0,4},{4,8},{8,12},{1,5},{5,9},{9,13},{2,6},{6,10},{10,14},{3,7},{... | collective-permute-start | bytes 27656 | tf_op jit(solution)/shard_map/ppermute | solution.py:16
  53.1 10.1 %collective-permute-start.3 = (f32[3,6,1,128]{3,0,2,1:T(4,128)S(1)}, f32[3,6,1,128]{3,0,2,1:T(4,128)S(1)}, u32[]{:S(2)}, u32[]{:S(2)}) collective-permute-start(f32[3,6,1,128]{3,0,2,1:T(4,128)S(1)} %get-tuple-element.64), channel_id=1, source_target_pairs={{4,0},{8,4},{12,8},{5,1},{9,5},{13,9},{6,2},{10,6},{14,10},{7,3},{... | collective-permute-start | bytes 27656 | tf_op jit(solution)/shard_map/ppermute | solution.py:19
  55.2 6.2 %collective-permute-start.40 = (f32[6,10,1]{2,1,0:T(8,128)S(1)}, f32[6,10,1]{2,1,0:T(8,128)S(1)}, u32[]{:S(2)}, u32[]{:S(2)}) collective-permute-start(f32[6,10,1]{2,1,0:T(8,128)S(1)} %get-tuple-element.73), channel_id=1, source_target_pairs={{1,0},{2,1},{3,2},{5,4},{6,5},{7,6},{9,8},{10,9},{11,10},{13,12},{... | collective-permute-start | bytes 728 | tf_op jit(solution)/shard_map/ppermute | solution.py:19
  56.5 6.1 %collective-permute-start.41 = (f32[6,10,1]{2,1,0:T(8,128)S(1)}, f32[6,10,1]{2,1,0:T(8,128)S(1)}, u32[]{:S(2)}, u32[]{:S(2)}) collective-permute-start(f32[6,10,1]{2,1,0:T(8,128)S(1)} %get-tuple-element.74), channel_id=1, source_target_pairs={{0,1},{1,2},{2,3},{4,5},{5,6},{6,7},{8,9},{9,10},{10,11},{12,13},{... | collective-permute-start | bytes 728 | tf_op jit(solution)/shard_map/ppermute | solution.py:16
  63.4 6.3 %collective-permute-start.4 = (f32[3,6,10,1]{3,0,2,1:T(4,128)S(1)}, f32[3,6,10,1]{3,0,2,1:T(4,128)S(1)}, u32[]{:S(2)}, u32[]{:S(2)}) collective-permute-start(f32[3,6,10,1]{3,0,2,1:T(4,128)S(1)} %get-tuple-element.55), channel_id=1, source_target_pairs={{0,1},{1,2},{2,3},{4,5},{5,6},{6,7},{8,9},{9,10},{10,11},{12,13},{... | collective-permute-start | bytes 2168 | tf_op jit(solution)/shard_map/ppermute | solution.py:16
  67.3 6.4 %collective-permute-start.5 = (f32[3,6,10,1]{3,0,2,1:T(4,128)S(1)}, f32[3,6,10,1]{3,0,2,1:T(4,128)S(1)}, u32[]{:S(2)}, u32[]{:S(2)}) collective-permute-start(f32[3,6,10,1]{3,0,2,1:T(4,128)S(1)} %get-tuple-element.56), channel_id=1, source_target_pairs={{1,0},{2,1},{3,2},{5,4},{6,5},{7,6},{9,8},{10,9},{11,10},{13,12},{... | collective-permute-start | bytes 2168 | tf_op jit(solution)/shard_map/ppermute | solution.py:19
  68.9 10.9 %copy-start.1 = (f32[3,4,8,128]{3,2,1,0:T(8,128)S(1)}, f32[3,4,8,128]{3,2,1,0:T(8,128)}, u32[]{:S(2)}) copy-start(f32[3,4,8,128]{3,2,1,0:T(8,128)} %param.5) | copy-start | bytes 147460
  80.1 5.5 %collective-permute-start.6 = (f32[3,1,8,128]{3,0,2,1:T(4,128)S(1)}, f32[3,1,8,128]{3,0,2,1:T(4,128)S(1)}, u32[]{:S(2)}, u32[]{:S(2)}) collective-permute-start(f32[3,1,8,128]{3,0,2,1:T(4,128)S(1)} %get-tuple-element.69), channel_id=1, source_target_pairs={{0,16},{1,17},{2,18},{3,19},{4,20},{5,21},{6,22},{7,23},{8,24},{9,... | collective-permute-start | bytes 36872 | tf_op jit(solution)/shard_map/ppermute | solution.py:16
  84.0 4.5 %collective-permute-start.7 = (f32[3,1,8,128]{3,0,2,1:T(4,128)S(1)}, f32[3,1,8,128]{3,0,2,1:T(4,128)S(1)}, u32[]{:S(2)}, u32[]{:S(2)}) collective-permute-start(f32[3,1,8,128]{3,0,2,1:T(4,128)S(1)} %get-tuple-element.70), channel_id=1, source_target_pairs={{16,0},{17,1},{18,2},{19,3},{20,4},{21,5},{22,6},{23,7},{24,8},{25... | collective-permute-start | bytes 36872 | tf_op jit(solution)/shard_map/ppermute | solution.py:19
  88.5 8.5 %collective-permute-start.8 = (f32[3,6,1,128]{3,0,2,1:T(4,128)S(1)}, f32[3,6,1,128]{3,0,2,1:T(4,128)S(1)}, u32[]{:S(2)}, u32[]{:S(2)}) collective-permute-start(f32[3,6,1,128]{3,0,2,1:T(4,128)S(1)} %get-tuple-element.61), channel_id=1, source_target_pairs={{0,4},{4,8},{8,12},{1,5},{5,9},{9,13},{2,6},{6,10},{10,14},{3,7},{... | collective-permute-start | bytes 27656 | tf_op jit(solution)/shard_map/ppermute | solution.py:16
  94.8 5.0 %collective-permute-start.9 = (f32[3,6,1,128]{3,0,2,1:T(4,128)S(1)}, f32[3,6,1,128]{3,0,2,1:T(4,128)S(1)}, u32[]{:S(2)}, u32[]{:S(2)}) collective-permute-start(f32[3,6,1,128]{3,0,2,1:T(4,128)S(1)} %get-tuple-element.62), channel_id=1, source_target_pairs={{4,0},{8,4},{12,8},{5,1},{9,5},{13,9},{6,2},{10,6},{14,10},{7,3},{... | collective-permute-start | bytes 27656 | tf_op jit(solution)/shard_map/ppermute | solution.py:19
  100.0 6.2 %collective-permute-start.10 = (f32[3,6,10,1]{3,0,2,1:T(4,128)S(1)}, f32[3,6,10,1]{3,0,2,1:T(4,128)S(1)}, u32[]{:S(2)}, u32[]{:S(2)}) collective-permute-start(f32[3,6,10,1]{3,0,2,1:T(4,128)S(1)} %get-tuple-element.51), channel_id=1, source_target_pairs={{0,1},{1,2},{2,3},{4,5},{5,6},{6,7},{8,9},{9,10},{10,11},{12,13},{... | collective-permute-start | bytes 2168 | tf_op jit(solution)/shard_map/ppermute | solution.py:16
  103.6 5.8 %collective-permute-start.11 = (f32[3,6,10,1]{3,0,2,1:T(4,128)S(1)}, f32[3,6,10,1]{3,0,2,1:T(4,128)S(1)}, u32[]{:S(2)}, u32[]{:S(2)}) collective-permute-start(f32[3,6,10,1]{3,0,2,1:T(4,128)S(1)} %get-tuple-element.52), channel_id=1, source_target_pairs={{1,0},{2,1},{3,2},{5,4},{6,5},{7,6},{9,8},{10,9},{11,10},{13,12},{... | collective-permute-start | bytes 2168 | tf_op jit(solution)/shard_map/ppermute | solution.py:19
  119.2 2.8 %collective-permute-start.12 = (f32[3,1,4,64]{3,0,2,1:T(4,128)S(1)}, f32[3,1,4,64]{3,0,2,1:T(4,128)S(1)}, u32[]{:S(2)}, u32[]{:S(2)}) collective-permute-start(f32[3,1,4,64]{3,0,2,1:T(4,128)S(1)} %get-tuple-element.91), channel_id=1, source_target_pairs={{0,16},{1,17},{2,18},{3,19},{4,20},{5,21},{6,22},{7,23},{8,24},{9,... | collective-permute-start | bytes 9224 | tf_op jit(solution)/shard_map/ppermute | solution.py:16
  120.5 4.4 %collective-permute-start.13 = (f32[3,1,4,64]{3,0,2,1:T(4,128)S(1)}, f32[3,1,4,64]{3,0,2,1:T(4,128)S(1)}, u32[]{:S(2)}, u32[]{:S(2)}) collective-permute-start(f32[3,1,4,64]{3,0,2,1:T(4,128)S(1)} %get-tuple-element.92), channel_id=1, source_target_pairs={{16,0},{17,1},{18,2},{19,3},{20,4},{21,5},{22,6},{23,7},{24,8},{25... | collective-permute-start | bytes 9224 | tf_op jit(solution)/shard_map/ppermute | solution.py:19
  124.9 6.8 %collective-permute-start.14 = (f32[3,4,1,64]{3,0,2,1:T(4,128)S(1)}, f32[3,4,1,64]{3,0,2,1:T(4,128)S(1)}, u32[]{:S(2)}, u32[]{:S(2)}) collective-permute-start(f32[3,4,1,64]{3,0,2,1:T(4,128)S(1)} %get-tuple-element.81), channel_id=1, source_target_pairs={{0,4},{4,8},{8,12},{1,5},{5,9},{9,13},{2,6},{6,10},{10,14},{3,7},{... | collective-permute-start | bytes 9224 | tf_op jit(solution)/shard_map/ppermute | solution.py:16
  129.6 5.0 %collective-permute-start.15 = (f32[3,4,1,64]{3,0,2,1:T(4,128)S(1)}, f32[3,4,1,64]{3,0,2,1:T(4,128)S(1)}, u32[]{:S(2)}, u32[]{:S(2)}) collective-permute-start(f32[3,4,1,64]{3,0,2,1:T(4,128)S(1)} %get-tuple-element.82), channel_id=1, source_target_pairs={{4,0},{8,4},{12,8},{5,1},{9,5},{13,9},{6,2},{10,6},{14,10},{7,3},{... | collective-permute-start | bytes 9224 | tf_op jit(solution)/shard_map/ppermute | solution.py:19
  134.7 5.2 %collective-permute-start.16 = (f32[3,4,6,1]{3,0,2,1:T(4,128)S(1)}, f32[3,4,6,1]{3,0,2,1:T(4,128)S(1)}, u32[]{:S(2)}, u32[]{:S(2)}) collective-permute-start(f32[3,4,6,1]{3,0,2,1:T(4,128)S(1)} %get-tuple-element.79), channel_id=1, source_target_pairs={{0,1},{1,2},{2,3},{4,5},{5,6},{6,7},{8,9},{9,10},{10,11},{12,13},{... | collective-permute-start | bytes 872 | tf_op jit(solution)/shard_map/ppermute | solution.py:16
  137.9 4.8 %collective-permute-start.17 = (f32[3,4,6,1]{3,0,2,1:T(4,128)S(1)}, f32[3,4,6,1]{3,0,2,1:T(4,128)S(1)}, u32[]{:S(2)}, u32[]{:S(2)}) collective-permute-start(f32[3,4,6,1]{3,0,2,1:T(4,128)S(1)} %get-tuple-element.80), channel_id=1, source_target_pairs={{1,0},{2,1},{3,2},{5,4},{6,5},{7,6},{9,8},{10,9},{11,10},{13,12},{... | collective-permute-start | bytes 872 | tf_op jit(solution)/shard_map/ppermute | solution.py:19
  147.9 2.9 %collective-permute-start.18 = (f32[3,1,8,128]{3,0,2,1:T(4,128)S(1)}, f32[3,1,8,128]{3,0,2,1:T(4,128)S(1)}, u32[]{:S(2)}, u32[]{:S(2)}) collective-permute-start(f32[3,1,8,128]{3,0,2,1:T(4,128)S(1)} %get-tuple-element.67), channel_id=1, source_target_pairs={{0,16},{1,17},{2,18},{3,19},{4,20},{5,21},{6,22},{7,23},{8,24},{9,... | collective-permute-start | bytes 36872 | tf_op jit(solution)/shard_map/ppermute | solution.py:16
  149.2 4.5 %collective-permute-start.19 = (f32[3,1,8,128]{3,0,2,1:T(4,128)S(1)}, f32[3,1,8,128]{3,0,2,1:T(4,128)S(1)}, u32[]{:S(2)}, u32[]{:S(2)}) collective-permute-start(f32[3,1,8,128]{3,0,2,1:T(4,128)S(1)} %get-tuple-element.68), channel_id=1, source_target_pairs={{16,0},{17,1},{18,2},{19,3},{20,4},{21,5},{22,6},{23,7},{24,8},{25... | collective-permute-start | bytes 36872 | tf_op jit(solution)/shard_map/ppermute | solution.py:19
  153.7 7.0 %collective-permute-start.20 = (f32[3,6,1,128]{3,0,2,1:T(4,128)S(1)}, f32[3,6,1,128]{3,0,2,1:T(4,128)S(1)}, u32[]{:S(2)}, u32[]{:S(2)}) collective-permute-start(f32[3,6,1,128]{3,0,2,1:T(4,128)S(1)} %get-tuple-element.59), channel_id=1, source_target_pairs={{0,4},{4,8},{8,12},{1,5},{5,9},{9,13},{2,6},{6,10},{10,14},{3,7},{... | collective-permute-start | bytes 27656 | tf_op jit(solution)/shard_map/ppermute | solution.py:16
  158.5 5.0 %collective-permute-start.21 = (f32[3,6,1,128]{3,0,2,1:T(4,128)S(1)}, f32[3,6,1,128]{3,0,2,1:T(4,128)S(1)}, u32[]{:S(2)}, u32[]{:S(2)}) collective-permute-start(f32[3,6,1,128]{3,0,2,1:T(4,128)S(1)} %get-tuple-element.60), channel_id=1, source_target_pairs={{4,0},{8,4},{12,8},{5,1},{9,5},{13,9},{6,2},{10,6},{14,10},{7,3},{... | collective-permute-start | bytes 27656 | tf_op jit(solution)/shard_map/ppermute | solution.py:19
  163.7 4.2 %collective-permute-start.22 = (f32[3,6,10,1]{3,0,2,1:T(4,128)S(1)}, f32[3,6,10,1]{3,0,2,1:T(4,128)S(1)}, u32[]{:S(2)}, u32[]{:S(2)}) collective-permute-start(f32[3,6,10,1]{3,0,2,1:T(4,128)S(1)} %get-tuple-element.47), channel_id=1, source_target_pairs={{0,1},{1,2},{2,3},{4,5},{5,6},{6,7},{8,9},{9,10},{10,11},{12,13},{... | collective-permute-start | bytes 2168 | tf_op jit(solution)/shard_map/ppermute | solution.py:16
  165.4 5.8 %collective-permute-start.23 = (f32[3,6,10,1]{3,0,2,1:T(4,128)S(1)}, f32[3,6,10,1]{3,0,2,1:T(4,128)S(1)}, u32[]{:S(2)}, u32[]{:S(2)}) collective-permute-start(f32[3,6,10,1]{3,0,2,1:T(4,128)S(1)} %get-tuple-element.48), channel_id=1, source_target_pairs={{1,0},{2,1},{3,2},{5,4},{6,5},{7,6},{9,8},{10,9},{11,10},{13,12},{... | collective-permute-start | bytes 2168 | tf_op jit(solution)/shard_map/ppermute | solution.py:19
  177.4 2.9 %collective-permute-start.24 = (f32[3,1,8,128]{3,0,2,1:T(4,128)S(1)}, f32[3,1,8,128]{3,0,2,1:T(4,128)S(1)}, u32[]{:S(2)}, u32[]{:S(2)}) collective-permute-start(f32[3,1,8,128]{3,0,2,1:T(4,128)S(1)} %get-tuple-element.65), channel_id=1, source_target_pairs={{0,16},{1,17},{2,18},{3,19},{4,20},{5,21},{6,22},{7,23},{8,24},{9,... | collective-permute-start | bytes 36872 | tf_op jit(solution)/shard_map/ppermute | solution.py:16
  178.8 4.5 %collective-permute-start.25 = (f32[3,1,8,128]{3,0,2,1:T(4,128)S(1)}, f32[3,1,8,128]{3,0,2,1:T(4,128)S(1)}, u32[]{:S(2)}, u32[]{:S(2)}) collective-permute-start(f32[3,1,8,128]{3,0,2,1:T(4,128)S(1)} %get-tuple-element.66), channel_id=1, source_target_pairs={{16,0},{17,1},{18,2},{19,3},{20,4},{21,5},{22,6},{23,7},{24,8},{25... | collective-permute-start | bytes 36872 | tf_op jit(solution)/shard_map/ppermute | solution.py:19
  183.3 6.9 %collective-permute-start.26 = (f32[3,6,1,128]{3,0,2,1:T(4,128)S(1)}, f32[3,6,1,128]{3,0,2,1:T(4,128)S(1)}, u32[]{:S(2)}, u32[]{:S(2)}) collective-permute-start(f32[3,6,1,128]{3,0,2,1:T(4,128)S(1)} %get-tuple-element.57), channel_id=1, source_target_pairs={{0,4},{4,8},{8,12},{1,5},{5,9},{9,13},{2,6},{6,10},{10,14},{3,7},{... | collective-permute-start | bytes 27656 | tf_op jit(solution)/shard_map/ppermute | solution.py:16
  187.9 5.0 %collective-permute-start.27 = (f32[3,6,1,128]{3,0,2,1:T(4,128)S(1)}, f32[3,6,1,128]{3,0,2,1:T(4,128)S(1)}, u32[]{:S(2)}, u32[]{:S(2)}) collective-permute-start(f32[3,6,1,128]{3,0,2,1:T(4,128)S(1)} %get-tuple-element.58), channel_id=1, source_target_pairs={{4,0},{8,4},{12,8},{5,1},{9,5},{13,9},{6,2},{10,6},{14,10},{7,3},{... | collective-permute-start | bytes 27656 | tf_op jit(solution)/shard_map/ppermute | solution.py:19
  193.1 4.0 %collective-permute-start.28 = (f32[3,6,10,1]{3,0,2,1:T(4,128)S(1)}, f32[3,6,10,1]{3,0,2,1:T(4,128)S(1)}, u32[]{:S(2)}, u32[]{:S(2)}) collective-permute-start(f32[3,6,10,1]{3,0,2,1:T(4,128)S(1)} %get-tuple-element.43), channel_id=1, source_target_pairs={{0,1},{1,2},{2,3},{4,5},{5,6},{6,7},{8,9},{9,10},{10,11},{12,13},{... | collective-permute-start | bytes 2168 | tf_op jit(solution)/shard_map/ppermute | solution.py:16
  194.8 5.8 %collective-permute-start.29 = (f32[3,6,10,1]{3,0,2,1:T(4,128)S(1)}, f32[3,6,10,1]{3,0,2,1:T(4,128)S(1)}, u32[]{:S(2)}, u32[]{:S(2)}) collective-permute-start(f32[3,6,10,1]{3,0,2,1:T(4,128)S(1)} %get-tuple-element.44), channel_id=1, source_target_pairs={{1,0},{2,1},{3,2},{5,4},{6,5},{7,6},{9,8},{10,9},{11,10},{13,12},{... | collective-permute-start | bytes 2168 | tf_op jit(solution)/shard_map/ppermute | solution.py:19
where the time goes:
time: 209 us; the launch traced here: 207 us
  starting transfers between devices  104 us (50%)
  waiting for transfers between devices  42.6 us (20%)
  matrix products  35.6 us (17%)
  local copies, waits for them, and re-layouts  11.2 us (5%)
  other arithmetic  9.08 us (4%)
  between operations  4.47 us (2%)
    ppermute x21, starting transfers between devices, padded_2(): lax.ppermute(lax.slice_in_dim(block, block.shape[dim] - width, None, axis...  70.7 us
    ppermute x21, waiting for transfers between devices, padded_2(): lax.ppermute(lax.slice_in_dim(block, 0, width, axis=dim), axis, backward)  39.7 us
    dot_general x135, matrix products, stencil_sum(): jnp.einsum('ij,jxyz->ixyz', block, slab, precision=lax.Precision.HIGHEST)  35.6 us
    ppermute x21, starting transfers between devices, padded_2(): lax.ppermute(lax.slice_in_dim(block, 0, width, axis=dim), axis, backward)  33.8 us
    mul x1, other arithmetic, on_device(): pressure = OMEGA * pinv * rhs_pressure  5.8 us
  transfers between devices with their start and end apart: 42, of which 16 were waited for; matrix products, arithmetic and copies ran while one was open for 7% of the time, Pallas kernels for 0%

commit v1 on v0

v1 whole, which is shorter than its diff:
```python
import functools

import jax
import jax.numpy as jnp
from jax import lax
from jax.experimental import pallas as pl
from jax.experimental.pallas import tpu as pltpu
from jax.sharding import PartitionSpec as P

LOW_BOUND = 0.2
HIGH_BOUND = 1.8

SUB = 8
LANES = 128
COLS = 8
REACH = 6
FIELDS = 5
PAD = 3
ROWS = 5 * SUB
OWN = 2 * SUB


def cheb_consts():
    theta = (HIGH_BOUND + LOW_BOUND) / 2.0
    delta = (HIGH_BOUND - LOW_BOUND) / 2.0
    sigma = theta / delta
    rho_zero = 1.0 / sigma
    rho_one = 1.0 / (2.0 * sigma - rho_zero)
    return (theta, delta, rho_zero, rho_one)


def first_pairs(count):
    return [(i, i ^ 1) for i in range(count) if i ^ 1 < count]


def second_pairs(count):
    pairs = []
    for i in range(1, count - 1, 2):
        pairs += [(i, i + 1), (i + 1, i)]
    return pairs


def matched(block, axis, pairs):
    if not pairs:
        return jnp.zeros_like(block)
    return lax.ppermute(block, axis, pairs)


def lane_iota():
    return lax.broadcasted_iota(jnp.int32, (SUB, LANES), 1)


def pack_kernel(planes, tab_ref, rhs_ref, press_ref, ids_ref, main_ref, a_ref, b_ref):
    lane = lane_iota()
    odd = lax.axis_index("gz") % 2 == 1
    layers = tab_ref.shape[1]
    for f in range(FIELDS):
        a_ref[f] = jnp.zeros((SUB, LANES), jnp.float32)
        b_ref[f] = jnp.zeros((SUB, LANES), jnp.float32)
    up = [jnp.zeros((SUB, LANES), jnp.float32)] * FIELDS
    down = [jnp.zeros((SUB, LANES), jnp.float32)] * FIELDS
    width = 2 * COLS
    for p in range(planes):
        ids = ids_ref[p]
        eta = jnp.zeros((SUB, LANES), jnp.float32)
        dinv = jnp.zeros((SUB, LANES), jnp.float32)
        for layer in range(layers):
            hit = ids == layer
            eta = jnp.where(hit, tab_ref[0, layer], eta)
            dinv = jnp.where(hit, tab_ref[1, layer], dinv)
        values = [rhs_ref[j, p] * dinv for j in range(3)]
        values += [eta, eta * press_ref[p] * (1.0 / 9.0)]
        for f in range(FIELDS):
            main_ref[f * planes + p] = values[f]
            high = pltpu.roll(values[f], (p * width + COLS) % LANES, 1)
            up[f] = jnp.where((lane >= p * width) & (lane < p * width + COLS), high, up[f])
            low = pltpu.roll(values[f], (p * width + COLS) % LANES, 1)
            down[f] = jnp.where(
                (lane >= p * width + COLS) & (lane < (p + 1) * width), low, down[f]
            )
    for f in range(FIELDS):
        a_ref[f] = jnp.where(odd, down[f], up[f])
        b_ref[f] = jnp.where(odd, up[f], down[f])


def tile_span(planes_from, planes_to, stride):
    first = planes_from * stride // LANES
    last = ((planes_to + 1) * stride - 1) // LANES
    return first, last - first + 1


def cycle_kernel(
    planes,
    blocks,
    paired,
    own_ref,
    a_ref,
    b_ref,
    coef_ref,
    vel_ref,
    press_ref,
    fields,
    work,
    shifted,
    second_x,
    resid,
    sums,
    press,
    out,
):
    theta, delta, rho_zero, rho_one = cheb_consts()
    weight = 2.0 * rho_one / delta
    carry = rho_one * rho_zero
    total = planes * blocks
    stride = LANES + 2 * COLS
    tiles = fields.shape[1]
    lane = lane_iota()
    zero = jnp.zeros((SUB, LANES), jnp.float32)
    gx = lax.axis_index("gx")
    y_odd = lax.axis_index("gy") % 2 == 1

    def span(grow):
        if paired:
            low = tile_span(0, min(planes - 1 + grow, total - 1), stride)
            high = tile_span(max(planes - grow, 0), total - 1, stride)
            count = max(low[1], high[1])
            return low[0] + gx * (high[0] - low[0]), count
        own = blocks // 2
        lo = max(own * planes - grow, 0)
        hi = min((own + 1) * planes - 1 + grow, total - 1)
        return tile_span(lo, hi, stride)

    def slot(q):
        return (q + gx) % 2 if paired else q

    for k in list(range(PAD)) + list(range(PAD + tiles, 2 * PAD + tiles)):
        for r in range(1, 4):
            for j in range(3):
                work[j, k, r * SUB : (r + 1) * SUB, :] = zero
            press[k, r * SUB : (r + 1) * SUB, :] = zero

    def assemble(src, row):
        for f in range(FIELDS):
            halo = {}
            for q in range(blocks):
                tile = src[slot(q), FIELDS * planes + f]
                turn = (q * planes * 2 * COLS) % LANES
                halo[q] = pltpu.roll(tile, turn, 1) if turn else tile
            mains = {}
            for k in range(tiles):
                pieces = []
                for plane in range(total):
                    q, p = divmod(plane, planes)
                    at = plane * stride
                    for kind, lo, hi in (
                        ("halo", at, at + COLS),
                        ("main", at + COLS, at + COLS + LANES),
                        ("halo", at + COLS + LANES, at + stride),
                    ):
                        lo, hi = max(lo, k * LANES), min(hi, (k + 1) * LANES)
                        if lo >= hi:
                            continue
                        if kind == "halo":
                            piece = ("halo", q)
                        else:
                            piece = ("main", plane)
                        if pieces and pieces[-1][1] == piece:
                            continue
                        pieces.append((lo - k * LANES, piece))
                if (k + 1) * LANES > total * stride:
                    pieces.append((total * stride - k * LANES, None))
                value = None
                for start, piece in pieces:
                    if piece is None:
                        tile = zero
                    elif piece[0] == "halo":
                        tile = halo[piece[1]]
                    else:
                        plane = piece[1]
                        if plane not in mains:
                            q, p = divmod(plane, planes)
                            mains[plane] = pltpu.roll(
                                src[slot(q), f * planes + p],
                                (plane * stride + COLS) % LANES,
                                1,
                            )
                        tile = mains[plane]
                    value = tile if value is None else jnp.where(lane >= start, tile, value)
                fields[f, k, row : row + SUB, :] = value
                if f < 3:
                    work[f, PAD + k, row : row + SUB, :] = value
                if f == 4:
                    press[PAD + k, row : row + SUB, :] = value

    assemble(own_ref, OWN)

    @pl.when(y_odd)
    def _():
        assemble(a_ref, OWN - SUB)
        assemble(b_ref, OWN + SUB)

    @pl.when(jnp.logical_not(y_odd))
    def _():
        assemble(b_ref, OWN - SUB)
        assemble(a_ref, OWN + SUB)

    def shift_reader(load, offset):
        jump, turn = divmod(offset, LANES)
        cache = {}

        def turned(k):
            if k not in cache:
                cache[k] = pltpu.roll(load(k), LANES - turn, 1)
            return cache[k]

        def tile(k):
            if turn == 0:
                return load(k + jump)
            return jnp.where(lane < LANES - turn, turned(k + jump), turned(k + jump + 1))

        return tile

    def make_shifts(base, count, rows, scale):
        for j in range(3):
            for row in rows:
                def load(k, j=j, row=row):
                    return work[j, PAD + base + k, row : row + SUB, :]

                readers = {}
                for a in range(3):
                    for c in range(3):
                        if (a, c) != (1, 1):
                            readers[a * 3 + c] = shift_reader(
                                load, ((a - 1) * stride + (c - 1)) * scale
                            )
                for k in range(count):
                    for n, reader in readers.items():
                        shifted[n, j, k, row : row + SUB, :] = reader(k)

    def apply(base, count, rows, scale, group, emit):
        def step(first, width):
            spots = [(first + g, row) for g in range(width) for row in rows]
            totals = [[None] * 3 for _ in spots]
            for a in range(3):
                for c in range(3):
                    for b in range(3):
                        for j in range(3):
                            values = []
                            for k, row in spots:
                                at = row + (b - 1) * scale
                                if (a, c) == (1, 1):
                                    v = work[j, PAD + base + k, at : at + SUB, :]
                                else:
                                    v = shifted[a * 3 + c, j, k, at : at + SUB, :]
                                values.append(v)
                            for i in range(3):
                                n = (9 * a + 3 * b + c) * 9 + i * 3 + j
                                coef = jnp.broadcast_to(coef_ref[n : n + 1, :], (SUB, LANES))
                                for s, v in enumerate(values):
                                    term = coef * v
                                    old = totals[s][i]
                                    totals[s][i] = term if old is None else old + term
            results = []
            for (k, row), sums_of in zip(spots, totals):
                results.append(emit(base + k, row, sums_of))
            for stores in results:
                for ref, index, value in stores:
                    ref[index] = value

        whole = count // group
        if whole > 1:
            def body(n, _):
                step(n * group, group)
                return 0

            lax.fori_loop(0, whole, body, 0)
        elif whole == 1:
            step(0, group)
        if count % group:
            step(whole * group, count % group)

    def inside(k, row):
        return fields[3, k, row : row + SUB, :] > 0.0

    def emit_first(k, row, sums_of):
        keep = inside(k, row)
        stores = []
        for i in range(3):
            f0 = fields[i, k, row : row + SUB, :]
            value = jnp.where(keep, (1.0 + carry + weight) * f0 - weight * sums_of[i], 0.0)
            stores.append((work, (i, PAD + k, pl.ds(row, SUB), slice(None)), value))
            stores.append((second_x, (i, k, pl.ds(row, SUB), slice(None)), value))
        return stores

    make_shifts(0, tiles, [OWN - SUB, OWN, OWN + SUB], 1)
    apply(0, tiles, [OWN - SUB, OWN, OWN + SUB], 1, 1, emit_first)

    def emit_resid(k, row, sums_of):
        eta = fields[3, k, row : row + SUB, :]
        stores = []
        for i in range(3):
            value = eta * (fields[i, k, row : row + SUB, :] - sums_of[i])
            at = row - (OWN - SUB // 2)
            stores.append((resid, (i, k, pl.ds(at, SUB), slice(None)), value))
        return stores

    make_shifts(0, tiles, [OWN - SUB, OWN, OWN + SUB], 1)
    apply(0, tiles, [OWN - SUB // 2, OWN + SUB // 2], 1, 1, emit_resid)

    lane_even = lane % 2 == 0
    row_even = lax.broadcasted_iota(jnp.int32, (SUB, LANES), 0) % 2 == 0
    for r in range(2):
        row = OWN - SUB // 2 + r * SUB
        for k in range(tiles):
            for f in range(4):
                if f < 3:
                    v = resid[f, k, r * SUB : (r + 1) * SUB, :]
                else:
                    v = fields[3, k, row : row + SUB, :]
                v = v + jnp.where(row_even, pltpu.roll(v, SUB - 1, 0), pltpu.roll(v, 1, 0))
                v = v + jnp.where(lane_even, pltpu.roll(v, LANES - 1, 1), pltpu.roll(v, 1, 1))
                sums[f, k, r * SUB : (r + 1) * SUB, :] = v
        scale_at = {}
        for f in (3, 0, 1, 2):
            def load(k, f=f, r=r):
                if 0 <= k < tiles:
                    return sums[f, k, r * SUB : (r + 1) * SUB, :]
                return zero

            ahead, behind = shift_reader(load, stride), shift_reader(load, -stride)
            for k in range(tiles):
                plane = k * LANES // stride
                edge = (plane + 1) * stride - k * LANES
                near, far = (ahead(k), behind(k))
                if plane % 2:
                    near, far = far, near
                other = jnp.where(lane < edge, near, far) if edge < LANES else near
                v = load(k) + other
                if f == 3:
                    scale_at[k] = jnp.where(v > 0.0, 4.0 / v, 0.0)
                else:
                    work[f, PAD + k, row : row + SUB, :] = v * scale_at[k]

    def emit_start(k, row, sums_of):
        keep = inside(k, row)
        stores = []
        for i in range(3):
            fc = work[i, PAD + k, row : row + SUB, :]
            value = second_x[i, k, row : row + SUB, :] + (1.0 + carry + weight) * fc
            value = jnp.where(keep, value - weight * sums_of[i], 0.0)
            stores.append((work, (i, PAD + k, pl.ds(row, SUB), slice(None)), value))
        return stores

    base, count = span(2)
    make_shifts(base, count, [OWN - SUB // 2, OWN + SUB // 2], 2)
    apply(base, count, [OWN - 2, OWN - 2 + SUB], 2, 1, emit_start)

    def emit_middle(k, row, sums_of):
        keep = inside(k, row)
        stores = []
        for i in range(3):
            step = jnp.where(keep, fields[i, k, row : row + SUB, :] - sums_of[i], 0.0)
            value = work[i, PAD + k, row : row + SUB, :] + step
            stores.append((work, (i, PAD + k, pl.ds(row, SUB), slice(None)), value))
            stores.append((second_x, (i, k, pl.ds(row, SUB), slice(None)), step))
        return stores

    base, count = span(1)
    make_shifts(base, count, [OWN - 2, OWN - 2 + SUB], 1)
    apply(base, count, [OWN - 1, OWN - 1 + SUB], 1, 2, emit_middle)
    press_base, press_count = base, count

    base, count = span(0)

    def emit_last(k, row, sums_of):
        stores = []
        for i in range(3):
            value = work[i, PAD + k, row : row + SUB, :]
            value = value + carry * second_x[i, k, row : row + SUB, :]
            value = value + weight * (fields[i, k, row : row + SUB, :] - sums_of[i])
            stores.append((out, (i, k - base), value))
        return stores

    make_shifts(base, count, [OWN - 1, OWN + 1], 1)
    apply(base, count, [OWN], 1, count, emit_last)

    def beside(base, row):
        def load(k):
            return press[PAD + base + k, row : row + SUB, :]

        readers = [shift_reader(load, o) for o in (-stride, stride, -1, 1)]

        def tile(k):
            v = press[PAD + base + k, row - 1 : row - 1 + SUB, :]
            v = v + press[PAD + base + k, row + 1 : row + 1 + SUB, :]
            for reader in readers:
                v = v + reader(k)
            return v

        return tile

    news = []
    for row in (OWN - 1, OWN - 1 + SUB):
        near = beside(press_base, row)
        for k in range(press_count):
            v = fields[4, press_base + k, row : row + SUB, :] * (4.0 / 3.0) + near(k) * (1.0 / 9.0)
            sums[0, k, row - OWN + 1 : row - OWN + 1 + SUB, :] = jnp.where(
                inside(press_base + k, row), v, 0.0
            )
    for r, row in enumerate((OWN - 1, OWN - 1 + SUB)):
        for k in range(press_count):
            press[PAD + press_base + k, row : row + SUB, :] = sums[
                0, k, r * SUB : (r + 1) * SUB, :
            ]
    near = beside(base, OWN)
    for k in range(count):
        v = press[PAD + base + k, OWN : OWN + SUB, :] * (1.0 / 3.0)
        out[3, k] = v + fields[4, base + k, OWN : OWN + SUB, :] + near(k) * (1.0 / 9.0)

    for p in range(planes):
        if paired:
            at, turn = divmod(p * stride + COLS, LANES)
            turn = turn + gx * (planes * stride % LANES)
            back = (2 * LANES - turn) % LANES
            keep = lane < LANES - turn
        else:
            flat = (blocks // 2 * planes + p) * stride + COLS
            at, turn = divmod(flat, LANES)
            at = at - base
            back = LANES - turn
            keep = lane < LANES - turn
        for f in range(4):
            first = pltpu.roll(out[f, at], back, 1)
            v = jnp.where(keep, first, pltpu.roll(out[f, at + 1], back, 1))
            if f < 3:
                vel_ref[f, p] = v
            else:
                press_ref[p] = v


def on_device(rhs_velocity, rhs_pressure, layer_ids, visc_table, stencil):
    planes, rows, depth = rhs_pressure.shape
    assert rows == SUB and depth == LANES
    x_count, y_count, z_count = (lax.axis_size(n) for n in ("gx", "gy", "gz"))
    kc = (stencil[13, 0, 0] + stencil[13, 1, 1] + stencil[13, 2, 2]) / 3.0
    table = jnp.stack([visc_table, 1.0 / (visc_table * kc)])
    coef = jnp.broadcast_to((stencil / kc).reshape(-1, 1), (stencil.size, LANES))

    tile = jax.ShapeDtypeStruct((FIELDS, SUB, LANES), jnp.float32)
    vmem = pl.BlockSpec(memory_space=pltpu.VMEM)
    main, z_first, z_second = pl.pallas_call(
        functools.partial(pack_kernel, planes),
        out_shape=(
            jax.ShapeDtypeStruct((FIELDS * planes, SUB, LANES), jnp.float32),
            tile,
            tile,
        ),
        in_specs=[pl.BlockSpec(memory_space=pltpu.SMEM), vmem, vmem, vmem],
        out_specs=(vmem, vmem, vmem),
        name="pack",
    )(table, rhs_velocity, rhs_pressure, layer_ids)

    halo = matched(z_first, "gz", first_pairs(z_count))
    halo = halo + matched(z_second, "gz", second_pairs(z_count))
    block = jnp.concatenate([main, halo])

    paired = x_count == 2
    if paired:
        frame = jnp.stack([block, lax.ppermute(block, "gx", [(0, 1), (1, 0)])])
        blocks = 2
    else:
        hops = -(-REACH // planes)
        parts = []
        for hop in range(-hops, hops + 1):
            pairs = [(i, i - hop) for i in range(x_count) if 0 <= i - hop < x_count]
            parts.append(block if hop == 0 else matched(block, "gx", pairs))
        frame = jnp.stack(parts)
        blocks = 2 * hops + 1

    y_first = matched(frame, "gy", first_pairs(y_count))
    y_second = matched(frame, "gy", second_pairs(y_count))

    stride = LANES + 2 * COLS
    tiles = -(-planes * blocks * stride // LANES)
    f32 = jnp.float32
    return pl.pallas_call(
        functools.partial(cycle_kernel, planes, blocks, paired),
        out_shape=(
            jax.ShapeDtypeStruct(rhs_velocity.shape, f32),
            jax.ShapeDtypeStruct(rhs_pressure.shape, f32),
        ),
        in_specs=[vmem] * 4,
        out_specs=(vmem, vmem),
        scratch_shapes=[
            pltpu.VMEM((FIELDS, tiles, ROWS, LANES), f32),
            pltpu.VMEM((3, tiles + 2 * PAD, ROWS, LANES), f32),
            pltpu.VMEM((9, 3, tiles, ROWS, LANES), f32),
            pltpu.VMEM((3, tiles, ROWS, LANES), f32),
            pltpu.VMEM((3, tiles, 2 * SUB, LANES), f32),
            pltpu.VMEM((4, tiles, 2 * SUB, LANES), f32),
            pltpu.VMEM((tiles + 2 * PAD, ROWS, LANES), f32),
            pltpu.VMEM((4, tiles + 1, SUB, LANES), f32),
        ],
        name="cycle",
    )(frame, y_first, y_second, coef)


def solution(mesh):
    placed = (P(None, "gx", "gy", "gz"), P("gx", "gy", "gz"), P("gx", "gy", "gz"), P(), P())
    return jax.shard_map(
        on_device,
        mesh=mesh,
        in_specs=placed,
        out_specs=(P(None, "gx", "gy", "gz"), P("gx", "gy", "gz")),
        check_vma=False,
    )
```

time: 209 us -> 40.8 us (0.20)
  the two profiles are of different devices: /device:TPU:1 before, /device:TPU:17 now
where the time goes in v1:
time: 40.8 us; the launch traced here: 40.5 us
  Pallas kernels  14.3 us (35%)
  starting transfers between devices  10.8 us (26%)
  waiting for transfers between devices  8.11 us (20%)
  local copies, waits for them, and re-layouts  3.08 us (8%)
  between operations  2.65 us (6%)
  other arithmetic  1.51 us (4%)
    pallas_call x1, Pallas kernels, on_device(): pl.pallas_call(functools.partial(cycle_kernel, planes, blocks, paired), o...  12.7 us
    ppermute x4, starting transfers between devices, matched(): return lax.ppermute(block, axis, pairs)  9.53 us
    ppermute x4, waiting for transfers between devices, matched(): return lax.ppermute(block, axis, pairs)  5.84 us
    ppermute x1, waiting for transfers between devices, on_device(): frame = jnp.stack([block, lax.ppermute(block, 'gx', [(0, 1), (1, 0)])])  2.27 us
    pallas_call x1, Pallas kernels, on_device(): pl.pallas_call(functools.partial(pack_kernel, planes), out_shape=(jax.Sha...  1.53 us
    slice x1, local copies, waits for them, and re-layouts, on_device(): kc = (stencil[13, 0, 0] + stencil[13, 1, 1] + stencil[13, 2, 2]) / 3.0  1.33 us
    ppermute x1, starting transfers between devices, on_device(): frame = jnp.stack([block, lax.ppermute(block, 'gx', [(0, 1), (1, 0)])])  1.3 us
    broadcast_in_dim x2, local copies, waits for them, and re-layouts, on_device(): jnp.broadcast_to((stencil / kc).reshape(-1, 1), (stencil.size, LANES))  0.97 us
  transfers between devices with their start and end apart: 5, of which 3 were waited for; matrix products, arithmetic and copies ran while one was open for 1% of the time, Pallas kernels for 0%

profile of v1, /device:TPU:17, one launch (start us, length us, event | category | flops | bytes accessed | tf_op | source)
XLA Modules:
  0.0 40.5 jit_solution(6544204121975921205)
XLA Ops:
  0.6 1.3 %fusion.1 = (f32[1,1,1]{0,2,1:T(1,128)}, f32[1,1,1]{0,2,1:T(1,128)}, f32[1,1,1]{0,2,1:T(1,128)}) fusion(f32[27,3,3]{0,2,1:T(4,128)} %param.9), kind=kLoop, calls=%fused_computation.6 | loop fusion | bytes 24 | tf_op jit(solution)/shard_map/slice | solution.py:445
  3.9 0.0 copy-start.4
  3.9 0.6 %copy-done.4 = f32[8]{0:T(128)S(1)} copy-done((f32[8]{0:T(128)S(1)}, f32[8]{0:T(128)}, u32[]{:S(2)}) %copy-start.4) | copy-done | bytes 56
  4.6 0.6 %pad_maximum_fusion.2.tab_ref = f32[2,8]{1,0:T(2,128)} fusion(f32[1,8]{1,0:T(1,128)S(1)} %divide_bitcast_fusion, f32[1,8]{1,0:T(1,128)S(1)} %bitcast.8), kind=kLoop, calls=%fused_computation.3 | loop fusion | flops 16 | bytes 128 | tf_op jit(solution)/shard_map/stack | solution.py:446
  5.1 1.5 %pack.1 = (f32[20,8,128]{2,1,0:T(8,128)}, f32[5,8,128]{2,1,0:T(8,128)}, f32[5,8,128]{2,1,0:T(8,128)}) custom-call(f32[2,8]{1,0:T(2,128)} %pad_maximum_fusion.2.tab_ref, f32[3,4,8,128]{3,2,1,0:T(8,128)} %rhs_ref.1, f32[4,8,128]{2,1,0:T(8,128)} %press_ref.1, s32[4,8,128]{2,1,0:T(8,128)} %ids_ref.1), custom_call_target="tpu_custom_call" | custom-call | tf_op jit(solution)/shard_map/pack/pallas_call | solution.py:451
  6.7 1.3 %collective-permute-start = (f32[5,8,128]{2,1,0:T(8,128)}, f32[5,8,128]{2,1,0:T(8,128)S(1)}, u32[]{:S(2)}, u32[]{:S(2)}) collective-permute-start(f32[5,8,128]{2,1,0:T(8,128)} %get-tuple-element.6), channel_id=1, source_target_pairs={{0,1},{1,0},{2,3},{3,2},{4,5},{5,4},{6,7},{7,6},{8,9},{9,8},{10,11... | collective-permute-start | bytes 61448 | tf_op jit(solution)/shard_map/ppermute | solution.py:46
  8.0 1.9 %collective-permute-start.1 = (f32[5,8,128]{2,1,0:T(8,128)}, f32[5,8,128]{2,1,0:T(8,128)S(1)}, u32[]{:S(2)}, u32[]{:S(2)}) collective-permute-start(f32[5,8,128]{2,1,0:T(8,128)} %get-tuple-element.7), channel_id=1, source_target_pairs={{1,2},{2,1},{5,6},{6,5},{9,10},{10,9},{13,14},{14,13},{17,18},{18,... | collective-permute-start | bytes 61448 | tf_op jit(solution)/shard_map/ppermute | solution.py:46
  9.9 0.0 collective-permute-done
  9.9 2.8 %collective-permute-done.1 = f32[5,8,128]{2,1,0:T(8,128)S(1)} collective-permute-done((f32[5,8,128]{2,1,0:T(8,128)}, f32[5,8,128]{2,1,0:T(8,128)S(1)}, u32[]{:S(2)}, u32[]{:S(2)}) %collective-permute-start.1) | collective-permute-done | bytes 20512 | tf_op jit(solution)/shard_map/ppermute | solution.py:46
  12.7 0.9 %fusion = (f32[1,25,8,128]{3,2,1,0:T(8,128)S(1)}, f32[25,8,128]{2,1,0:T(8,128)S(1)}) fusion(f32[5,8,128]{2,1,0:T(8,128)S(1)} %add.13, f32[20,8,128]{2,1,0:T(8,128)} %get-tuple-element.5), kind=kLoop, calls=%fused_computation.5 | loop fusion | flops 25600 | bytes 307200 | tf_op jit(solution)/shard_map/stack | solution.py:469
  13.6 1.3 %collective-permute-start.2 = (f32[25,8,128]{2,1,0:T(8,128)S(1)}, f32[25,8,128]{2,1,0:T(8,128)S(1)}, u32[]{:S(2)}, u32[]{:S(2)}) collective-permute-start(f32[25,8,128]{2,1,0:T(8,128)S(1)} %get-tuple-element.9), channel_id=1, source_target_pairs={{0,16},{16,0},{1,17},{17,1},{2,18},{18,2},{3,19},{19,3},{4,20},{20... | collective-permute-start | bytes 307208 | tf_op jit(solution)/shard_map/ppermute | solution.py:469
  14.9 2.3 %collective-permute-done.2 = f32[25,8,128]{2,1,0:T(8,128)S(1)} collective-permute-done((f32[25,8,128]{2,1,0:T(8,128)S(1)}, f32[25,8,128]{2,1,0:T(8,128)S(1)}, u32[]{:S(2)}, u32[]{:S(2)}) %collective-permute-start.2) | collective-permute-done | bytes 102432 | tf_op jit(solution)/shard_map/ppermute | solution.py:469
  17.2 0.0 copy-start.3
  17.2 0.0 copy-start
  17.2 6.3 %collective-permute-start.4 = (f32[2,25,8,128]{3,2,1,0:T(8,128)S(1)}, f32[2,25,8,128]{3,2,1,0:T(8,128)S(1)}, u32[]{:S(2)}, u32[]{:S(2)}) collective-permute-start(f32[2,25,8,128]{3,2,1,0:T(8,128)S(1)} %pad_maximum_fusion.own_ref), channel_id=1, source_target_pairs={{4,8},{8,4},{5,9},{9,5},{6,10},{10,6},{7,11},{11,7},{20,24},{24,20... | collective-permute-start | bytes 614408 | tf_op jit(solution)/shard_map/ppermute | solution.py:46
  23.5 0.1 collective-permute-start.3
  23.5 0.0 copy-done.3
  23.6 0.1 copy.7
  23.7 0.2 broadcast_in_dim.7
  23.9 3.0 %collective-permute-done.4.b_ref = f32[2,25,8,128]{3,2,1,0:T(8,128)S(1)} collective-permute-done((f32[2,25,8,128]{3,2,1,0:T(8,128)S(1)}, f32[2,25,8,128]{3,2,1,0:T(8,128)S(1)}, u32[]{:S(2)}, u32[]{:S(2)}) %collective-permute-start.4) | collective-permute-done | bytes 204832 | tf_op jit(solution)/shard_map/ppermute | solution.py:46
  26.9 0.0 copy-start.1
  26.9 0.0 collective-permute-done.3.a_ref
  26.9 0.0 copy-start.2
  26.9 0.8 %broadcast_in_dim.8.coef_ref = f32[243,128]{1,0:T(8,128)} broadcast(f32[243]{0:T(256)S(1)} %broadcast_in_dim.7), dimensions={0} | broadcast | bytes 125388 | tf_op jit(solution)/shard_map/broadcast_in_dim | solution.py:447
  27.7 0.0 copy-done
  27.7 0.0 copy-done.1
  27.7 0.0 copy-done.2
  27.7 12.7 %cycle.1 = (f32[3,4,8,128]{3,2,1,0:T(8,128)}, f32[4,8,128]{2,1,0:T(8,128)}) custom-call(f32[2,25,8,128]{3,2,1,0:T(8,128)} %copy-done, f32[2,25,8,128]{3,2,1,0:T(8,128)} %copy-done.2, f32[2,25,8,128]{3,2,1,0:T(8,128)} %copy-done.1, f32[243,128]{1,0:T(8,128)} %broadcast_in_dim.8.coef_ref), custom_call_target="tpu_custom_call" | custom-call | tf_op jit(solution)/shard_map/cycle/pallas_call | solution.py:486
  (4 shorter events, 0.0 us)
Async XLA Ops:
  3.9 0.7 %copy-start.4 = (f32[8]{0:T(128)S(1)}, f32[8]{0:T(128)}, u32[]{:S(2)}) copy-start(f32[8]{0:T(128)} %param.8) | copy-start | bytes 100
  6.7 3.2 %collective-permute-start = (f32[5,8,128]{2,1,0:T(8,128)}, f32[5,8,128]{2,1,0:T(8,128)S(1)}, u32[]{:S(2)}, u32[]{:S(2)}) collective-permute-start(f32[5,8,128]{2,1,0:T(8,128)} %get-tuple-element.6), channel_id=1, source_target_pairs={{0,1},{1,0},{2,3},{3,2},{4,5},{5,4},{6,7},{7,6},{8,9},{9,8},{10,11... | collective-permute-start | bytes 61448 | tf_op jit(solution)/shard_map/ppermute | solution.py:46
  8.0 4.7 %collective-permute-start.1 = (f32[5,8,128]{2,1,0:T(8,128)}, f32[5,8,128]{2,1,0:T(8,128)S(1)}, u32[]{:S(2)}, u32[]{:S(2)}) collective-permute-start(f32[5,8,128]{2,1,0:T(8,128)} %get-tuple-element.7), channel_id=1, source_target_pairs={{1,2},{2,1},{5,6},{6,5},{9,10},{10,9},{13,14},{14,13},{17,18},{18,... | collective-permute-start | bytes 61448 | tf_op jit(solution)/shard_map/ppermute | solution.py:46
  13.6 3.6 %collective-permute-start.2 = (f32[25,8,128]{2,1,0:T(8,128)S(1)}, f32[25,8,128]{2,1,0:T(8,128)S(1)}, u32[]{:S(2)}, u32[]{:S(2)}) collective-permute-start(f32[25,8,128]{2,1,0:T(8,128)S(1)} %get-tuple-element.9), channel_id=1, source_target_pairs={{0,16},{16,0},{1,17},{17,1},{2,18},{18,2},{3,19},{19,3},{4,20},{20... | collective-permute-start | bytes 307208 | tf_op jit(solution)/shard_map/ppermute | solution.py:469
  17.2 6.4 %copy-start.3 = (f32[27,3,3]{0,2,1:T(4,128)S(1)}, f32[27,3,3]{0,2,1:T(4,128)}, u32[]{:S(2)}) copy-start(f32[27,3,3]{0,2,1:T(4,128)} %param.9) | copy-start | bytes 2920
  17.2 10.5 %copy-start = (f32[2,25,8,128]{3,2,1,0:T(8,128)}, f32[2,25,8,128]{3,2,1,0:T(8,128)S(1)}, u32[]{:S(2)}) copy-start(f32[2,25,8,128]{3,2,1,0:T(8,128)S(1)} %pad_maximum_fusion.own_ref) | copy-start | bytes 614404
  17.2 9.7 %collective-permute-start.4 = (f32[2,25,8,128]{3,2,1,0:T(8,128)S(1)}, f32[2,25,8,128]{3,2,1,0:T(8,128)S(1)}, u32[]{:S(2)}, u32[]{:S(2)}) collective-permute-start(f32[2,25,8,128]{3,2,1,0:T(8,128)S(1)} %pad_maximum_fusion.own_ref), channel_id=1, source_target_pairs={{4,8},{8,4},{5,9},{9,5},{6,10},{10,6},{7,11},{11,7},{20,24},{24,20... | collective-permute-start | bytes 614408 | tf_op jit(solution)/shard_map/ppermute | solution.py:46
  23.5 3.4 %collective-permute-start.3 = (f32[2,25,8,128]{3,2,1,0:T(8,128)S(1)}, f32[2,25,8,128]{3,2,1,0:T(8,128)S(1)}, u32[]{:S(2)}, u32[]{:S(2)}) collective-permute-start(f32[2,25,8,128]{3,2,1,0:T(8,128)S(1)} %pad_maximum_fusion.own_ref), channel_id=1, source_target_pairs={{0,4},{4,0},{8,12},{12,8},{1,5},{5,1},{9,13},{13,9},{2,6},{6,2},{1... | collective-permute-start | bytes 614408 | tf_op jit(solution)/shard_map/ppermute | solution.py:46
  26.9 0.8 %copy-start.1 = (f32[2,25,8,128]{3,2,1,0:T(8,128)}, f32[2,25,8,128]{3,2,1,0:T(8,128)S(1)}, u32[]{:S(2)}) copy-start(f32[2,25,8,128]{3,2,1,0:T(8,128)S(1)} %collective-permute-done.4.b_ref) | copy-start | bytes 614404
  26.9 0.8 %copy-start.2 = (f32[2,25,8,128]{3,2,1,0:T(8,128)}, f32[2,25,8,128]{3,2,1,0:T(8,128)S(1)}, u32[]{:S(2)}) copy-start(f32[2,25,8,128]{3,2,1,0:T(8,128)S(1)} %collective-permute-done.3.a_ref) | copy-start | bytes 614404

commit v2 on v1

--- a/solution.py
+++ b/solution.py
@@ -18,6 +18,8 @@
 PAD = 3
 ROWS = 5 * SUB
 OWN = 2 * SUB
+SMALL_VMEM = 4 * 1024 * 1024
+CYCLE_VMEM = 32 * 1024 * 1024
 
 
 def cheb_consts():
@@ -50,33 +52,73 @@
     return lax.broadcasted_iota(jnp.int32, (SUB, LANES), 1)
 
 
-def pack_kernel(planes, tab_ref, rhs_ref, press_ref, ids_ref, main_ref, a_ref, b_ref):
+def diagonal_mean(stencil_ref):
+    middle = stencil_ref.shape[2] // 2
+    return (stencil_ref[0, 0, middle] + stencil_ref[1, 1, middle] + stencil_ref[2, 2, middle]) / 3.0
+
+
+def coef_kernel(stencil_ref, coef_ref):
+    scale = 1.0 / jnp.full((1, LANES), diagonal_mean(stencil_ref), jnp.float32)
+    for i in range(3):
+        for j in range(3):
+            for o in range(stencil_ref.shape[2]):
+                n = o * 9 + i * 3 + j
+                coef_ref[n : n + 1, :] = scale * stencil_ref[i, j, o]
+
+
+def pack_kernel(
+    planes,
+    visc_hbm,
+    stencil_hbm,
+    rhs_hbm,
+    press_hbm,
+    ids_hbm,
+    main_ref,
+    a_ref,
+    b_ref,
+    visc_ref,
+    stencil_ref,
+    rhs_ref,
+    press_ref,
+    ids_ref,
+    arrived,
+):
+    copies = [
+        pltpu.make_async_copy(src, dst, arrived.at[n])
+        for n, (src, dst) in enumerate(
+            (
+                (visc_hbm, visc_ref),
+                (stencil_hbm, stencil_ref),
+                (ids_hbm, ids_ref),
+                (rhs_hbm, rhs_ref),
+                (press_hbm, press_ref),
+            )
+        )
+    ]
+    for copy in copies:
+        copy.start()
+    for copy in copies:
+        copy.wait()
     lane = lane_iota()
     odd = lax.axis_index("gz") % 2 == 1
-    layers = tab_ref.shape[1]
-    for f in range(FIELDS):
-        a_ref[f] = jnp.zeros((SUB, LANES), jnp.float32)
-        b_ref[f] = jnp.zeros((SUB, LANES), jnp.float32)
+    kc = jnp.full((SUB, LANES), diagonal_mean(stencil_ref), jnp.float32)
     up = [jnp.zeros((SUB, LANES), jnp.float32)] * FIELDS
     down = [jnp.zeros((SUB, LANES), jnp.float32)] * FIELDS
     width = 2 * COLS
     for p in range(planes):
         ids = ids_ref[p]
         eta = jnp.zeros((SUB, LANES), jnp.float32)
-        dinv = jnp.zeros((SUB, LANES), jnp.float32)
-        for layer in range(layers):
-            hit = ids == layer
-            eta = jnp.where(hit, tab_ref[0, layer], eta)
-            dinv = jnp.where(hit, tab_ref[1, layer], dinv)
+        for layer in range(visc_ref.shape[0]):
+            eta = jnp.where(ids == layer, visc_ref[layer], eta)
+        dinv = 1.0 / (eta * kc)
         values = [rhs_ref[j, p] * dinv for j in range(3)]
         values += [eta, eta * press_ref[p] * (1.0 / 9.0)]
         for f in range(FIELDS):
             main_ref[f * planes + p] = values[f]
-            high = pltpu.roll(values[f], (p * width + COLS) % LANES, 1)
-            up[f] = jnp.where((lane >= p * width) & (lane < p * width + COLS), high, up[f])
-            low = pltpu.roll(values[f], (p * width + COLS) % LANES, 1)
+            turned = pltpu.roll(values[f], (p * width + COLS) % LANES, 1)
+            up[f] = jnp.where((lane >= p * width) & (lane < p * width + COLS), turned, up[f])
             down[f] = jnp.where(
-                (lane >= p * width + COLS) & (lane < (p + 1) * width), low, down[f]
+                (lane >= p * width + COLS) & (lane < (p + 1) * width), turned, down[f]
             )
     for f in range(FIELDS):
         a_ref[f] = jnp.where(odd, down[f], up[f])
@@ -442,12 +484,19 @@
     planes, rows, depth = rhs_pressure.shape
     assert rows == SUB and depth == LANES
     x_count, y_count, z_count = (lax.axis_size(n) for n in ("gx", "gy", "gz"))
-    kc = (stencil[13, 0, 0] + stencil[13, 1, 1] + stencil[13, 2, 2]) / 3.0
-    table = jnp.stack([visc_table, 1.0 / (visc_table * kc)])
-    coef = jnp.broadcast_to((stencil / kc).reshape(-1, 1), (stencil.size, LANES))
+    entries = jnp.transpose(stencil, (1, 2, 0))
 
     tile = jax.ShapeDtypeStruct((FIELDS, SUB, LANES), jnp.float32)
     vmem = pl.BlockSpec(memory_space=pltpu.VMEM)
+    smem = pl.BlockSpec(memory_space=pltpu.SMEM)
+    coef = pl.pallas_call(
+        coef_kernel,
+        out_shape=jax.ShapeDtypeStruct((stencil.size, LANES), jnp.float32),
+        in_specs=[smem],
+        out_specs=vmem,
+        compiler_params=pltpu.CompilerParams(vmem_limit_bytes=SMALL_VMEM),
+        name="coef",
+    )(entries)
     main, z_first, z_second = pl.pallas_call(
         functools.partial(pack_kernel, planes),
         out_shape=(
@@ -455,10 +504,24 @@
             tile,
             tile,
         ),
-        in_specs=[pl.BlockSpec(memory_space=pltpu.SMEM), vmem, vmem, vmem],
+        in_specs=[pl.BlockSpec(memory_space=pltpu.HBM)] * 5,
         out_specs=(vmem, vmem, vmem),
+        scratch_shapes=[
+            pltpu.SMEM(visc_table.shape, visc_table.dtype),
+            pltpu.SMEM(entries.shape, entries.dtype),
+            pltpu.VMEM(rhs_velocity.shape, rhs_velocity.dtype),
+            pltpu.VMEM(rhs_pressure.shape, rhs_pressure.dtype),
+            pltpu.VMEM(layer_ids.shape, layer_ids.dtype),
+            pltpu.SemaphoreType.DMA((5,)),
+        ],
+        compiler_params=pltpu.CompilerParams(vmem_limit_bytes=SMALL_VMEM),
         name="pack",
-    )(table, rhs_velocity, rhs_pressure, layer_ids)
+    )(
+        *(
+            pltpu.with_memory_space_constraint(v, pltpu.HBM)
+            for v in (visc_table, entries, rhs_velocity, rhs_pressure, layer_ids)
+        )
+    )
 
     halo = matched(z_first, "gz", first_pairs(z_count))
     halo = halo + matched(z_second, "gz", second_pairs(z_count))
@@ -501,6 +564,7 @@
             pltpu.VMEM((tiles + 2 * PAD, ROWS, LANES), f32),
             pltpu.VMEM((4, tiles + 1, SUB, LANES), f32),
         ],
+        compiler_params=pltpu.CompilerParams(vmem_limit_bytes=CYCLE_VMEM),
         name="cycle",
     )(frame, y_first, y_second, coef)
 

time: 40.8 us -> 32.6 us (0.80)
  local copies, waits for them, and re-layouts: 3.08 us -> 0.01 us
  between operations: 2.65 us -> 0.69 us
  other arithmetic: 1.51 us -> 0.04 us
  Pallas kernels: 14.3 us -> 13.3 us
  waiting for transfers between devices: 8.11 us -> 7.48 us
    slice x1 -> x0, local copies, waits for them, and re-layouts: 1.33 us -> none  [on_device(): kc = (stencil[13, 0, 0] + stencil[13, 1, 1] + stencil[13, 2, 2]) / 3.0]
    pallas_call x1, Pallas kernels: 12.7 us -> 11.6 us  [on_device(): pl.pallas_call(functools.partial(cycle_kernel, planes, blocks, paired), o...]
    broadcast_in_dim x2 -> x0, local copies, waits for them, and re-layouts: 0.97 us -> none  [on_device(): jnp.broadcast_to((stencil / kc).reshape(-1, 1), (stencil.size, LANES))]
    another operation x2, other arithmetic: 0.91 us -> 0.04 us  [on_device(): frame = jnp.stack([block, lax.ppermute(block, 'gx', [(0, 1), (1, 0)])])]
    pallas_call x0 -> x1, Pallas kernels: none -> 0.71 us  [on_device(): pl.pallas_call(coef_kernel, out_shape=jax.ShapeDtypeStruct((stencil.size,...]
    unnamed x10 -> x2, local copies, waits for them, and re-layouts: 0.67 us -> 0.01 us
    ppermute x4, waiting for transfers between devices: 5.84 us -> 5.21 us  [matched(): return lax.ppermute(block, axis, pairs)]
    another operation x2 -> x0, other arithmetic: 0.58 us -> none  [on_device(): table = jnp.stack([visc_table, 1.0 / (visc_table * kc)])]
  transfers between devices with their start and end apart: 5 -> 5, of which waited for: 3 -> 3; matrix products, arithmetic and copies ran while one was open for 1% -> 0% of each run, Pallas kernels for 0% -> 2%
where the time goes in v2:
time: 32.6 us; the launch traced here: 32.4 us
  Pallas kernels  13.3 us (41%)
  starting transfers between devices  10.9 us (33%)
  waiting for transfers between devices  7.48 us (23%)
  between operations  0.69 us (2%)
    pallas_call x1, Pallas kernels, on_device(): pl.pallas_call(functools.partial(cycle_kernel, planes, blocks, paired), o...  11.6 us
    ppermute x4, starting transfers between devices, matched(): return lax.ppermute(block, axis, pairs)  9.59 us
    ppermute x4, waiting for transfers between devices, matched(): return lax.ppermute(block, axis, pairs)  5.21 us
    ppermute x1, waiting for transfers between devices, on_device(): frame = jnp.stack([block, lax.ppermute(block, 'gx', [(0, 1), (1, 0)])])  2.27 us
    ppermute x1, starting transfers between devices, on_device(): frame = jnp.stack([block, lax.ppermute(block, 'gx', [(0, 1), (1, 0)])])  1.3 us
    pallas_call x1, Pallas kernels, on_device(): pl.pallas_call(functools.partial(pack_kernel, planes), out_shape=(jax.Sha...  0.96 us
    pallas_call x1, Pallas kernels, on_device(): pl.pallas_call(coef_kernel, out_shape=jax.ShapeDtypeStruct((stencil.size,...  0.71 us
  transfers between devices with their start and end apart: 5, of which 3 were waited for; matrix products, arithmetic and copies ran while one was open for 0% of the time, Pallas kernels for 2%

profile of v2, /device:TPU:17, one launch (start us, length us, event | category | flops | bytes accessed | tf_op | source)
XLA Modules:
  0.0 32.4 jit_solution(3859029316114126657)
XLA Ops:
  0.6 1.0 %pack.1 = (f32[20,8,128]{2,1,0:T(8,128)S(1)}, f32[5,8,128]{2,1,0:T(8,128)S(1)}, f32[5,8,128]{2,1,0:T(8,128)S(1)}) custom-call(f32[8]{0:T(128)} %visc_hbm.1, f32[3,3,27]{2,1,0:T(4,128)} %bitcast.4, f32[3,4,8,128]{3,2,1,0:T(8,128)} %rhs_hbm.1, f32[4,8,128]{2,1,0:T(8,128)} %press_hbm.1, s32[4,8,128]{2,1,0:T(8,128)} %ids_hbm.1), custom_call_target="tpu_custom_call" | custom-call | tf_op jit(solution)/shard_map/pack/pallas_call | solution.py:500
  1.6 1.4 %collective-permute-start = (f32[5,8,128]{2,1,0:T(8,128)S(1)}, f32[5,8,128]{2,1,0:T(8,128)S(1)}, u32[]{:S(2)}, u32[]{:S(2)}) collective-permute-start(f32[5,8,128]{2,1,0:T(8,128)S(1)} %get-tuple-element.6), channel_id=1, source_target_pairs={{0,1},{1,0},{2,3},{3,2},{4,5},{5,4},{6,7},{7,6},{8,9},{9,8},{10,11... | collective-permute-start | bytes 61448 | tf_op jit(solution)/shard_map/ppermute | solution.py:48
  3.0 1.9 %collective-permute-start.1 = (f32[5,8,128]{2,1,0:T(8,128)S(1)}, f32[5,8,128]{2,1,0:T(8,128)S(1)}, u32[]{:S(2)}, u32[]{:S(2)}) collective-permute-start(f32[5,8,128]{2,1,0:T(8,128)S(1)} %get-tuple-element.7), channel_id=1, source_target_pairs={{1,2},{2,1},{5,6},{6,5},{9,10},{10,9},{13,14},{14,13},{17,18},{18,... | collective-permute-start | bytes 61448 | tf_op jit(solution)/shard_map/ppermute | solution.py:48
  4.9 0.0 collective-permute-done
  4.9 2.6 %collective-permute-done.1 = f32[5,8,128]{2,1,0:T(8,128)S(1)} collective-permute-done((f32[5,8,128]{2,1,0:T(8,128)S(1)}, f32[5,8,128]{2,1,0:T(8,128)S(1)}, u32[]{:S(2)}, u32[]{:S(2)}) %collective-permute-start.1) | collective-permute-done | bytes 20512 | tf_op jit(solution)/shard_map/ppermute | solution.py:48
  7.5 1.3 %collective-permute-start.2 = (f32[25,8,128]{2,1,0:T(8,128)S(1)}, f32[25,8,128]{2,1,0:T(8,128)S(1)}, u32[]{:S(2)}, u32[]{:S(2)}) collective-permute-start(f32[25,8,128]{2,1,0:T(8,128)S(1)} %get-tuple-element.9), channel_id=1, source_target_pairs={{0,16},{16,0},{1,17},{17,1},{2,18},{18,2},{3,19},{19,3},{4,20},{20... | collective-permute-start | bytes 307208 | tf_op jit(solution)/shard_map/ppermute | solution.py:532
  8.8 2.3 %collective-permute-done.2 = f32[25,8,128]{2,1,0:T(8,128)S(1)} collective-permute-done((f32[25,8,128]{2,1,0:T(8,128)S(1)}, f32[25,8,128]{2,1,0:T(8,128)S(1)}, u32[]{:S(2)}, u32[]{:S(2)}) %collective-permute-start.2) | collective-permute-done | bytes 102432 | tf_op jit(solution)/shard_map/ppermute | solution.py:532
  11.1 0.0 copy-start
  11.1 6.3 %collective-permute-start.4 = (f32[2,25,8,128]{3,2,1,0:T(8,128)S(1)}, f32[2,25,8,128]{3,2,1,0:T(8,128)S(1)}, u32[]{:S(2)}, u32[]{:S(2)}) collective-permute-start(f32[2,25,8,128]{3,2,1,0:T(8,128)S(1)} %pad_maximum_fusion.own_ref), channel_id=1, source_target_pairs={{4,8},{8,4},{5,9},{9,5},{6,10},{10,6},{7,11},{11,7},{20,24},{24,20... | collective-permute-start | bytes 614408 | tf_op jit(solution)/shard_map/ppermute | solution.py:48
  17.4 0.1 collective-permute-start.3
  17.4 0.0 copy-done
  17.5 0.7 %coef.1.coef_ref = f32[243,128]{1,0:T(8,128)S(1)} custom-call(f32[3,3,27]{2,1,0:T(4,128)S(1)} %bitcast.5), custom_call_target="tpu_custom_call" | custom-call | tf_op jit(solution)/shard_map/coef/pallas_call | solution.py:492
  18.2 2.6 %collective-permute-done.4.b_ref = f32[2,25,8,128]{3,2,1,0:T(8,128)S(1)} collective-permute-done((f32[2,25,8,128]{3,2,1,0:T(8,128)S(1)}, f32[2,25,8,128]{3,2,1,0:T(8,128)S(1)}, u32[]{:S(2)}, u32[]{:S(2)}) %collective-permute-start.4) | collective-permute-done | bytes 204832 | tf_op jit(solution)/shard_map/ppermute | solution.py:48
  20.8 0.0 collective-permute-done.3.a_ref
  20.8 11.6 %cycle.1 = (f32[3,4,8,128]{3,2,1,0:T(8,128)}, f32[4,8,128]{2,1,0:T(8,128)}) custom-call(f32[2,25,8,128]{3,2,1,0:T(8,128)S(1)} %pad_maximum_fusion.own_ref, f32[2,25,8,128]{3,2,1,0:T(8,128)S(1)} %collective-permute-done.3.a_ref, f32[2,25,8,128]{3,2,1,0:T(8,128)S(1)} %collective-permute-done.4.b_ref, f32[243,128]{1,0:T(8,128)S(1)} %coef.1.coef_ref), custom_call_target="tpu_custom_call" | custom-call | tf_op jit(solution)/shard_map/cycle/pallas_call | solution.py:549
  (3 shorter events, 0.0 us)
Async XLA Ops:
  1.6 3.3 %collective-permute-start = (f32[5,8,128]{2,1,0:T(8,128)S(1)}, f32[5,8,128]{2,1,0:T(8,128)S(1)}, u32[]{:S(2)}, u32[]{:S(2)}) collective-permute-start(f32[5,8,128]{2,1,0:T(8,128)S(1)} %get-tuple-element.6), channel_id=1, source_target_pairs={{0,1},{1,0},{2,3},{3,2},{4,5},{5,4},{6,7},{7,6},{8,9},{9,8},{10,11... | collective-permute-start | bytes 61448 | tf_op jit(solution)/shard_map/ppermute | solution.py:48
  3.0 4.5 %collective-permute-start.1 = (f32[5,8,128]{2,1,0:T(8,128)S(1)}, f32[5,8,128]{2,1,0:T(8,128)S(1)}, u32[]{:S(2)}, u32[]{:S(2)}) collective-permute-start(f32[5,8,128]{2,1,0:T(8,128)S(1)} %get-tuple-element.7), channel_id=1, source_target_pairs={{1,2},{2,1},{5,6},{6,5},{9,10},{10,9},{13,14},{14,13},{17,18},{18,... | collective-permute-start | bytes 61448 | tf_op jit(solution)/shard_map/ppermute | solution.py:48
  7.5 3.6 %collective-permute-start.2 = (f32[25,8,128]{2,1,0:T(8,128)S(1)}, f32[25,8,128]{2,1,0:T(8,128)S(1)}, u32[]{:S(2)}, u32[]{:S(2)}) collective-permute-start(f32[25,8,128]{2,1,0:T(8,128)S(1)} %get-tuple-element.9), channel_id=1, source_target_pairs={{0,16},{16,0},{1,17},{17,1},{2,18},{18,2},{3,19},{19,3},{4,20},{20... | collective-permute-start | bytes 307208 | tf_op jit(solution)/shard_map/ppermute | solution.py:532
  11.1 6.4 %copy-start = (f32[27,3,3]{0,2,1:T(4,128)S(1)}, f32[27,3,3]{0,2,1:T(4,128)}, u32[]{:S(2)}) copy-start(f32[27,3,3]{0,2,1:T(4,128)} %param.9) | copy-start | bytes 2920
  11.1 9.7 %collective-permute-start.4 = (f32[2,25,8,128]{3,2,1,0:T(8,128)S(1)}, f32[2,25,8,128]{3,2,1,0:T(8,128)S(1)}, u32[]{:S(2)}, u32[]{:S(2)}) collective-permute-start(f32[2,25,8,128]{3,2,1,0:T(8,128)S(1)} %pad_maximum_fusion.own_ref), channel_id=1, source_target_pairs={{4,8},{8,4},{5,9},{9,5},{6,10},{10,6},{7,11},{11,7},{20,24},{24,20... | collective-permute-start | bytes 614408 | tf_op jit(solution)/shard_map/ppermute | solution.py:48
  17.4 3.4 %collective-permute-start.3 = (f32[2,25,8,128]{3,2,1,0:T(8,128)S(1)}, f32[2,25,8,128]{3,2,1,0:T(8,128)S(1)}, u32[]{:S(2)}, u32[]{:S(2)}) collective-permute-start(f32[2,25,8,128]{3,2,1,0:T(8,128)S(1)} %pad_maximum_fusion.own_ref), channel_id=1, source_target_pairs={{0,4},{4,0},{8,12},{12,8},{1,5},{5,1},{9,13},{13,9},{2,6},{6,2},{1... | collective-permute-start | bytes 614408 | tf_op jit(solution)/shard_map/ppermute | solution.py:48

commit v3 on v2

--- a/solution.py
+++ b/solution.py
@@ -16,8 +16,12 @@
 REACH = 6
 FIELDS = 5
 PAD = 3
-ROWS = 5 * SUB
-OWN = 2 * SUB
+ROWS = 3 * SUB
+OWN = SUB
+ROWS_RESID = OWN - 4
+ROWS_START = OWN - 2
+ROWS_MIDDLE = OWN - 1
+DEPTH = 2 * LANES
 SMALL_VMEM = 4 * 1024 * 1024
 CYCLE_VMEM = 32 * 1024 * 1024
 
@@ -57,13 +61,53 @@
     return (stencil_ref[0, 0, middle] + stencil_ref[1, 1, middle] + stencil_ref[2, 2, middle]) / 3.0
 
 
-def coef_kernel(stencil_ref, coef_ref):
-    scale = 1.0 / jnp.full((1, LANES), diagonal_mean(stencil_ref), jnp.float32)
-    for i in range(3):
-        for j in range(3):
-            for o in range(stencil_ref.shape[2]):
-                n = o * 9 + i * 3 + j
-                coef_ref[n : n + 1, :] = scale * stencil_ref[i, j, o]
+def band_kernel(stencil_ref, smooth_ref, resid_ref, coarse_ref, middle_ref):
+    scale = 1.0 / jnp.full((SUB, LANES), diagonal_mean(stencil_ref), jnp.float32)
+    sub = lax.broadcasted_iota(jnp.int32, (SUB, LANES), 0)
+    lane = lane_iota()
+    parts = []
+    for half in range(DEPTH // LANES):
+        spot = lane + half * LANES
+        chunk = jnp.zeros((SUB, LANES), jnp.int32)
+        for n in range(1, DEPTH // ROWS + 1):
+            chunk = jnp.where(spot >= n * ROWS, n, chunk)
+        used = chunk < 9
+        reach = jnp.where(used, spot - chunk * ROWS - sub, 1000)
+        term = chunk // 3
+        parts.append((reach, chunk - 3 * term, term == 2))
+    for a in range(3):
+        for c in range(3):
+            for i in range(3):
+                rows_of = []
+                for b in range(3):
+                    entry = [
+                        scale * stencil_ref[i, j, 9 * a + 3 * b + c] for j in range(3)
+                    ]
+                    row = []
+                    for reach, j_at, low_at in parts:
+                        full = jnp.where(
+                            j_at == 0, entry[0], jnp.where(j_at == 1, entry[1], entry[2])
+                        )
+                        high = full.astype(jnp.bfloat16).astype(jnp.float32)
+                        row.append(jnp.where(low_at, full - high, high))
+                    rows_of.append(row)
+                for ref, start, step in (
+                    (smooth_ref, 0, 1),
+                    (resid_ref, ROWS_RESID, 1),
+                    (coarse_ref, ROWS_START, 2),
+                    (middle_ref, ROWS_MIDDLE, 1),
+                ):
+                    for r in range(ref.shape[1] // SUB):
+                        for half, (reach, j_at, low_at) in enumerate(parts):
+                            value = jnp.zeros((SUB, LANES), jnp.float32)
+                            for b in range(3):
+                                at = r * SUB + start + step * (b - 1)
+                                value = jnp.where(reach == at, rows_of[b][half], value)
+                            ref[
+                                (3 * a + c) * 3 + i,
+                                r * SUB : (r + 1) * SUB,
+                                half * LANES : (half + 1) * LANES,
+                            ] = value
 
 
 def pack_kernel(
@@ -138,12 +182,16 @@
     own_ref,
     a_ref,
     b_ref,
-    coef_ref,
+    smooth_ref,
+    resid_band,
+    coarse_ref,
+    middle_ref,
     vel_ref,
     press_ref,
     fields,
     work,
-    shifted,
+    split,
+    products,
     second_x,
     resid,
     sums,
@@ -175,11 +223,16 @@
     def slot(q):
         return (q + gx) % 2 if paired else q
 
-    for k in list(range(PAD)) + list(range(PAD + tiles, 2 * PAD + tiles)):
-        for r in range(1, 4):
-            for j in range(3):
-                work[j, k, r * SUB : (r + 1) * SUB, :] = zero
+    edges = list(range(PAD)) + list(range(PAD + tiles, 2 * PAD + tiles))
+    for k in edges:
+        for r in range(3):
             press[k, r * SUB : (r + 1) * SUB, :] = zero
+        for n in range(27):
+            for r in range(2):
+                products[k, (n * 2 + r) * SUB : (n * 2 + r + 1) * SUB, :] = zero
+    for k in range(tiles):
+        for r in range(3 * 3 * 3, DEPTH // SUB):
+            split[r * SUB : (r + 1) * SUB, k * LANES : (k + 1) * LANES] = zero
 
     def assemble(src, row):
         for f in range(FIELDS):
@@ -230,7 +283,7 @@
                     value = tile if value is None else jnp.where(lane >= start, tile, value)
                 fields[f, k, row : row + SUB, :] = value
                 if f < 3:
-                    work[f, PAD + k, row : row + SUB, :] = value
+                    work[f, k, row : row + SUB, :] = value
                 if f == 4:
                     press[PAD + k, row : row + SUB, :] = value
 
@@ -262,97 +315,77 @@
 
         return tile
 
-    def make_shifts(base, count, rows, scale):
+    def apply(src, count, dst, spots, band_ref, first, rows, scale, emit):
+        height = rows * SUB
         for j in range(3):
-            for row in rows:
-                def load(k, j=j, row=row):
-                    return work[j, PAD + base + k, row : row + SUB, :]
-
-                readers = {}
+            for r in range(3):
+                at = (j * 3 + r) * SUB
+                for k in range(count):
+                    v = work[j, src + k, r * SUB : (r + 1) * SUB, :]
+                    high = v.astype(jnp.bfloat16).astype(jnp.float32)
+                    lanes = slice(k * LANES, (k + 1) * LANES)
+                    split[at : at + SUB, lanes] = high
+                    split[at + 3 * ROWS : at + 3 * ROWS + SUB, lanes] = v - high
+                    split[at + 6 * ROWS : at + 6 * ROWS + SUB, lanes] = high
+        band = band_ref[:, first : first + height, :].reshape(27 * height, DEPTH)
+        for k in range(0, count, 2):
+            width = min(2, count - k)
+            product = jnp.dot(
+                band,
+                split[:, k * LANES : (k + width) * LANES],
+                preferred_element_type=jnp.float32,
+                precision=lax.Precision.DEFAULT,
+            )
+            for w in range(width):
+                products[PAD + k + w, : 27 * height, :] = product[:, w * LANES : (w + 1) * LANES]
+        shift = dst - src
+        if not isinstance(shift, int):
+            for k in range(count, min(count + 2, tiles)):
+                for n in range(27 * rows):
+                    products[PAD + k, n * SUB : (n + 1) * SUB, :] = zero
+        for r in range(rows):
+            for i in range(3):
+                readers = []
                 for a in range(3):
                     for c in range(3):
-                        if (a, c) != (1, 1):
-                            readers[a * 3 + c] = shift_reader(
-                                load, ((a - 1) * stride + (c - 1)) * scale
-                            )
-                for k in range(count):
-                    for n, reader in readers.items():
-                        shifted[n, j, k, row : row + SUB, :] = reader(k)
-
-    def apply(base, count, rows, scale, group, emit):
-        def step(first, width):
-            spots = [(first + g, row) for g in range(width) for row in rows]
-            totals = [[None] * 3 for _ in spots]
-            for a in range(3):
-                for c in range(3):
-                    for b in range(3):
-                        for j in range(3):
-                            values = []
-                            for k, row in spots:
-                                at = row + (b - 1) * scale
-                                if (a, c) == (1, 1):
-                                    v = work[j, PAD + base + k, at : at + SUB, :]
-                                else:
-                                    v = shifted[a * 3 + c, j, k, at : at + SUB, :]
-                                values.append(v)
-                            for i in range(3):
-                                n = (9 * a + 3 * b + c) * 9 + i * 3 + j
-                                coef = jnp.broadcast_to(coef_ref[n : n + 1, :], (SUB, LANES))
-                                for s, v in enumerate(values):
-                                    term = coef * v
-                                    old = totals[s][i]
-                                    totals[s][i] = term if old is None else old + term
-            results = []
-            for (k, row), sums_of in zip(spots, totals):
-                results.append(emit(base + k, row, sums_of))
-            for stores in results:
-                for ref, index, value in stores:
-                    ref[index] = value
-
-        whole = count // group
-        if whole > 1:
-            def body(n, _):
-                step(n * group, group)
-                return 0
-
-            lax.fori_loop(0, whole, body, 0)
-        elif whole == 1:
-            step(0, group)
-        if count % group:
-            step(whole * group, count % group)
+                        row = ((3 * a + c) * 3 + i) * height + r * SUB
+
+                        def load(k, row=row):
+                            if isinstance(shift, int) and not 0 <= shift + k < count:
+                                return zero
+                            return products[PAD + shift + k, row : row + SUB, :]
+
+                        offset = ((a - 1) * stride + (c - 1)) * scale
+                        readers.append(shift_reader(load, offset))
+                for k in range(spots):
+                    total_of = readers[0](k)
+                    for reader in readers[1:]:
+                        total_of = total_of + reader(k)
+                    emit(dst + k, r, i, total_of)
 
     def inside(k, row):
         return fields[3, k, row : row + SUB, :] > 0.0
 
-    def emit_first(k, row, sums_of):
-        keep = inside(k, row)
-        stores = []
-        for i in range(3):
-            f0 = fields[i, k, row : row + SUB, :]
-            value = jnp.where(keep, (1.0 + carry + weight) * f0 - weight * sums_of[i], 0.0)
-            stores.append((work, (i, PAD + k, pl.ds(row, SUB), slice(None)), value))
-            stores.append((second_x, (i, k, pl.ds(row, SUB), slice(None)), value))
-        return stores
-
-    make_shifts(0, tiles, [OWN - SUB, OWN, OWN + SUB], 1)
-    apply(0, tiles, [OWN - SUB, OWN, OWN + SUB], 1, 1, emit_first)
-
-    def emit_resid(k, row, sums_of):
-        eta = fields[3, k, row : row + SUB, :]
-        stores = []
-        for i in range(3):
-            value = eta * (fields[i, k, row : row + SUB, :] - sums_of[i])
-            at = row - (OWN - SUB // 2)
-            stores.append((resid, (i, k, pl.ds(at, SUB), slice(None)), value))
-        return stores
-
-    make_shifts(0, tiles, [OWN - SUB, OWN, OWN + SUB], 1)
-    apply(0, tiles, [OWN - SUB // 2, OWN + SUB // 2], 1, 1, emit_resid)
+    def emit_first(k, r, i, total_of):
+        at = slice(r * SUB, (r + 1) * SUB)
+        value = (1.0 + carry + weight) * fields[i, k, at, :] - weight * total_of
+        value = jnp.where(inside(k, r * SUB), value, 0.0)
+        work[i, k, at, :] = value
+        second_x[i, k, at, :] = value
+
+    apply(0, tiles, 0, tiles, smooth_ref, 0, 3, 1, emit_first)
+
+    def emit_resid(k, r, i, total_of):
+        at = slice(ROWS_RESID + r * SUB, ROWS_RESID + (r + 1) * SUB)
+        value = fields[3, k, at, :] * (fields[i, k, at, :] - total_of)
+        resid[i, k, r * SUB : (r + 1) * SUB, :] = value
+
+    apply(0, tiles, 0, tiles, resid_band, 0, 2, 1, emit_resid)
 
     lane_even = lane % 2 == 0
     row_even = lax.broadcasted_iota(jnp.int32, (SUB, LANES), 0) % 2 == 0
     for r in range(2):
-        row = OWN - SUB // 2 + r * SUB
+        row = ROWS_RESID + r * SUB
         for k in range(tiles):
             for f in range(4):
                 if f < 3:
@@ -381,50 +414,35 @@
                 if f == 3:
                     scale_at[k] = jnp.where(v > 0.0, 4.0 / v, 0.0)
                 else:
-                    work[f, PAD + k, row : row + SUB, :] = v * scale_at[k]
-
-    def emit_start(k, row, sums_of):
-        keep = inside(k, row)
-        stores = []
-        for i in range(3):
-            fc = work[i, PAD + k, row : row + SUB, :]
-            value = second_x[i, k, row : row + SUB, :] + (1.0 + carry + weight) * fc
-            value = jnp.where(keep, value - weight * sums_of[i], 0.0)
-            stores.append((work, (i, PAD + k, pl.ds(row, SUB), slice(None)), value))
-        return stores
-
-    base, count = span(2)
-    make_shifts(base, count, [OWN - SUB // 2, OWN + SUB // 2], 2)
-    apply(base, count, [OWN - 2, OWN - 2 + SUB], 2, 1, emit_start)
-
-    def emit_middle(k, row, sums_of):
-        keep = inside(k, row)
-        stores = []
-        for i in range(3):
-            step = jnp.where(keep, fields[i, k, row : row + SUB, :] - sums_of[i], 0.0)
-            value = work[i, PAD + k, row : row + SUB, :] + step
-            stores.append((work, (i, PAD + k, pl.ds(row, SUB), slice(None)), value))
-            stores.append((second_x, (i, k, pl.ds(row, SUB), slice(None)), step))
-        return stores
-
-    base, count = span(1)
-    make_shifts(base, count, [OWN - 2, OWN - 2 + SUB], 1)
-    apply(base, count, [OWN - 1, OWN - 1 + SUB], 1, 2, emit_middle)
-    press_base, press_count = base, count
+                    work[f, k, row : row + SUB, :] = v * scale_at[k]
+
+    def emit_start(k, r, i, total_of):
+        at = slice(ROWS_START + r * SUB, ROWS_START + (r + 1) * SUB)
+        value = second_x[i, k, at, :] + (1.0 + carry + weight) * work[i, k, at, :]
+        value = jnp.where(inside(k, ROWS_START + r * SUB), value - weight * total_of, 0.0)
+        work[i, k, at, :] = value
+
+    wide, wide_count = span(2)
+    apply(0, tiles, wide, wide_count, coarse_ref, 0, 2, 2, emit_start)
+
+    def emit_middle(k, r, i, total_of):
+        at = slice(ROWS_MIDDLE + r * SUB, ROWS_MIDDLE + (r + 1) * SUB)
+        step = jnp.where(inside(k, ROWS_MIDDLE + r * SUB), fields[i, k, at, :] - total_of, 0.0)
+        work[i, k, at, :] = work[i, k, at, :] + step
+        second_x[i, k, at, :] = step
+
+    near_base, near_count = span(1)
+    apply(wide, wide_count, near_base, near_count, middle_ref, 0, 2, 1, emit_middle)
 
     base, count = span(0)
 
-    def emit_last(k, row, sums_of):
-        stores = []
-        for i in range(3):
-            value = work[i, PAD + k, row : row + SUB, :]
-            value = value + carry * second_x[i, k, row : row + SUB, :]
-            value = value + weight * (fields[i, k, row : row + SUB, :] - sums_of[i])
-            stores.append((out, (i, k - base), value))
-        return stores
-
-    make_shifts(base, count, [OWN - 1, OWN + 1], 1)
-    apply(base, count, [OWN], 1, count, emit_last)
+    def emit_last(k, r, i, total_of):
+        at = slice(OWN, OWN + SUB)
+        value = work[i, k, at, :] + carry * second_x[i, k, at, :]
+        out[i, k - base] = value + weight * (fields[i, k, at, :] - total_of)
+
+    apply(near_base, near_count, base, count, smooth_ref, OWN, 1, 1, emit_last)
+    press_base, press_count = near_base, near_count
 
     def beside(base, row):
         def load(k):
@@ -441,19 +459,15 @@
 
         return tile
 
-    news = []
-    for row in (OWN - 1, OWN - 1 + SUB):
+    starts = (OWN - 1, OWN + 1)
+    for r, row in enumerate(starts):
         near = beside(press_base, row)
         for k in range(press_count):
             v = fields[4, press_base + k, row : row + SUB, :] * (4.0 / 3.0) + near(k) * (1.0 / 9.0)
-            sums[0, k, row - OWN + 1 : row - OWN + 1 + SUB, :] = jnp.where(
-                inside(press_base + k, row), v, 0.0
-            )
-    for r, row in enumerate((OWN - 1, OWN - 1 + SUB)):
+            sums[r, k, :SUB, :] = jnp.where(inside(press_base + k, row), v, 0.0)
+    for r, row in enumerate(starts):
         for k in range(press_count):
-            press[PAD + press_base + k, row : row + SUB, :] = sums[
-                0, k, r * SUB : (r + 1) * SUB, :
-            ]
+            press[PAD + press_base + k, row : row + SUB, :] = sums[r, k, :SUB, :]
     near = beside(base, OWN)
     for k in range(count):
         v = press[PAD + base + k, OWN : OWN + SUB, :] * (1.0 / 3.0)
@@ -489,14 +503,16 @@
     tile = jax.ShapeDtypeStruct((FIELDS, SUB, LANES), jnp.float32)
     vmem = pl.BlockSpec(memory_space=pltpu.VMEM)
     smem = pl.BlockSpec(memory_space=pltpu.SMEM)
-    coef = pl.pallas_call(
-        coef_kernel,
-        out_shape=jax.ShapeDtypeStruct((stencil.size, LANES), jnp.float32),
+    bands = pl.pallas_call(
+        band_kernel,
+        out_shape=tuple(
+            jax.ShapeDtypeStruct((27, r * SUB, DEPTH), jnp.float32) for r in (3, 2, 2, 2)
+        ),
         in_specs=[smem],
-        out_specs=vmem,
+        out_specs=(vmem,) * 4,
         compiler_params=pltpu.CompilerParams(vmem_limit_bytes=SMALL_VMEM),
-        name="coef",
-    )(entries)
+        name="bands",
+    )(pltpu.with_memory_space_constraint(entries, pltpu.HBM))
     main, z_first, z_second = pl.pallas_call(
         functools.partial(pack_kernel, planes),
         out_shape=(
@@ -552,12 +568,13 @@
             jax.ShapeDtypeStruct(rhs_velocity.shape, f32),
             jax.ShapeDtypeStruct(rhs_pressure.shape, f32),
         ),
-        in_specs=[vmem] * 4,
+        in_specs=[vmem] * 7,
         out_specs=(vmem, vmem),
         scratch_shapes=[
             pltpu.VMEM((FIELDS, tiles, ROWS, LANES), f32),
-            pltpu.VMEM((3, tiles + 2 * PAD, ROWS, LANES), f32),
-            pltpu.VMEM((9, 3, tiles, ROWS, LANES), f32),
+            pltpu.VMEM((3, tiles, ROWS, LANES), f32),
+            pltpu.VMEM((DEPTH, tiles * LANES), f32),
+            pltpu.VMEM((tiles + 2 * PAD, 27 * ROWS, LANES), f32),
             pltpu.VMEM((3, tiles, ROWS, LANES), f32),
             pltpu.VMEM((3, tiles, 2 * SUB, LANES), f32),
             pltpu.VMEM((4, tiles, 2 * SUB, LANES), f32),
@@ -566,7 +583,7 @@
         ],
         compiler_params=pltpu.CompilerParams(vmem_limit_bytes=CYCLE_VMEM),
         name="cycle",
-    )(frame, y_first, y_second, coef)
+    )(frame, y_first, y_second, *bands)
 
 
 def solution(mesh):

time: 32.6 us -> 26.2 us (0.80)
  Pallas kernels: 13.3 us -> 7.48 us
  waiting for transfers between devices: 7.48 us -> 6.9 us
    pallas_call x1, Pallas kernels: 11.6 us -> 5.21 us  [on_device(): pl.pallas_call(functools.partial(cycle_kernel, planes, blocks, paired), o...]
    pallas_call x1, Pallas kernels: 0.71 us -> 1.3 us  [on_device(): pl.pallas_call(band_kernel, out_shape=tuple((jax.ShapeDtypeStruct((27, r...]
    ppermute x4, waiting for transfers between devices: 5.21 us -> 4.63 us  [matched(): return lax.ppermute(block, axis, pairs)]
  transfers between devices with their start and end apart: 5 -> 5, of which waited for: 3 -> 3; matrix products, arithmetic and copies ran while one was open for 0% -> 0% of each run, Pallas kernels for 2% -> 5%
where the time goes in v3:
time: 26.2 us; the launch traced here: 26 us
  starting transfers between devices  10.9 us (42%)
  Pallas kernels  7.48 us (29%)
  waiting for transfers between devices  6.9 us (26%)
  between operations  0.69 us (3%)
    ppermute x4, starting transfers between devices, matched(): return lax.ppermute(block, axis, pairs)  9.6 us
    pallas_call x1, Pallas kernels, on_device(): pl.pallas_call(functools.partial(cycle_kernel, planes, blocks, paired), o...  5.21 us
    ppermute x4, waiting for transfers between devices, matched(): return lax.ppermute(block, axis, pairs)  4.63 us
    ppermute x1, waiting for transfers between devices, on_device(): frame = jnp.stack([block, lax.ppermute(block, 'gx', [(0, 1), (1, 0)])])  2.27 us
    ppermute x1, starting transfers between devices, on_device(): frame = jnp.stack([block, lax.ppermute(block, 'gx', [(0, 1), (1, 0)])])  1.3 us
    pallas_call x1, Pallas kernels, on_device(): pl.pallas_call(band_kernel, out_shape=tuple((jax.ShapeDtypeStruct((27, r...  1.3 us
    pallas_call x1, Pallas kernels, on_device(): pl.pallas_call(functools.partial(pack_kernel, planes), out_shape=(jax.Sha...  0.96 us
  transfers between devices with their start and end apart: 5, of which 3 were waited for; matrix products, arithmetic and copies ran while one was open for 0% of the time, Pallas kernels for 5%

profile of v3, /device:TPU:17, one launch (start us, length us, event | category | flops | bytes accessed | tf_op | source)
XLA Modules:
  0.0 26.0 jit_solution(18380505637856934121)
XLA Ops:
  0.6 1.0 %pack.1 = (f32[20,8,128]{2,1,0:T(8,128)S(1)}, f32[5,8,128]{2,1,0:T(8,128)S(1)}, f32[5,8,128]{2,1,0:T(8,128)S(1)}) custom-call(f32[8]{0:T(128)} %visc_hbm.1, f32[3,3,27]{2,1,0:T(4,128)} %bitcast.5, f32[3,4,8,128]{3,2,1,0:T(8,128)} %rhs_hbm.1, f32[4,8,128]{2,1,0:T(8,128)} %press_hbm.1, s32[4,8,128]{2,1,0:T(8,128)} %ids_hbm.1), custom_call_target="tpu_custom_call" | custom-call | tf_op jit(solution)/shard_map/pack/pallas_call | solution.py:516
  1.6 1.4 %collective-permute-start = (f32[5,8,128]{2,1,0:T(8,128)S(1)}, f32[5,8,128]{2,1,0:T(8,128)S(1)}, u32[]{:S(2)}, u32[]{:S(2)}) collective-permute-start(f32[5,8,128]{2,1,0:T(8,128)S(1)} %get-tuple-element.10), channel_id=1, source_target_pairs={{0,1},{1,0},{2,3},{3,2},{4,5},{5,4},{6,7},{7,6},{8,9},{9,8},{10,11... | collective-permute-start | bytes 61448 | tf_op jit(solution)/shard_map/ppermute | solution.py:52
  3.0 1.9 %collective-permute-start.1 = (f32[5,8,128]{2,1,0:T(8,128)S(1)}, f32[5,8,128]{2,1,0:T(8,128)S(1)}, u32[]{:S(2)}, u32[]{:S(2)}) collective-permute-start(f32[5,8,128]{2,1,0:T(8,128)S(1)} %get-tuple-element.11), channel_id=1, source_target_pairs={{1,2},{2,1},{5,6},{6,5},{9,10},{10,9},{13,14},{14,13},{17,18},{18,... | collective-permute-start | bytes 61448 | tf_op jit(solution)/shard_map/ppermute | solution.py:52
  4.9 0.0 collective-permute-done
  4.9 2.6 %collective-permute-done.1 = f32[5,8,128]{2,1,0:T(8,128)S(1)} collective-permute-done((f32[5,8,128]{2,1,0:T(8,128)S(1)}, f32[5,8,128]{2,1,0:T(8,128)S(1)}, u32[]{:S(2)}, u32[]{:S(2)}) %collective-permute-start.1) | collective-permute-done | bytes 20512 | tf_op jit(solution)/shard_map/ppermute | solution.py:52
  7.5 1.3 %collective-permute-start.2 = (f32[25,8,128]{2,1,0:T(8,128)S(1)}, f32[25,8,128]{2,1,0:T(8,128)S(1)}, u32[]{:S(2)}, u32[]{:S(2)}) collective-permute-start(f32[25,8,128]{2,1,0:T(8,128)S(1)} %get-tuple-element.17), channel_id=1, source_target_pairs={{0,16},{16,0},{1,17},{17,1},{2,18},{18,2},{3,19},{19,3},{4,20},{20... | collective-permute-start | bytes 307208 | tf_op jit(solution)/shard_map/ppermute | solution.py:548
  8.8 2.3 %collective-permute-done.2 = f32[25,8,128]{2,1,0:T(8,128)S(1)} collective-permute-done((f32[25,8,128]{2,1,0:T(8,128)S(1)}, f32[25,8,128]{2,1,0:T(8,128)S(1)}, u32[]{:S(2)}, u32[]{:S(2)}) %collective-permute-start.2) | collective-permute-done | bytes 102432 | tf_op jit(solution)/shard_map/ppermute | solution.py:548
  11.1 6.3 %collective-permute-start.4 = (f32[2,25,8,128]{3,2,1,0:T(8,128)S(1)}, f32[2,25,8,128]{3,2,1,0:T(8,128)S(1)}, u32[]{:S(2)}, u32[]{:S(2)}) collective-permute-start(f32[2,25,8,128]{3,2,1,0:T(8,128)S(1)} %pad_maximum_fusion.own_ref), channel_id=1, source_target_pairs={{4,8},{8,4},{5,9},{9,5},{6,10},{10,6},{7,11},{11,7},{20,24},{24,20... | collective-permute-start | bytes 614408 | tf_op jit(solution)/shard_map/ppermute | solution.py:52
  17.4 0.1 collective-permute-start.3
  17.4 1.3 %bands.1 = (f32[27,24,256]{2,1,0:T(8,128)S(1)}, f32[27,16,256]{2,1,0:T(8,128)S(1)}, f32[27,16,256]{2,1,0:T(8,128)S(1)}, f32[27,16,256]{2,1,0:T(8,128)S(1)}) custom-call(f32[3,3,27]{2,1,0:T(4,128)} %bitcast.6), custom_call_target="tpu_custom_call" | custom-call | tf_op jit(solution)/shard_map/bands/pallas_call | solution.py:506
  18.8 2.0 %collective-permute-done.4.b_ref = f32[2,25,8,128]{3,2,1,0:T(8,128)S(1)} collective-permute-done((f32[2,25,8,128]{3,2,1,0:T(8,128)S(1)}, f32[2,25,8,128]{3,2,1,0:T(8,128)S(1)}, u32[]{:S(2)}, u32[]{:S(2)}) %collective-permute-start.4) | collective-permute-done | bytes 204832 | tf_op jit(solution)/shard_map/ppermute | solution.py:52
  20.8 0.0 collective-permute-done.3.a_ref
  20.8 5.2 %cycle.1 = (f32[3,4,8,128]{3,2,1,0:T(8,128)}, f32[4,8,128]{2,1,0:T(8,128)}) custom-call(f32[2,25,8,128]{3,2,1,0:T(8,128)S(1)} %pad_maximum_fusion.own_ref, f32[2,25,8,128]{3,2,1,0:T(8,128)S(1)} %collective-permute-done.3.a_ref, f32[2,25,8,128]{3,2,1,0:T(8,128)S(1)} %collective-permute-done.4.b_ref, f32[27,24,256]{2,1,0:T(8,128)S(1)} %get-tuple-element.12.smooth_ref, ...), custom_call_target="tpu_custom_call" | custom-call | tf_op jit(solution)/shard_map/cycle/pallas_call | solution.py:565
  (3 shorter events, 0.0 us)
Async XLA Ops:
  1.6 3.3 %collective-permute-start = (f32[5,8,128]{2,1,0:T(8,128)S(1)}, f32[5,8,128]{2,1,0:T(8,128)S(1)}, u32[]{:S(2)}, u32[]{:S(2)}) collective-permute-start(f32[5,8,128]{2,1,0:T(8,128)S(1)} %get-tuple-element.10), channel_id=1, source_target_pairs={{0,1},{1,0},{2,3},{3,2},{4,5},{5,4},{6,7},{7,6},{8,9},{9,8},{10,11... | collective-permute-start | bytes 61448 | tf_op jit(solution)/shard_map/ppermute | solution.py:52
  3.0 4.5 %collective-permute-start.1 = (f32[5,8,128]{2,1,0:T(8,128)S(1)}, f32[5,8,128]{2,1,0:T(8,128)S(1)}, u32[]{:S(2)}, u32[]{:S(2)}) collective-permute-start(f32[5,8,128]{2,1,0:T(8,128)S(1)} %get-tuple-element.11), channel_id=1, source_target_pairs={{1,2},{2,1},{5,6},{6,5},{9,10},{10,9},{13,14},{14,13},{17,18},{18,... | collective-permute-start | bytes 61448 | tf_op jit(solution)/shard_map/ppermute | solution.py:52
  7.5 3.6 %collective-permute-start.2 = (f32[25,8,128]{2,1,0:T(8,128)S(1)}, f32[25,8,128]{2,1,0:T(8,128)S(1)}, u32[]{:S(2)}, u32[]{:S(2)}) collective-permute-start(f32[25,8,128]{2,1,0:T(8,128)S(1)} %get-tuple-element.17), channel_id=1, source_target_pairs={{0,16},{16,0},{1,17},{17,1},{2,18},{18,2},{3,19},{19,3},{4,20},{20... | collective-permute-start | bytes 307208 | tf_op jit(solution)/shard_map/ppermute | solution.py:548
  11.1 9.7 %collective-permute-start.4 = (f32[2,25,8,128]{3,2,1,0:T(8,128)S(1)}, f32[2,25,8,128]{3,2,1,0:T(8,128)S(1)}, u32[]{:S(2)}, u32[]{:S(2)}) collective-permute-start(f32[2,25,8,128]{3,2,1,0:T(8,128)S(1)} %pad_maximum_fusion.own_ref), channel_id=1, source_target_pairs={{4,8},{8,4},{5,9},{9,5},{6,10},{10,6},{7,11},{11,7},{20,24},{24,20... | collective-permute-start | bytes 614408 | tf_op jit(solution)/shard_map/ppermute | solution.py:52
  17.4 3.4 %collective-permute-start.3 = (f32[2,25,8,128]{3,2,1,0:T(8,128)S(1)}, f32[2,25,8,128]{3,2,1,0:T(8,128)S(1)}, u32[]{:S(2)}, u32[]{:S(2)}) collective-permute-start(f32[2,25,8,128]{3,2,1,0:T(8,128)S(1)} %pad_maximum_fusion.own_ref), channel_id=1, source_target_pairs={{0,4},{4,0},{8,12},{12,8},{1,5},{5,1},{9,13},{13,9},{2,6},{6,2},{1... | collective-permute-start | bytes 614408 | tf_op jit(solution)/shard_map/ppermute | solution.py:52

commit v4 on v3

v4 whole, which is shorter than its diff:
```python
import functools

import jax
import jax.numpy as jnp
from jax import lax
from jax.experimental import pallas as pl
from jax.experimental.pallas import tpu as pltpu
from jax.sharding import PartitionSpec as P

LOW_BOUND = 0.2
HIGH_BOUND = 1.8

SUB = 8
LANES = 128
COLS = 8
REACH = 6
FIELDS = 5
LEAD = 2
STRIP = 4 * COLS
ROWS = 3 * SUB
OWN = SUB
ROWS_RESID = OWN - 4
ROWS_START = OWN - 2
ROWS_MIDDLE = OWN - 1
DEPTH = 2 * LANES
PIECE = 9 * SUB * 3
SMALL_VMEM = 4 * 1024 * 1024
CYCLE_VMEM = 32 * 1024 * 1024


def cheb_consts():
    theta = (HIGH_BOUND + LOW_BOUND) / 2.0
    delta = (HIGH_BOUND - LOW_BOUND) / 2.0
    sigma = theta / delta
    rho_zero = 1.0 / sigma
    rho_one = 1.0 / (2.0 * sigma - rho_zero)
    return (theta, delta, rho_zero, rho_one)


def first_pairs(count):
    return [(i, i ^ 1) for i in range(count) if i ^ 1 < count]


def second_pairs(count):
    pairs = []
    for i in range(1, count - 1, 2):
        pairs += [(i, i + 1), (i + 1, i)]
    return pairs


def matched(block, axis, pairs):
    if not pairs:
        return jnp.zeros_like(block)
    return lax.ppermute(block, axis, pairs)


def lane_iota():
    return lax.broadcasted_iota(jnp.int32, (SUB, LANES), 1)


def diagonal_mean(stencil_ref):
    middle = stencil_ref.shape[2] // 2
    return (stencil_ref[0, 0, middle] + stencil_ref[1, 1, middle] + stencil_ref[2, 2, middle]) / 3.0


def band_kernel(stencil_ref, smooth_ref, resid_ref, coarse_ref, middle_ref):
    scale = 1.0 / jnp.full((SUB, LANES), diagonal_mean(stencil_ref), jnp.float32)
    sub = lax.broadcasted_iota(jnp.int32, (SUB, LANES), 0)
    lane = lane_iota()
    zero = jnp.zeros((SUB, LANES), jnp.float32)
    halves = []
    for half in range(DEPTH // LANES):
        spot = lane + half * LANES
        groups = range(half * LANES // ROWS, min(((half + 1) * LANES - 1) // ROWS, 8) + 1)
        start = jnp.full((SUB, LANES), groups[0] * ROWS, jnp.int32)
        for n in groups[1:]:
            start = jnp.where(spot >= n * ROWS, n * ROWS, start)
        reach = jnp.where(spot < 9 * ROWS, spot - start - sub, 1000)
        halves.append((reach, [(n, start == n * ROWS) for n in groups]))
    for c in range(3):
        for i in range(3):
            rows_of = []
            for b in range(3):
                row = []
                for reach, groups in halves:
                    full = zero
                    for n, here in groups:
                        a, j = divmod(n, 3)
                        full = jnp.where(here, stencil_ref[i, j, 9 * a + 3 * b + c], full)
                    full = scale * full
                    high = full.astype(jnp.bfloat16).astype(jnp.float32)
                    row.append((high, full - high))
                rows_of.append(row)
            for ref, start, step in (
                (smooth_ref, 0, 1),
                (resid_ref, ROWS_RESID, 1),
                (coarse_ref, ROWS_START, 2),
                (middle_ref, ROWS_MIDDLE, 1),
            ):
                for r in range(ref.shape[1] // SUB):
                    for half, (reach, _) in enumerate(halves):
                        high, low = zero, zero
                        for b in range(3):
                            here = reach == r * SUB + start + step * (b - 1)
                            high = jnp.where(here, rows_of[b][half][0], high)
                            low = jnp.where(here, rows_of[b][half][1], low)
                        for term, value in enumerate((high, low, high)):
                            at = (2 * term + half) * LANES
                            ref[c * 3 + i, r * SUB : (r + 1) * SUB, at : at + LANES] = value


def pack_kernel(
    planes,
    visc_hbm,
    stencil_hbm,
    rhs_hbm,
    press_hbm,
    ids_hbm,
    main_ref,
    a_ref,
    b_ref,
    visc_ref,
    stencil_ref,
    rhs_ref,
    press_ref,
    ids_ref,
    arrived,
):
    copies = [
        pltpu.make_async_copy(src, dst, arrived.at[n])
        for n, (src, dst) in enumerate(
            (
                (visc_hbm, visc_ref),
                (stencil_hbm, stencil_ref),
                (ids_hbm, ids_ref),
                (rhs_hbm, rhs_ref),
                (press_hbm, press_ref),
            )
        )
    ]
    for copy in copies:
        copy.start()
    for copy in copies:
        copy.wait()
    lane = lane_iota()
    odd = lax.axis_index("gz") % 2 == 1
    kc = jnp.full((SUB, LANES), diagonal_mean(stencil_ref), jnp.float32)
    zero = jnp.zeros((SUB, LANES), jnp.float32)
    up, down, own = [zero] * FIELDS, [zero] * FIELDS, [zero] * FIELDS
    for p in range(planes):
        ids = ids_ref[p]
        eta = jnp.zeros((SUB, LANES), jnp.float32)
        for layer in range(visc_ref.shape[0]):
            eta = jnp.where(ids == layer, visc_ref[layer], eta)
        dinv = 1.0 / (eta * kc)
        values = [rhs_ref[j, p] * dinv for j in range(3)]
        values += [eta, eta * press_ref[p] * (1.0 / 9.0)]
        quarter = lane // COLS - p * (STRIP // COLS)
        for f in range(FIELDS):
            main_ref[f * planes + p] = values[f]
            near = pltpu.roll(values[f], (p * STRIP + COLS) % LANES, 1)
            far = pltpu.roll(values[f], (p * STRIP + 3 * COLS) % LANES, 1)
            up[f] = jnp.where(quarter == 0, near, up[f])
            own[f] = jnp.where(quarter == 1, near, jnp.where(quarter == 2, far, own[f]))
            down[f] = jnp.where(quarter == 3, far, down[f])
    for f in range(FIELDS):
        main_ref[FIELDS * planes + f] = own[f]
        a_ref[f] = jnp.where(odd, down[f], up[f])
        b_ref[f] = jnp.where(odd, up[f], down[f])


def cycle_kernel(
    planes,
    blocks,
    paired,
    own_ref,
    a_ref,
    b_ref,
    smooth_ref,
    resid_band,
    coarse_ref,
    middle_ref,
    vel_ref,
    press_ref,
    fields,
    work,
    split,
    products,
    edge,
    second_x,
    resid,
    press,
):
    theta, delta, rho_zero, rho_one = cheb_consts()
    weight = 2.0 * rho_one / delta
    carry = rho_one * rho_zero
    total = planes * blocks
    strips = total + 2 * LEAD
    lane = lane_iota()
    zero = jnp.zeros((SUB, LANES), jnp.float32)
    gx = lax.axis_index("gx")
    y_odd = lax.axis_index("gy") % 2 == 1

    def span(grow):
        if paired:
            low = (0, min(planes - 1 + grow, total - 1))
            high = max(planes - grow, 0)
            return gx * high, low[1] + 1
        own = blocks // 2
        lo = max(own * planes - grow, 0)
        return lo, min((own + 1) * planes + grow, total) - lo

    def place(plane):
        if isinstance(plane, int):
            return plane // planes, plane % planes
        block = lax.div(plane, planes)
        return block, plane - block * planes

    def slot(q):
        return (q + gx) % 2 if paired else q

    for k in [*range(LEAD), *range(LEAD + total, strips)]:
        for r in range(3):
            for j in range(3):
                work[j, k, r * SUB : (r + 1) * SUB, :] = zero
            press[k, r * SUB : (r + 1) * SUB, :] = zero

    def assemble(src, row):
        at = slice(row, row + SUB)
        for q in range(blocks):
            here = slot(q)
            for f in range(FIELDS):
                for p in range(planes + 1):
                    strip = p == planes
                    index = FIELDS * planes + f if strip else f * planes + p
                    value = src[here, index]
                    fields[f, total + q if strip else q * planes + p, at, :] = value
                    spot = strips + q if strip else LEAD + q * planes + p
                    if f < 3:
                        work[f, spot, at, :] = value
                    if f == 4:
                        press[spot, at, :] = value

    assemble(own_ref, OWN)

    @pl.when(y_odd)
    def _():
        assemble(a_ref, OWN - SUB)
        assemble(b_ref, OWN + SUB)

    @pl.when(jnp.logical_not(y_odd))
    def _():
        assemble(b_ref, OWN - SUB)
        assemble(a_ref, OWN + SUB)

    def strip_shift(tiles_of, offset):
        turn = (LANES - offset * STRIP) % LANES
        turned = [pltpu.roll(v, turn, 1) for v in tiles_of] + [zero]
        shifted = []
        for q in range(blocks):
            if offset > 0:
                shifted.append(jnp.where(lane < LANES - offset * STRIP, turned[q], turned[q + 1]))
            else:
                shifted.append(jnp.where(lane >= -offset * STRIP, turned[q], turned[q - 1]))
        return shifted

    def edge_source(ahead, behind, scale):
        moved = pltpu.roll(behind, 2 * COLS + 2 * scale, 1)
        far = lane % STRIP
        return jnp.where((far >= 3 * COLS + scale) & (far < 3 * COLS + 2 * scale), moved, ahead)

    def edge_turn(p, scale):
        return LANES - 3 * COLS - scale - STRIP * p

    def z_shifts(ahead, behind, source, p, scale):
        outer = pltpu.roll(source, edge_turn(p, scale), 1)
        ahead = pltpu.roll(ahead, LANES - scale, 1)
        behind = pltpu.roll(behind, scale, 1)
        return jnp.where(lane >= LANES - scale, outer, ahead) + jnp.where(
            lane < scale, outer, behind
        )

    def parts_of(v):
        high = v.astype(jnp.bfloat16).astype(jnp.float32)
        return high, v - high

    blank = jnp.zeros((DEPTH - PIECE, 2 * LANES), jnp.float32)

    def product(band, high, low):
        width = high.shape[1]
        return jnp.dot(
            band,
            jnp.concatenate(
                [high, blank[:, :width], high, blank[:, :width], low, blank[:, :width]]
            ),
            preferred_element_type=jnp.float32,
            precision=lax.Precision.DEFAULT,
        )

    def apply(base, count, band_ref, first, rows, scale, emit, with_strips=True):
        height = rows * SUB
        half = -(-count // 2)
        band = band_ref[:, first : first + height, :].reshape(9 * height, 3 * DEPTH)
        for n in range(half + 2 * scale):
            for side in range(2):
                for j in range(3):
                    for r in range(3):
                        spot = LEAD + base - scale + side * half + n
                        high, low = parts_of(work[j, spot, r * SUB : (r + 1) * SUB, :])
                        at = ((n * 3 + j) * 3 + r) * SUB
                        lanes = slice(side * LANES, (side + 1) * LANES)
                        split[0, at : at + SUB, lanes] = high
                        split[1, at : at + SUB, lanes] = low
        size = 9 * SUB
        for q in range(0, blocks, 2):
            width = min(2, blocks - q)
            pieces = []
            for a in range(3):
                for j in range(3):
                    for r in range(3):
                        tiles_of = [
                            work[j, strips + p, r * SUB : (r + 1) * SUB, :] for p in range(blocks)
                        ]
                        if a != 1:
                            tiles_of = strip_shift(tiles_of, (a - 1) * scale)
                        pieces.append([parts_of(v) for v in tiles_of[q : q + width]])
            high, low = (
                jnp.concatenate(
                    [jnp.concatenate([v[n] for v in piece], axis=1) for piece in pieces]
                )
                for n in range(2)
            )
            made = product(band, high, low)
            for w in range(width):
                products[total + 2 + q + w, : 9 * height, :] = made[:, w * LANES : (w + 1) * LANES]
        for n in range(half):
            high, low = (
                jnp.concatenate(
                    [
                        split[part, (n + a * scale) * size : (n + a * scale + 1) * size, :]
                        for a in range(3)
                    ]
                )
                for part in range(2)
            )
            made = product(band, high, low)
            for side in range(2):
                products[n + side * half, : 9 * height, :] = made[
                    :, side * LANES : (side + 1) * LANES
                ]

        def of(k, c, i, r):
            at = (c * 3 + i) * height + r * SUB
            return products[k, at : at + SUB, :]

        for i in range(3):
            for r in range(rows):
                for q in range(blocks):
                    behind, middle, ahead = (of(total + 2 + q, c, i, r) for c in range(3))
                    at = (i * 3 + r) * SUB
                    edge[q, at : at + SUB, :] = edge_source(ahead, behind, scale)
                    if with_strips:
                        middle = middle + pltpu.roll(ahead, LANES - scale, 1)
                        middle = middle + pltpu.roll(behind, scale, 1)
                        emit(total + q, strips + q, None, r, i, middle)
        for i in range(3):
            for r in range(rows):
                for k in range(count):
                    q, p = place(base + k)
                    behind, middle, ahead = (of(k, c, i, r) for c in range(3))
                    at = (i * 3 + r) * SUB
                    sides = z_shifts(ahead, behind, edge[q, at : at + SUB, :], p, scale)
                    emit(base + k, LEAD + base + k, k, r, i, middle + sides)

    def inside(t, row):
        return fields[3, t, row : row + SUB, :] > 0.0

    def emit_first(t, w, k, r, i, total_of):
        at = slice(r * SUB, (r + 1) * SUB)
        value = (1.0 + carry + weight) * fields[i, t, at, :] - weight * total_of
        value = jnp.where(inside(t, r * SUB), value, 0.0)
        work[i, w, at, :] = value
        second_x[i, t, at, :] = value

    apply(0, total, smooth_ref, 0, 3, 1, emit_first)

    lane_even = lane % 2 == 0
    row_even = lax.broadcasted_iota(jnp.int32, (SUB, LANES), 0) % 2 == 0

    def pair_sums(v):
        v = v + jnp.where(row_even, pltpu.roll(v, SUB - 1, 0), pltpu.roll(v, 1, 0))
        return v + jnp.where(lane_even, pltpu.roll(v, LANES - 1, 1), pltpu.roll(v, 1, 1))

    def emit_resid(t, w, k, r, i, total_of):
        at = slice(ROWS_RESID + r * SUB, ROWS_RESID + (r + 1) * SUB)
        value = fields[3, t, at, :] * (fields[i, t, at, :] - total_of)
        resid[i, t, r * SUB : (r + 1) * SUB, :] = pair_sums(value)

    apply(0, total, resid_band, 0, 2, 1, emit_resid)

    plane_even = lane // STRIP % 2 == 0
    for r in range(2):
        at = slice(ROWS_RESID + r * SUB, ROWS_RESID + (r + 1) * SUB)
        rows_at = slice(r * SUB, (r + 1) * SUB)
        for t in [*range(0, total, 2), *range(total, total + blocks)]:
            weigh = None
            for f in (3, 0, 1, 2):
                def load(k):
                    if f == 3:
                        return pair_sums(fields[3, k, at, :])
                    return resid[f, k, rows_at, :]

                v = load(t)
                if t < total:
                    v = v + load(t + 1)
                else:
                    ahead = pltpu.roll(v, LANES - STRIP, 1)
                    v = v + jnp.where(plane_even, ahead, pltpu.roll(v, STRIP, 1))
                if f == 3:
                    weigh = jnp.where(v > 0.0, 4.0 / v, 0.0)
                elif t < total:
                    work[f, LEAD + t, at, :] = v * weigh
                    work[f, LEAD + t + 1, at, :] = v * weigh
                else:
                    work[f, strips + t - total, at, :] = v * weigh

    def emit_start(t, w, k, r, i, total_of):
        at = slice(ROWS_START + r * SUB, ROWS_START + (r + 1) * SUB)
        value = second_x[i, t, at, :] + (1.0 + carry + weight) * work[i, w, at, :]
        value = jnp.where(inside(t, ROWS_START + r * SUB), value - weight * total_of, 0.0)
        work[i, w, at, :] = value

    apply(*span(2), coarse_ref, 0, 2, 2, emit_start)

    def emit_middle(t, w, k, r, i, total_of):
        at = slice(ROWS_MIDDLE + r * SUB, ROWS_MIDDLE + (r + 1) * SUB)
        step = jnp.where(inside(t, ROWS_MIDDLE + r * SUB), fields[i, t, at, :] - total_of, 0.0)
        work[i, w, at, :] = work[i, w, at, :] + step
        second_x[i, t, at, :] = step

    apply(*span(1), middle_ref, 0, 2, 1, emit_middle)

    own = slice(OWN, OWN + SUB)

    def emit_last(t, w, k, r, i, total_of):
        value = work[i, w, own, :] + carry * second_x[i, t, own, :]
        vel_ref[i, k] = value + weight * (fields[i, t, own, :] - total_of)

    apply(*span(0), smooth_ref, OWN, 1, 1, emit_last, with_strips=False)

    def strip_sides(row):
        return [press[strips + q, row : row + SUB, :] for q in range(blocks)]

    def beside(k, row, at):
        v = press[LEAD + k, row - 1 : row - 1 + SUB, :]
        v = v + press[LEAD + k, row + 1 : row + 1 + SUB, :]
        v = v + press[LEAD + k - 1, row : row + SUB, :] + press[LEAD + k + 1, row : row + SUB, :]
        q, p = place(k)
        here = press[LEAD + k, row : row + SUB, :]
        return v + z_shifts(here, here, edge[q, at : at + SUB, :], p, 1)

    def set_edges(row, at):
        for q in range(blocks):
            v = press[strips + q, row : row + SUB, :]
            edge[q, at : at + SUB, :] = edge_source(v, v, 1)

    starts = (OWN - 1, OWN + 1)
    base, count = span(1)
    news = []
    for n, row in enumerate(starts):
        set_edges(row, n * SUB)
        tiles_of = strip_sides(row)
        far = strip_shift(tiles_of, 1), strip_shift(tiles_of, -1)
        for q in range(blocks):
            v = press[strips + q, row - 1 : row - 1 + SUB, :]
            v = v + press[strips + q, row + 1 : row + 1 + SUB, :] + far[0][q] + far[1][q]
            v = v + pltpu.roll(tiles_of[q], LANES - 1, 1) + pltpu.roll(tiles_of[q], 1, 1)
            news.append((total + q, strips + q, row, v))
        for k in range(count):
            news.append((base + k, LEAD + base + k, row, beside(base + k, row, n * SUB)))
    for n, (t, w, row, near) in enumerate(news):
        v = fields[4, t, row : row + SUB, :] * (4.0 / 3.0) + near * (1.0 / 9.0)
        resid[0, n, :SUB, :] = jnp.where(inside(t, row), v, 0.0)
    for n, (t, w, row, near) in enumerate(news):
        press[w, row : row + SUB, :] = resid[0, n, :SUB, :]
    base, count = span(0)
    set_edges(OWN, 0)
    for k in range(count):
        v = press[LEAD + base + k, own, :] * (1.0 / 3.0) + fields[4, base + k, own, :]
        press_ref[k] = v + beside(base + k, OWN, 0) * (1.0 / 9.0)


def on_device(rhs_velocity, rhs_pressure, layer_ids, visc_table, stencil):
    planes, rows, depth = rhs_pressure.shape
    assert rows == SUB and depth == LANES and planes * STRIP == LANES
    x_count, y_count, z_count = (lax.axis_size(n) for n in ("gx", "gy", "gz"))
    entries = jnp.transpose(stencil, (1, 2, 0))

    tile = jax.ShapeDtypeStruct((FIELDS, SUB, LANES), jnp.float32)
    vmem = pl.BlockSpec(memory_space=pltpu.VMEM)
    smem = pl.BlockSpec(memory_space=pltpu.SMEM)
    bands = pl.pallas_call(
        band_kernel,
        out_shape=tuple(
            jax.ShapeDtypeStruct((9, r * SUB, 3 * DEPTH), jnp.float32) for r in (3, 2, 2, 2)
        ),
        in_specs=[smem],
        out_specs=(vmem,) * 4,
        compiler_params=pltpu.CompilerParams(vmem_limit_bytes=SMALL_VMEM),
        name="bands",
    )(pltpu.with_memory_space_constraint(entries, pltpu.HBM))
    main, z_first, z_second = pl.pallas_call(
        functools.partial(pack_kernel, planes),
        out_shape=(
            jax.ShapeDtypeStruct((FIELDS * (planes + 1), SUB, LANES), jnp.float32),
            tile,
            tile,
        ),
        in_specs=[pl.BlockSpec(memory_space=pltpu.HBM)] * 5,
        out_specs=(vmem, vmem, vmem),
        scratch_shapes=[
            pltpu.SMEM(visc_table.shape, visc_table.dtype),
            pltpu.SMEM(entries.shape, entries.dtype),
            pltpu.VMEM(rhs_velocity.shape, rhs_velocity.dtype),
            pltpu.VMEM(rhs_pressure.shape, rhs_pressure.dtype),
            pltpu.VMEM(layer_ids.shape, layer_ids.dtype),
            pltpu.SemaphoreType.DMA((5,)),
        ],
        compiler_params=pltpu.CompilerParams(vmem_limit_bytes=SMALL_VMEM),
        name="pack",
    )(
        *(
            pltpu.with_memory_space_constraint(v, pltpu.HBM)
            for v in (visc_table, entries, rhs_velocity, rhs_pressure, layer_ids)
        )
    )

    halo = matched(z_first, "gz", first_pairs(z_count))
    halo = halo + matched(z_second, "gz", second_pairs(z_count))
    inner = FIELDS * planes
    block = jnp.concatenate([main[:inner], main[inner:] + halo])

    paired = x_count == 2
    if paired:
        frame = jnp.stack([block, lax.ppermute(block, "gx", [(0, 1), (1, 0)])])
        blocks = 2
    else:
        hops = -(-REACH // planes)
        parts = []
        for hop in range(-hops, hops + 1):
            pairs = [(i, i - hop) for i in range(x_count) if 0 <= i - hop < x_count]
            parts.append(block if hop == 0 else matched(block, "gx", pairs))
        frame = jnp.stack(parts)
        blocks = 2 * hops + 1

    y_first = matched(frame, "gy", first_pairs(y_count))
    y_second = matched(frame, "gy", second_pairs(y_count))

    total = planes * blocks
    tiles = total + blocks
    f32 = jnp.float32
    return pl.pallas_call(
        functools.partial(cycle_kernel, planes, blocks, paired),
        out_shape=(
            jax.ShapeDtypeStruct(rhs_velocity.shape, f32),
            jax.ShapeDtypeStruct(rhs_pressure.shape, f32),
        ),
        in_specs=[vmem] * 7,
        out_specs=(vmem, vmem),
        scratch_shapes=[
            pltpu.VMEM((FIELDS, tiles, ROWS, LANES), f32),
            pltpu.VMEM((3, tiles + 2 * LEAD, ROWS, LANES), f32),
            pltpu.VMEM((2, (total // 2 + 2 * LEAD) * 9 * SUB, 2 * LANES), f32),
            pltpu.VMEM((tiles + 2, 9 * ROWS, LANES), f32),
            pltpu.VMEM((blocks, 3 * ROWS, LANES), f32),
            pltpu.VMEM((3, tiles, ROWS, LANES), f32),
            pltpu.VMEM((3, 2 * tiles, 2 * SUB, LANES), f32),
            pltpu.VMEM((tiles + 2 * LEAD, ROWS, LANES), f32),
        ],
        compiler_params=pltpu.CompilerParams(vmem_limit_bytes=CYCLE_VMEM),
        name="cycle",
    )(frame, y_first, y_second, *bands)


def solution(mesh):
    placed = (P(None, "gx", "gy", "gz"), P("gx", "gy", "gz"), P("gx", "gy", "gz"), P(), P())
    return jax.shard_map(
        on_device,
        mesh=mesh,
        in_specs=placed,
        out_specs=(P(None, "gx", "gy", "gz"), P("gx", "gy", "gz")),
        check_vma=False,
    )
```

time: 26.2 us -> 25 us (0.954)
  Pallas kernels: 7.48 us -> 5.94 us
    pallas_call x1, Pallas kernels: 5.21 us -> 3.89 us  [on_device(): pl.pallas_call(functools.partial(cycle_kernel, planes, blocks, paired), o...]
  transfers between devices with their start and end apart: 5 -> 5, of which waited for: 3 -> 3; matrix products, arithmetic and copies ran while one was open for 0% -> 0% of each run, Pallas kernels for 5% -> 4%
where the time goes in v4:
time: 25 us; the launch traced here: 24.7 us
  starting transfers between devices  10.9 us (44%)
  waiting for transfers between devices  7.13 us (29%)
  Pallas kernels  5.94 us (24%)
  between operations  0.69 us (3%)
    ppermute x4, starting transfers between devices, matched(): return lax.ppermute(block, axis, pairs)  9.59 us
    ppermute x4, waiting for transfers between devices, matched(): return lax.ppermute(block, axis, pairs)  4.86 us
    pallas_call x1, Pallas kernels, on_device(): pl.pallas_call(functools.partial(cycle_kernel, planes, blocks, paired), o...  3.89 us
    ppermute x1, waiting for transfers between devices, on_device(): frame = jnp.stack([block, lax.ppermute(block, 'gx', [(0, 1), (1, 0)])])  2.27 us
    ppermute x1, starting transfers between devices, on_device(): frame = jnp.stack([block, lax.ppermute(block, 'gx', [(0, 1), (1, 0)])])  1.3 us
    pallas_call x1, Pallas kernels, on_device(): pl.pallas_call(band_kernel, out_shape=tuple((jax.ShapeDtypeStruct((9, r *...  1.06 us
    pallas_call x1, Pallas kernels, on_device(): pl.pallas_call(functools.partial(pack_kernel, planes), out_shape=(jax.Sha...  0.99 us
  transfers between devices with their start and end apart: 5, of which 3 were waited for; matrix products, arithmetic and copies ran while one was open for 0% of the time, Pallas kernels for 4%

profile of v4, /device:TPU:17, one launch (start us, length us, event | category | flops | bytes accessed | tf_op | source)
XLA Modules:
  0.0 24.7 jit_solution(3459926028878936338)
XLA Ops:
  0.6 1.0 %pack.1 = (f32[25,8,128]{2,1,0:T(8,128)S(1)}, f32[5,8,128]{2,1,0:T(8,128)S(1)}, f32[5,8,128]{2,1,0:T(8,128)S(1)}) custom-call(f32[8]{0:T(128)} %visc_hbm.1, f32[3,3,27]{2,1,0:T(4,128)} %bitcast.5, f32[3,4,8,128]{3,2,1,0:T(8,128)} %rhs_hbm.1, f32[4,8,128]{2,1,0:T(8,128)} %press_hbm.1, s32[4,8,128]{2,1,0:T(8,128)} %ids_hbm.1), custom_call_target="tpu_custom_call" | custom-call | tf_op jit(solution)/shard_map/pack/pallas_call | solution.py:512
  1.6 1.4 %collective-permute-start = (f32[5,8,128]{2,1,0:T(8,128)S(1)}, f32[5,8,128]{2,1,0:T(8,128)S(1)}, u32[]{:S(2)}, u32[]{:S(2)}) collective-permute-start(f32[5,8,128]{2,1,0:T(8,128)S(1)} %get-tuple-element.10), channel_id=1, source_target_pairs={{0,1},{1,0},{2,3},{3,2},{4,5},{5,4},{6,7},{7,6},{8,9},{9,8},{10,11... | collective-permute-start | bytes 61448 | tf_op jit(solution)/shard_map/ppermute | solution.py:54
  3.0 1.9 %collective-permute-start.1 = (f32[5,8,128]{2,1,0:T(8,128)S(1)}, f32[5,8,128]{2,1,0:T(8,128)S(1)}, u32[]{:S(2)}, u32[]{:S(2)}) collective-permute-start(f32[5,8,128]{2,1,0:T(8,128)S(1)} %get-tuple-element.11), channel_id=1, source_target_pairs={{1,2},{2,1},{5,6},{6,5},{9,10},{10,9},{13,14},{14,13},{17,18},{18,... | collective-permute-start | bytes 61448 | tf_op jit(solution)/shard_map/ppermute | solution.py:54
  4.9 0.0 collective-permute-done
  4.9 2.6 %collective-permute-done.1 = f32[5,8,128]{2,1,0:T(8,128)S(1)} collective-permute-done((f32[5,8,128]{2,1,0:T(8,128)S(1)}, f32[5,8,128]{2,1,0:T(8,128)S(1)}, u32[]{:S(2)}, u32[]{:S(2)}) %collective-permute-start.1) | collective-permute-done | bytes 20512 | tf_op jit(solution)/shard_map/ppermute | solution.py:54
  7.5 1.3 %collective-permute-start.2 = (f32[25,8,128]{2,1,0:T(8,128)S(1)}, f32[25,8,128]{2,1,0:T(8,128)S(1)}, u32[]{:S(2)}, u32[]{:S(2)}) collective-permute-start(f32[25,8,128]{2,1,0:T(8,128)S(1)} %get-tuple-element.17), channel_id=1, source_target_pairs={{0,16},{16,0},{1,17},{17,1},{2,18},{18,2},{3,19},{19,3},{4,20},{20... | collective-permute-start | bytes 307208 | tf_op jit(solution)/shard_map/ppermute | solution.py:545
  8.8 2.3 %collective-permute-done.2 = f32[25,8,128]{2,1,0:T(8,128)S(1)} collective-permute-done((f32[25,8,128]{2,1,0:T(8,128)S(1)}, f32[25,8,128]{2,1,0:T(8,128)S(1)}, u32[]{:S(2)}, u32[]{:S(2)}) %collective-permute-start.2) | collective-permute-done | bytes 102432 | tf_op jit(solution)/shard_map/ppermute | solution.py:545
  11.1 6.3 %collective-permute-start.4 = (f32[2,25,8,128]{3,2,1,0:T(8,128)S(1)}, f32[2,25,8,128]{3,2,1,0:T(8,128)S(1)}, u32[]{:S(2)}, u32[]{:S(2)}) collective-permute-start(f32[2,25,8,128]{3,2,1,0:T(8,128)S(1)} %pad_maximum_fusion.own_ref), channel_id=1, source_target_pairs={{4,8},{8,4},{5,9},{9,5},{6,10},{10,6},{7,11},{11,7},{20,24},{24,20... | collective-permute-start | bytes 614408 | tf_op jit(solution)/shard_map/ppermute | solution.py:54
  17.4 0.1 collective-permute-start.3
  17.5 1.1 %bands.1 = (f32[9,24,768]{2,1,0:T(8,128)S(1)}, f32[9,16,768]{2,1,0:T(8,128)S(1)}, f32[9,16,768]{2,1,0:T(8,128)S(1)}, f32[9,16,768]{2,1,0:T(8,128)S(1)}) custom-call(f32[3,3,27]{2,1,0:T(4,128)} %bitcast.6), custom_call_target="tpu_custom_call" | custom-call | tf_op jit(solution)/shard_map/bands/pallas_call | solution.py:502
  18.5 2.3 %collective-permute-done.4.b_ref = f32[2,25,8,128]{3,2,1,0:T(8,128)S(1)} collective-permute-done((f32[2,25,8,128]{3,2,1,0:T(8,128)S(1)}, f32[2,25,8,128]{3,2,1,0:T(8,128)S(1)}, u32[]{:S(2)}, u32[]{:S(2)}) %collective-permute-start.4) | collective-permute-done | bytes 204832 | tf_op jit(solution)/shard_map/ppermute | solution.py:54
  20.8 0.0 collective-permute-done.3.a_ref
  20.8 3.9 %cycle.1 = (f32[3,4,8,128]{3,2,1,0:T(8,128)}, f32[4,8,128]{2,1,0:T(8,128)}) custom-call(f32[2,25,8,128]{3,2,1,0:T(8,128)S(1)} %pad_maximum_fusion.own_ref, f32[2,25,8,128]{3,2,1,0:T(8,128)S(1)} %collective-permute-done.3.a_ref, f32[2,25,8,128]{3,2,1,0:T(8,128)S(1)} %collective-permute-done.4.b_ref, f32[9,24,768]{2,1,0:T(8,128)S(1)} %get-tuple-element.12.smooth_ref, ...), custom_call_target="tpu_custom_call" | custom-call | tf_op jit(solution)/shard_map/cycle/pallas_call | solution.py:562
  (4 shorter events, 0.1 us)
Async XLA Ops:
  1.6 3.3 %collective-permute-start = (f32[5,8,128]{2,1,0:T(8,128)S(1)}, f32[5,8,128]{2,1,0:T(8,128)S(1)}, u32[]{:S(2)}, u32[]{:S(2)}) collective-permute-start(f32[5,8,128]{2,1,0:T(8,128)S(1)} %get-tuple-element.10), channel_id=1, source_target_pairs={{0,1},{1,0},{2,3},{3,2},{4,5},{5,4},{6,7},{7,6},{8,9},{9,8},{10,11... | collective-permute-start | bytes 61448 | tf_op jit(solution)/shard_map/ppermute | solution.py:54
  3.0 4.5 %collective-permute-start.1 = (f32[5,8,128]{2,1,0:T(8,128)S(1)}, f32[5,8,128]{2,1,0:T(8,128)S(1)}, u32[]{:S(2)}, u32[]{:S(2)}) collective-permute-start(f32[5,8,128]{2,1,0:T(8,128)S(1)} %get-tuple-element.11), channel_id=1, source_target_pairs={{1,2},{2,1},{5,6},{6,5},{9,10},{10,9},{13,14},{14,13},{17,18},{18,... | collective-permute-start | bytes 61448 | tf_op jit(solution)/shard_map/ppermute | solution.py:54
  7.5 3.6 %collective-permute-start.2 = (f32[25,8,128]{2,1,0:T(8,128)S(1)}, f32[25,8,128]{2,1,0:T(8,128)S(1)}, u32[]{:S(2)}, u32[]{:S(2)}) collective-permute-start(f32[25,8,128]{2,1,0:T(8,128)S(1)} %get-tuple-element.17), channel_id=1, source_target_pairs={{0,16},{16,0},{1,17},{17,1},{2,18},{18,2},{3,19},{19,3},{4,20},{20... | collective-permute-start | bytes 307208 | tf_op jit(solution)/shard_map/ppermute | solution.py:545
  11.1 9.7 %collective-permute-start.4 = (f32[2,25,8,128]{3,2,1,0:T(8,128)S(1)}, f32[2,25,8,128]{3,2,1,0:T(8,128)S(1)}, u32[]{:S(2)}, u32[]{:S(2)}) collective-permute-start(f32[2,25,8,128]{3,2,1,0:T(8,128)S(1)} %pad_maximum_fusion.own_ref), channel_id=1, source_target_pairs={{4,8},{8,4},{5,9},{9,5},{6,10},{10,6},{7,11},{11,7},{20,24},{24,20... | collective-permute-start | bytes 614408 | tf_op jit(solution)/shard_map/ppermute | solution.py:54
  17.4 3.4 %collective-permute-start.3 = (f32[2,25,8,128]{3,2,1,0:T(8,128)S(1)}, f32[2,25,8,128]{3,2,1,0:T(8,128)S(1)}, u32[]{:S(2)}, u32[]{:S(2)}) collective-permute-start(f32[2,25,8,128]{3,2,1,0:T(8,128)S(1)} %pad_maximum_fusion.own_ref), channel_id=1, source_target_pairs={{0,4},{4,0},{8,12},{12,8},{1,5},{5,1},{9,13},{13,9},{2,6},{6,2},{1... | collective-permute-start | bytes 614408 | tf_op jit(solution)/shard_map/ppermute | solution.py:54

commit v5 on v4

--- a/solution.py
+++ b/solution.py
@@ -14,6 +14,7 @@
 LANES = 128
 COLS = 8
 REACH = 6
+PRESS_REACH = 2
 FIELDS = 5
 LEAD = 2
 STRIP = 4 * COLS
@@ -169,6 +170,42 @@
         b_ref[f] = jnp.where(odd, up[f], down[f])
 
 
+def packed_row(planes, f, p):
+    if f < FIELDS - 1:
+        return (f * (planes + 1) + p) * REACH
+    return (FIELDS - 1) * (planes + 1) * REACH + p * PRESS_REACH
+
+
+def packed_rows(planes):
+    return -(-packed_row(planes, FIELDS - 1, planes + 1) // SUB) * SUB
+
+
+def message_kernel(planes, blocks, *refs):
+    parts, (a_ref, b_ref) = refs[:blocks], refs[blocks:]
+    odd = lax.axis_index("gy") % 2 == 1
+    rows = packed_rows(planes)
+
+    def pack(to_low, to_high):
+        for q in range(blocks):
+            for ref in (to_low, to_high):
+                ref[q, rows - SUB :, :] = jnp.zeros((SUB, LANES), jnp.float32)
+            for f in range(FIELDS):
+                count = REACH if f < FIELDS - 1 else PRESS_REACH
+                for p in range(planes + 1):
+                    index = FIELDS * planes + f if p == planes else f * planes + p
+                    at = packed_row(planes, f, p)
+                    to_low[q, at : at + count, :] = parts[q][index, :count, :]
+                    to_high[q, at : at + count, :] = parts[q][index, SUB - count :, :]
+
+    @pl.when(odd)
+    def _():
+        pack(a_ref, b_ref)
+
+    @pl.when(jnp.logical_not(odd))
+    def _():
+        pack(b_ref, a_ref)
+
+
 def cycle_kernel(
     planes,
     blocks,
@@ -191,7 +228,7 @@
     resid,
     press,
 ):
-    theta, delta, rho_zero, rho_one = cheb_consts()
+    _, delta, rho_zero, rho_one = cheb_consts()
     weight = 2.0 * rho_one / delta
     carry = rho_one * rho_zero
     total = planes * blocks
@@ -225,15 +262,14 @@
                 work[j, k, r * SUB : (r + 1) * SUB, :] = zero
             press[k, r * SUB : (r + 1) * SUB, :] = zero
 
-    def assemble(src, row):
+    def assemble(row, tile_of):
         at = slice(row, row + SUB)
         for q in range(blocks):
             here = slot(q)
             for f in range(FIELDS):
                 for p in range(planes + 1):
                     strip = p == planes
-                    index = FIELDS * planes + f if strip else f * planes + p
-                    value = src[here, index]
+                    value = tile_of(here, f, p)
                     fields[f, total + q if strip else q * planes + p, at, :] = value
                     spot = strips + q if strip else LEAD + q * planes + p
                     if f < 3:
@@ -241,17 +277,39 @@
                     if f == 4:
                         press[spot, at, :] = value
 
-    assemble(own_ref, OWN)
+    def own_tile(q, f, p):
+        return own_ref[q, FIELDS * planes + f if p == planes else f * planes + p]
+
+    def low_tile(ref):
+        def tile(q, f, p):
+            count = REACH if f < FIELDS - 1 else PRESS_REACH
+            at = packed_row(planes, f, p) + count - SUB
+            if at < 0:
+                return pltpu.roll(ref[q, :SUB, :], -at, 0)
+            return ref[q, at : at + SUB, :]
+
+        return tile
+
+    def high_tile(ref):
+        def tile(q, f, p):
+            at = packed_row(planes, f, p)
+            over = max(at + SUB - ref.shape[1], 0)
+            v = ref[q, at - over : at - over + SUB, :]
+            return pltpu.roll(v, SUB - over, 0) if over else v
+
+        return tile
+
+    assemble(OWN, own_tile)
 
     @pl.when(y_odd)
     def _():
-        assemble(a_ref, OWN - SUB)
-        assemble(b_ref, OWN + SUB)
+        assemble(OWN - SUB, low_tile(a_ref))
+        assemble(OWN + SUB, high_tile(b_ref))
 
     @pl.when(jnp.logical_not(y_odd))
     def _():
-        assemble(b_ref, OWN - SUB)
-        assemble(a_ref, OWN + SUB)
+        assemble(OWN - SUB, low_tile(b_ref))
+        assemble(OWN + SUB, high_tile(a_ref))
 
     def strip_shift(tiles_of, offset):
         turn = (LANES - offset * STRIP) % LANES
@@ -286,10 +344,10 @@
 
     blank = jnp.zeros((DEPTH - PIECE, 2 * LANES), jnp.float32)
 
-    def product(band, high, low):
+    def product(band_of, high, low):
         width = high.shape[1]
         return jnp.dot(
-            band,
+            band_of(),
             jnp.concatenate(
                 [high, blank[:, :width], high, blank[:, :width], low, blank[:, :width]]
             ),
@@ -300,7 +358,10 @@
     def apply(base, count, band_ref, first, rows, scale, emit, with_strips=True):
         height = rows * SUB
         half = -(-count // 2)
-        band = band_ref[:, first : first + height, :].reshape(9 * height, 3 * DEPTH)
+
+        def band_of():
+            return band_ref[:, first : first + height, :].reshape(9 * height, 3 * DEPTH)
+
         for n in range(half + 2 * scale):
             for side in range(2):
                 for j in range(3):
@@ -330,24 +391,9 @@
                 )
                 for n in range(2)
             )
-            made = product(band, high, low)
+            made = product(band_of, high, low)
             for w in range(width):
                 products[total + 2 + q + w, : 9 * height, :] = made[:, w * LANES : (w + 1) * LANES]
-        for n in range(half):
-            high, low = (
-                jnp.concatenate(
-                    [
-                        split[part, (n + a * scale) * size : (n + a * scale + 1) * size, :]
-                        for a in range(3)
-                    ]
-                )
-                for part in range(2)
-            )
-            made = product(band, high, low)
-            for side in range(2):
-                products[n + side * half, : 9 * height, :] = made[
-                    :, side * LANES : (side + 1) * LANES
-                ]
 
         def of(k, c, i, r):
             at = (c * 3 + i) * height + r * SUB
@@ -363,14 +409,35 @@
                         middle = middle + pltpu.roll(ahead, LANES - scale, 1)
                         middle = middle + pltpu.roll(behind, scale, 1)
                         emit(total + q, strips + q, None, r, i, middle)
-        for i in range(3):
-            for r in range(rows):
-                for k in range(count):
-                    q, p = place(base + k)
+
+        def finish(k):
+            q, p = place(base + k)
+            for i in range(3):
+                for r in range(rows):
                     behind, middle, ahead = (of(k, c, i, r) for c in range(3))
                     at = (i * 3 + r) * SUB
                     sides = z_shifts(ahead, behind, edge[q, at : at + SUB, :], p, scale)
                     emit(base + k, LEAD + base + k, k, r, i, middle + sides)
+
+        for n in range(half + 1):
+            if n < half:
+                high, low = (
+                    jnp.concatenate(
+                        [
+                            split[part, (n + a * scale) * size : (n + a * scale + 1) * size, :]
+                            for a in range(3)
+                        ]
+                    )
+                    for part in range(2)
+                )
+                made = product(band_of, high, low)
+                for side in range(2):
+                    products[n + side * half, : 9 * height, :] = made[
+                        :, side * LANES : (side + 1) * LANES
+                    ]
+            for side in range(2):
+                if n and n - 1 + side * half < count:
+                    finish(n - 1 + side * half)
 
     def inside(t, row):
         return fields[3, t, row : row + SUB, :] > 0.0
@@ -542,19 +609,27 @@
 
     paired = x_count == 2
     if paired:
-        frame = jnp.stack([block, lax.ppermute(block, "gx", [(0, 1), (1, 0)])])
-        blocks = 2
+        parts = [block, lax.ppermute(block, "gx", [(0, 1), (1, 0)])]
     else:
         hops = -(-REACH // planes)
         parts = []
         for hop in range(-hops, hops + 1):
             pairs = [(i, i - hop) for i in range(x_count) if 0 <= i - hop < x_count]
             parts.append(block if hop == 0 else matched(block, "gx", pairs))
-        frame = jnp.stack(parts)
-        blocks = 2 * hops + 1
-
-    y_first = matched(frame, "gy", first_pairs(y_count))
-    y_second = matched(frame, "gy", second_pairs(y_count))
+    blocks = len(parts)
+    frame = jnp.stack(parts)
+
+    message = jax.ShapeDtypeStruct((blocks, packed_rows(planes), LANES), jnp.float32)
+    y_first, y_second = pl.pallas_call(
+        functools.partial(message_kernel, planes, blocks),
+        out_shape=(message, message),
+        in_specs=[vmem] * blocks,
+        out_specs=(vmem, vmem),
+        compiler_params=pltpu.CompilerParams(vmem_limit_bytes=SMALL_VMEM),
+        name="message",
+    )(*parts)
+    y_first = matched(y_first, "gy", first_pairs(y_count))
+    y_second = matched(y_second, "gy", second_pairs(y_count))
 
     total = planes * blocks
     tiles = total + blocks

time: 25 us -> 25 us (level)
  no operation moved by 1% of the time
where the time goes in v5:
time: 25 us; the launch traced here: 24.7 us
  starting transfers between devices  10.9 us (44%)
  waiting for transfers between devices  7.08 us (28%)
  Pallas kernels  5.97 us (24%)
  between operations  0.71 us (3%)
    ppermute x4, starting transfers between devices, matched(): return lax.ppermute(block, axis, pairs)  9.6 us
    ppermute x4, waiting for transfers between devices, matched(): return lax.ppermute(block, axis, pairs)  4.81 us
    pallas_call x1, Pallas kernels, on_device(): pl.pallas_call(functools.partial(cycle_kernel, planes, blocks, paired), o...  3.89 us
    ppermute x1, waiting for transfers between devices, on_device(): parts = [block, lax.ppermute(block, 'gx', [(0, 1), (1, 0)])]  2.27 us
    ppermute x1, starting transfers between devices, on_device(): parts = [block, lax.ppermute(block, 'gx', [(0, 1), (1, 0)])]  1.3 us
    pallas_call x1, Pallas kernels, on_device(): pl.pallas_call(band_kernel, out_shape=tuple((jax.ShapeDtypeStruct((9, r *...  1.06 us
    pallas_call x1, Pallas kernels, on_device(): pl.pallas_call(functools.partial(pack_kernel, planes), out_shape=(jax.Sha...  0.99 us
  transfers between devices with their start and end apart: 5, of which 3 were waited for; matrix products, arithmetic and copies ran while one was open for 0% of the time, Pallas kernels for 4%

profile of v5, /device:TPU:17, one launch (start us, length us, event | category | flops | bytes accessed | tf_op | source)
XLA Modules:
  0.0 24.7 jit_solution(16295476464760466432)
XLA Ops:
  0.6 1.0 %pack.1 = (f32[25,8,128]{2,1,0:T(8,128)S(1)}, f32[5,8,128]{2,1,0:T(8,128)S(1)}, f32[5,8,128]{2,1,0:T(8,128)S(1)}) custom-call(f32[8]{0:T(128)} %visc_hbm.1, f32[3,3,27]{2,1,0:T(4,128)} %bitcast.5, f32[3,4,8,128]{3,2,1,0:T(8,128)} %rhs_hbm.1, f32[4,8,128]{2,1,0:T(8,128)} %press_hbm.1, s32[4,8,128]{2,1,0:T(8,128)} %ids_hbm.1), custom_call_target="tpu_custom_call" | custom-call | tf_op jit(solution)/shard_map/pack/pallas_call | solution.py:579
  1.6 1.4 %collective-permute-start = (f32[5,8,128]{2,1,0:T(8,128)S(1)}, f32[5,8,128]{2,1,0:T(8,128)S(1)}, u32[]{:S(2)}, u32[]{:S(2)}) collective-permute-start(f32[5,8,128]{2,1,0:T(8,128)S(1)} %get-tuple-element.12), channel_id=1, source_target_pairs={{0,1},{1,0},{2,3},{3,2},{4,5},{5,4},{6,7},{7,6},{8,9},{9,8},{10,11... | collective-permute-start | bytes 61448 | tf_op jit(solution)/shard_map/ppermute | solution.py:55
  3.0 1.9 %collective-permute-start.1 = (f32[5,8,128]{2,1,0:T(8,128)S(1)}, f32[5,8,128]{2,1,0:T(8,128)S(1)}, u32[]{:S(2)}, u32[]{:S(2)}) collective-permute-start(f32[5,8,128]{2,1,0:T(8,128)S(1)} %get-tuple-element.13), channel_id=1, source_target_pairs={{1,2},{2,1},{5,6},{6,5},{9,10},{10,9},{13,14},{14,13},{17,18},{18,... | collective-permute-start | bytes 61448 | tf_op jit(solution)/shard_map/ppermute | solution.py:55
  4.9 0.0 collective-permute-done
  4.9 2.6 %collective-permute-done.1 = f32[5,8,128]{2,1,0:T(8,128)S(1)} collective-permute-done((f32[5,8,128]{2,1,0:T(8,128)S(1)}, f32[5,8,128]{2,1,0:T(8,128)S(1)}, u32[]{:S(2)}, u32[]{:S(2)}) %collective-permute-start.1) | collective-permute-done | bytes 20512 | tf_op jit(solution)/shard_map/ppermute | solution.py:55
  7.5 1.3 %collective-permute-start.2 = (f32[25,8,128]{2,1,0:T(8,128)S(1)}, f32[25,8,128]{2,1,0:T(8,128)S(1)}, u32[]{:S(2)}, u32[]{:S(2)}) collective-permute-start(f32[25,8,128]{2,1,0:T(8,128)S(1)} %get-tuple-element.21.refs_0_), channel_id=1, source_target_pairs={{0,16},{16,0},{1,17},{17,1},{2,18},{18,2},{3,19},{19,3},{4,20},{20... | collective-permute-start | bytes 307208 | tf_op jit(solution)/shard_map/ppermute | solution.py:612
  8.8 2.3 %collective-permute-done.2.refs_1_ = f32[25,8,128]{2,1,0:T(8,128)S(1)} collective-permute-done((f32[25,8,128]{2,1,0:T(8,128)S(1)}, f32[25,8,128]{2,1,0:T(8,128)S(1)}, u32[]{:S(2)}, u32[]{:S(2)}) %collective-permute-start.2) | collective-permute-done | bytes 102432 | tf_op jit(solution)/shard_map/ppermute | solution.py:612
  11.1 3.3 %collective-permute-start.3 = (f32[2,136,128]{2,1,0:T(8,128)S(1)}, f32[2,136,128]{2,1,0:T(8,128)S(1)}, u32[]{:S(2)}, u32[]{:S(2)}) collective-permute-start(f32[2,136,128]{2,1,0:T(8,128)S(1)} %get-tuple-element.14), channel_id=1, source_target_pairs={{0,4},{4,0},{8,12},{12,8},{1,5},{5,1},{9,13},{13,9},{2,6},{6,2},{1... | collective-permute-start | bytes 417800 | tf_op jit(solution)/shard_map/ppermute | solution.py:55
  14.5 3.0 %collective-permute-start.4 = (f32[2,136,128]{2,1,0:T(8,128)S(1)}, f32[2,136,128]{2,1,0:T(8,128)S(1)}, u32[]{:S(2)}, u32[]{:S(2)}) collective-permute-start(f32[2,136,128]{2,1,0:T(8,128)S(1)} %get-tuple-element.15), channel_id=1, source_target_pairs={{4,8},{8,4},{5,9},{9,5},{6,10},{10,6},{7,11},{11,7},{20,24},{24,20... | collective-permute-start | bytes 417800 | tf_op jit(solution)/shard_map/ppermute | solution.py:55
  17.5 1.1 %bands.1 = (f32[9,24,768]{2,1,0:T(8,128)S(1)}, f32[9,16,768]{2,1,0:T(8,128)S(1)}, f32[9,16,768]{2,1,0:T(8,128)S(1)}, f32[9,16,768]{2,1,0:T(8,128)S(1)}) custom-call(f32[3,3,27]{2,1,0:T(4,128)} %bitcast.6), custom_call_target="tpu_custom_call" | custom-call | tf_op jit(solution)/shard_map/bands/pallas_call | solution.py:569
  18.6 0.0 collective-permute-done.3.a_ref
  18.6 2.2 %collective-permute-done.4.b_ref = f32[2,136,128]{2,1,0:T(8,128)S(1)} collective-permute-done((f32[2,136,128]{2,1,0:T(8,128)S(1)}, f32[2,136,128]{2,1,0:T(8,128)S(1)}, u32[]{:S(2)}, u32[]{:S(2)}) %collective-permute-start.4) | collective-permute-done | bytes 139296 | tf_op jit(solution)/shard_map/ppermute | solution.py:55
  20.8 3.9 %cycle.1 = (f32[3,4,8,128]{3,2,1,0:T(8,128)}, f32[4,8,128]{2,1,0:T(8,128)}) custom-call(f32[2,25,8,128]{3,2,1,0:T(8,128)S(1)} %pad_maximum_fusion.own_ref, f32[2,136,128]{2,1,0:T(8,128)S(1)} %collective-permute-done.3.a_ref, f32[2,136,128]{2,1,0:T(8,128)S(1)} %collective-permute-done.4.b_ref, f32[9,24,768]{2,1,0:T(8,128)S(1)} %get-tuple-element.16.smooth_ref, ...), custom_call_target="tpu_custom_call" | custom-call | tf_op jit(solution)/shard_map/cycle/pallas_call | solution.py:637
  (5 shorter events, 0.1 us)
Async XLA Ops:
  1.6 3.3 %collective-permute-start = (f32[5,8,128]{2,1,0:T(8,128)S(1)}, f32[5,8,128]{2,1,0:T(8,128)S(1)}, u32[]{:S(2)}, u32[]{:S(2)}) collective-permute-start(f32[5,8,128]{2,1,0:T(8,128)S(1)} %get-tuple-element.12), channel_id=1, source_target_pairs={{0,1},{1,0},{2,3},{3,2},{4,5},{5,4},{6,7},{7,6},{8,9},{9,8},{10,11... | collective-permute-start | bytes 61448 | tf_op jit(solution)/shard_map/ppermute | solution.py:55
  3.0 4.5 %collective-permute-start.1 = (f32[5,8,128]{2,1,0:T(8,128)S(1)}, f32[5,8,128]{2,1,0:T(8,128)S(1)}, u32[]{:S(2)}, u32[]{:S(2)}) collective-permute-start(f32[5,8,128]{2,1,0:T(8,128)S(1)} %get-tuple-element.13), channel_id=1, source_target_pairs={{1,2},{2,1},{5,6},{6,5},{9,10},{10,9},{13,14},{14,13},{17,18},{18,... | collective-permute-start | bytes 61448 | tf_op jit(solution)/shard_map/ppermute | solution.py:55
  7.5 3.6 %collective-permute-start.2 = (f32[25,8,128]{2,1,0:T(8,128)S(1)}, f32[25,8,128]{2,1,0:T(8,128)S(1)}, u32[]{:S(2)}, u32[]{:S(2)}) collective-permute-start(f32[25,8,128]{2,1,0:T(8,128)S(1)} %get-tuple-element.21.refs_0_), channel_id=1, source_target_pairs={{0,16},{16,0},{1,17},{17,1},{2,18},{18,2},{3,19},{19,3},{4,20},{20... | collective-permute-start | bytes 307208 | tf_op jit(solution)/shard_map/ppermute | solution.py:612
  11.1 7.4 %collective-permute-start.3 = (f32[2,136,128]{2,1,0:T(8,128)S(1)}, f32[2,136,128]{2,1,0:T(8,128)S(1)}, u32[]{:S(2)}, u32[]{:S(2)}) collective-permute-start(f32[2,136,128]{2,1,0:T(8,128)S(1)} %get-tuple-element.14), channel_id=1, source_target_pairs={{0,4},{4,0},{8,12},{12,8},{1,5},{5,1},{9,13},{13,9},{2,6},{6,2},{1... | collective-permute-start | bytes 417800 | tf_op jit(solution)/shard_map/ppermute | solution.py:55
  14.5 6.4 %collective-permute-start.4 = (f32[2,136,128]{2,1,0:T(8,128)S(1)}, f32[2,136,128]{2,1,0:T(8,128)S(1)}, u32[]{:S(2)}, u32[]{:S(2)}) collective-permute-start(f32[2,136,128]{2,1,0:T(8,128)S(1)} %get-tuple-element.15), channel_id=1, source_target_pairs={{4,8},{8,4},{5,9},{9,5},{6,10},{10,6},{7,11},{11,7},{20,24},{24,20... | collective-permute-start | bytes 417800 | tf_op jit(solution)/shard_map/ppermute | solution.py:55

commit v6 on v5

--- a/solution.py
+++ b/solution.py
@@ -42,11 +42,21 @@
     return [(i, i ^ 1) for i in range(count) if i ^ 1 < count]
 
 
-def second_pairs(count):
+def second_pairs(x_count, count):
     pairs = []
-    for i in range(1, count - 1, 2):
-        pairs += [(i, i + 1), (i + 1, i)]
+    for x in range(x_count):
+        for i in range(1, count - 1, 2):
+            here = x * count + i
+            pairs += [(here, here + 1), (here + 1, here)]
+    if pairs and wraps(x_count, count):
+        for x in range(x_count):
+            for i in (0, count - 1):
+                pairs.append((x * count + i, (x ^ 1) * count + i))
     return pairs
+
+
+def wraps(x_count, count):
+    return x_count % 2 == 0 and count % 2 == 0
 
 
 def matched(block, axis, pairs):
@@ -144,7 +154,9 @@
     for copy in copies:
         copy.wait()
     lane = lane_iota()
-    odd = lax.axis_index("gz") % 2 == 1
+    count, at = lax.axis_size("gz"), lax.axis_index("gz")
+    odd = at % 2 == 1
+    at_end = (at == 0) | (at == count - 1)
     kc = jnp.full((SUB, LANES), diagonal_mean(stencil_ref), jnp.float32)
     zero = jnp.zeros((SUB, LANES), jnp.float32)
     up, down, own = [zero] * FIELDS, [zero] * FIELDS, [zero] * FIELDS
@@ -167,7 +179,8 @@
     for f in range(FIELDS):
         main_ref[FIELDS * planes + f] = own[f]
         a_ref[f] = jnp.where(odd, down[f], up[f])
-        b_ref[f] = jnp.where(odd, up[f], down[f])
+        outer = jnp.where(odd, up[f], down[f])
+        b_ref[f] = jnp.where(at_end, 0.0, outer) if wraps(lax.axis_size("gx"), count) else outer
 
 
 def packed_row(planes, f, p):
@@ -204,6 +217,13 @@
     @pl.when(jnp.logical_not(odd))
     def _():
         pack(b_ref, a_ref)
+
+    if wraps(lax.axis_size("gx"), lax.axis_size("gy")):
+        at = lax.axis_index("gy")
+
+        @pl.when((at == 0) | (at == lax.axis_size("gy") - 1))
+        def _():
+            b_ref[...] = jnp.zeros_like(b_ref)
 
 
 def cycle_kernel(
@@ -603,7 +623,7 @@
     )
 
     halo = matched(z_first, "gz", first_pairs(z_count))
-    halo = halo + matched(z_second, "gz", second_pairs(z_count))
+    halo = halo + matched(z_second, ("gx", "gz"), second_pairs(x_count, z_count))
     inner = FIELDS * planes
     block = jnp.concatenate([main[:inner], main[inner:] + halo])
 
@@ -629,7 +649,7 @@
         name="message",
     )(*parts)
     y_first = matched(y_first, "gy", first_pairs(y_count))
-    y_second = matched(y_second, "gy", second_pairs(y_count))
+    y_second = matched(y_second, ("gx", "gy"), second_pairs(x_count, y_count))
 
     total = planes * blocks
     tiles = total + blocks

time: 25 us -> 22.6 us (0.904)
  the two profiles are of different devices: /device:TPU:17 before, /device:TPU:0 now
where the time goes in v6:
time: 22.6 us; the launch traced here: 22.4 us
  starting transfers between devices  7.88 us (35%)
  waiting for transfers between devices  7.83 us (35%)
  Pallas kernels  5.98 us (26%)
  between operations  0.68 us (3%)
    ppermute x4, starting transfers between devices, matched(): return lax.ppermute(block, axis, pairs)  6.29 us
    ppermute x4, waiting for transfers between devices, matched(): return lax.ppermute(block, axis, pairs)  4.69 us
    pallas_call x1, Pallas kernels, on_device(): pl.pallas_call(functools.partial(cycle_kernel, planes, blocks, paired), o...  3.89 us
    ppermute x1, waiting for transfers between devices, on_device(): parts = [block, lax.ppermute(block, 'gx', [(0, 1), (1, 0)])]  3.14 us
    ppermute x1, starting transfers between devices, on_device(): parts = [block, lax.ppermute(block, 'gx', [(0, 1), (1, 0)])]  1.58 us
    pallas_call x1, Pallas kernels, on_device(): pl.pallas_call(band_kernel, out_shape=tuple((jax.ShapeDtypeStruct((9, r *...  1.06 us
    pallas_call x1, Pallas kernels, on_device(): pl.pallas_call(functools.partial(pack_kernel, planes), out_shape=(jax.Sha...  0.99 us
  transfers between devices with their start and end apart: 5, of which 4 were waited for; matrix products, arithmetic and copies ran while one was open for 0% of the time, Pallas kernels for 5%

profile of v6, /device:TPU:0, one launch (start us, length us, event | category | flops | bytes accessed | tf_op | source)
XLA Modules:
  0.0 22.4 jit_solution(13542164580561187511)
XLA Ops:
  0.6 1.0 %pack.1 = (f32[25,8,128]{2,1,0:T(8,128)S(1)}, f32[5,8,128]{2,1,0:T(8,128)S(1)}, f32[5,8,128]{2,1,0:T(8,128)S(1)}) custom-call(f32[8]{0:T(128)} %visc_hbm.1, f32[3,3,27]{2,1,0:T(4,128)} %bitcast.5, f32[3,4,8,128]{3,2,1,0:T(8,128)} %rhs_hbm.1, f32[4,8,128]{2,1,0:T(8,128)} %press_hbm.1, s32[4,8,128]{2,1,0:T(8,128)} %ids_hbm.1), custom_call_target="tpu_custom_call" | custom-call | tf_op jit(solution)/shard_map/pack/pallas_call | solution.py:599
  1.6 3.1 %collective-permute-start = (f32[5,8,128]{2,1,0:T(8,128)S(1)}, f32[5,8,128]{2,1,0:T(8,128)S(1)}, u32[]{:S(2)}, u32[]{:S(2)}) collective-permute-start(f32[5,8,128]{2,1,0:T(8,128)S(1)} %get-tuple-element.12), channel_id=1, source_target_pairs={{0,1},{1,0},{2,3},{3,2},{4,5},{5,4},{6,7},{7,6},{8,9},{9,8},{10,11... | collective-permute-start | bytes 61448 | tf_op jit(solution)/shard_map/ppermute | solution.py:65
  4.7 1.5 %collective-permute-start.1 = (f32[5,8,128]{2,1,0:T(8,128)S(1)}, f32[5,8,128]{2,1,0:T(8,128)S(1)}, u32[]{:S(2)}, u32[]{:S(2)}) collective-permute-start(f32[5,8,128]{2,1,0:T(8,128)S(1)} %get-tuple-element.13), channel_id=1, source_target_pairs={{1,2},{2,1},{17,18},{18,17},{0,16},{3,19},{16,0},{19,3},{5,6},{6,5... | collective-permute-start | bytes 61448 | tf_op jit(solution)/shard_map/ppermute | solution.py:65
  6.3 0.2 %collective-permute-done = f32[5,8,128]{2,1,0:T(8,128)S(1)} collective-permute-done((f32[5,8,128]{2,1,0:T(8,128)S(1)}, f32[5,8,128]{2,1,0:T(8,128)S(1)}, u32[]{:S(2)}, u32[]{:S(2)}) %collective-permute-start) | collective-permute-done | bytes 20512 | tf_op jit(solution)/shard_map/ppermute | solution.py:65
  6.5 2.0 %collective-permute-done.1 = f32[5,8,128]{2,1,0:T(8,128)S(1)} collective-permute-done((f32[5,8,128]{2,1,0:T(8,128)S(1)}, f32[5,8,128]{2,1,0:T(8,128)S(1)}, u32[]{:S(2)}, u32[]{:S(2)}) %collective-permute-start.1) | collective-permute-done | bytes 20512 | tf_op jit(solution)/shard_map/ppermute | solution.py:65
  8.5 1.6 %collective-permute-start.2 = (f32[25,8,128]{2,1,0:T(8,128)S(1)}, f32[25,8,128]{2,1,0:T(8,128)S(1)}, u32[]{:S(2)}, u32[]{:S(2)}) collective-permute-start(f32[25,8,128]{2,1,0:T(8,128)S(1)} %get-tuple-element.21.refs_0_), channel_id=1, source_target_pairs={{0,16},{16,0},{1,17},{17,1},{2,18},{18,2},{3,19},{19,3},{4,20},{20... | collective-permute-start | bytes 307208 | tf_op jit(solution)/shard_map/ppermute | solution.py:632
  10.1 3.1 %collective-permute-done.2.refs_1_ = f32[25,8,128]{2,1,0:T(8,128)S(1)} collective-permute-done((f32[25,8,128]{2,1,0:T(8,128)S(1)}, f32[25,8,128]{2,1,0:T(8,128)S(1)}, u32[]{:S(2)}, u32[]{:S(2)}) %collective-permute-start.2) | collective-permute-done | bytes 102432 | tf_op jit(solution)/shard_map/ppermute | solution.py:632
  13.3 0.1 collective-permute-start.3
  13.4 1.6 %collective-permute-start.4 = (f32[2,136,128]{2,1,0:T(8,128)S(1)}, f32[2,136,128]{2,1,0:T(8,128)S(1)}, u32[]{:S(2)}, u32[]{:S(2)}) collective-permute-start(f32[2,136,128]{2,1,0:T(8,128)S(1)} %get-tuple-element.15), channel_id=1, source_target_pairs={{4,8},{8,4},{20,24},{24,20},{0,16},{12,28},{16,0},{28,12},{5,9},{9... | collective-permute-start | bytes 417800 | tf_op jit(solution)/shard_map/ppermute | solution.py:65
  15.0 1.1 %bands.1 = (f32[9,24,768]{2,1,0:T(8,128)S(1)}, f32[9,16,768]{2,1,0:T(8,128)S(1)}, f32[9,16,768]{2,1,0:T(8,128)S(1)}, f32[9,16,768]{2,1,0:T(8,128)S(1)}) custom-call(f32[3,3,27]{2,1,0:T(4,128)} %bitcast.6), custom_call_target="tpu_custom_call" | custom-call | tf_op jit(solution)/shard_map/bands/pallas_call | solution.py:589
  16.1 0.0 collective-permute-done.3.a_ref
  16.1 2.4 %collective-permute-done.4.b_ref = f32[2,136,128]{2,1,0:T(8,128)S(1)} collective-permute-done((f32[2,136,128]{2,1,0:T(8,128)S(1)}, f32[2,136,128]{2,1,0:T(8,128)S(1)}, u32[]{:S(2)}, u32[]{:S(2)}) %collective-permute-start.4) | collective-permute-done | bytes 139296 | tf_op jit(solution)/shard_map/ppermute | solution.py:65
  18.5 3.9 %cycle.1 = (f32[3,4,8,128]{3,2,1,0:T(8,128)}, f32[4,8,128]{2,1,0:T(8,128)}) custom-call(f32[2,25,8,128]{3,2,1,0:T(8,128)S(1)} %pad_maximum_fusion.own_ref, f32[2,136,128]{2,1,0:T(8,128)S(1)} %collective-permute-done.3.a_ref, f32[2,136,128]{2,1,0:T(8,128)S(1)} %collective-permute-done.4.b_ref, f32[9,24,768]{2,1,0:T(8,128)S(1)} %get-tuple-element.16.smooth_ref, ...), custom_call_target="tpu_custom_call" | custom-call | tf_op jit(solution)/shard_map/cycle/pallas_call | solution.py:657
  (5 shorter events, 0.1 us)
Async XLA Ops:
  1.6 4.9 %collective-permute-start = (f32[5,8,128]{2,1,0:T(8,128)S(1)}, f32[5,8,128]{2,1,0:T(8,128)S(1)}, u32[]{:S(2)}, u32[]{:S(2)}) collective-permute-start(f32[5,8,128]{2,1,0:T(8,128)S(1)} %get-tuple-element.12), channel_id=1, source_target_pairs={{0,1},{1,0},{2,3},{3,2},{4,5},{5,4},{6,7},{7,6},{8,9},{9,8},{10,11... | collective-permute-start | bytes 61448 | tf_op jit(solution)/shard_map/ppermute | solution.py:65
  4.7 3.8 %collective-permute-start.1 = (f32[5,8,128]{2,1,0:T(8,128)S(1)}, f32[5,8,128]{2,1,0:T(8,128)S(1)}, u32[]{:S(2)}, u32[]{:S(2)}) collective-permute-start(f32[5,8,128]{2,1,0:T(8,128)S(1)} %get-tuple-element.13), channel_id=1, source_target_pairs={{1,2},{2,1},{17,18},{18,17},{0,16},{3,19},{16,0},{19,3},{5,6},{6,5... | collective-permute-start | bytes 61448 | tf_op jit(solution)/shard_map/ppermute | solution.py:65
  8.5 4.7 %collective-permute-start.2 = (f32[25,8,128]{2,1,0:T(8,128)S(1)}, f32[25,8,128]{2,1,0:T(8,128)S(1)}, u32[]{:S(2)}, u32[]{:S(2)}) collective-permute-start(f32[25,8,128]{2,1,0:T(8,128)S(1)} %get-tuple-element.21.refs_0_), channel_id=1, source_target_pairs={{0,16},{16,0},{1,17},{17,1},{2,18},{18,2},{3,19},{19,3},{4,20},{20... | collective-permute-start | bytes 307208 | tf_op jit(solution)/shard_map/ppermute | solution.py:632
  13.3 2.8 %collective-permute-start.3 = (f32[2,136,128]{2,1,0:T(8,128)S(1)}, f32[2,136,128]{2,1,0:T(8,128)S(1)}, u32[]{:S(2)}, u32[]{:S(2)}) collective-permute-start(f32[2,136,128]{2,1,0:T(8,128)S(1)} %get-tuple-element.14), channel_id=1, source_target_pairs={{0,4},{4,0},{8,12},{12,8},{1,5},{5,1},{9,13},{13,9},{2,6},{6,2},{1... | collective-permute-start | bytes 417800 | tf_op jit(solution)/shard_map/ppermute | solution.py:65
  13.4 5.1 %collective-permute-start.4 = (f32[2,136,128]{2,1,0:T(8,128)S(1)}, f32[2,136,128]{2,1,0:T(8,128)S(1)}, u32[]{:S(2)}, u32[]{:S(2)}) collective-permute-start(f32[2,136,128]{2,1,0:T(8,128)S(1)} %get-tuple-element.15), channel_id=1, source_target_pairs={{4,8},{8,4},{20,24},{24,20},{0,16},{12,28},{16,0},{28,12},{5,9},{9... | collective-permute-start | bytes 417800 | tf_op jit(solution)/shard_map/ppermute | solution.py:65

commit v7 on v6

--- a/solution.py
+++ b/solution.py
@@ -23,8 +23,10 @@
 ROWS_RESID = OWN - 4
 ROWS_START = OWN - 2
 ROWS_MIDDLE = OWN - 1
-DEPTH = 2 * LANES
-PIECE = 9 * SUB * 3
+WINDOW = 2 * SUB
+WINDOW_COARSE = ROWS_START - 2
+WINDOW_MIDDLE = ROWS_MIDDLE - 1
+WINDOW_LAST = OWN - 1
 SMALL_VMEM = 4 * 1024 * 1024
 CYCLE_VMEM = 32 * 1024 * 1024
 
@@ -79,45 +81,42 @@
     sub = lax.broadcasted_iota(jnp.int32, (SUB, LANES), 0)
     lane = lane_iota()
     zero = jnp.zeros((SUB, LANES), jnp.float32)
-    halves = []
-    for half in range(DEPTH // LANES):
-        spot = lane + half * LANES
-        groups = range(half * LANES // ROWS, min(((half + 1) * LANES - 1) // ROWS, 8) + 1)
-        start = jnp.full((SUB, LANES), groups[0] * ROWS, jnp.int32)
-        for n in groups[1:]:
-            start = jnp.where(spot >= n * ROWS, n * ROWS, start)
-        reach = jnp.where(spot < 9 * ROWS, spot - start - sub, 1000)
-        halves.append((reach, [(n, start == n * ROWS) for n in groups]))
-    for c in range(3):
-        for i in range(3):
-            rows_of = []
-            for b in range(3):
-                row = []
-                for reach, groups in halves:
-                    full = zero
-                    for n, here in groups:
-                        a, j = divmod(n, 3)
-                        full = jnp.where(here, stencil_ref[i, j, 9 * a + 3 * b + c], full)
-                    full = scale * full
-                    high = full.astype(jnp.bfloat16).astype(jnp.float32)
-                    row.append((high, full - high))
-                rows_of.append(row)
-            for ref, start, step in (
-                (smooth_ref, 0, 1),
-                (resid_ref, ROWS_RESID, 1),
-                (coarse_ref, ROWS_START, 2),
-                (middle_ref, ROWS_MIDDLE, 1),
-            ):
-                for r in range(ref.shape[1] // SUB):
-                    for half, (reach, _) in enumerate(halves):
-                        high, low = zero, zero
-                        for b in range(3):
-                            here = reach == r * SUB + start + step * (b - 1)
-                            high = jnp.where(here, rows_of[b][half][0], high)
-                            low = jnp.where(here, rows_of[b][half][1], low)
-                        for term, value in enumerate((high, low, high)):
-                            at = (2 * term + half) * LANES
-                            ref[c * 3 + i, r * SUB : (r + 1) * SUB, at : at + LANES] = value
+    kinds = (
+        (ROWS, ((smooth_ref, 0, 1), (resid_ref, ROWS_RESID, 1))),
+        (WINDOW, ((coarse_ref, ROWS_START - WINDOW_COARSE, 2), (middle_ref, 1, 1))),
+    )
+    for depth, users in kinds:
+        for half in range(-(-27 * depth // LANES)):
+            spot = lane + half * LANES
+            first = half * LANES // depth
+            last = min(((half + 1) * LANES - 1) // depth, 26)
+            start = jnp.full((SUB, LANES), first * depth, jnp.int32)
+            for n in range(first + 1, last + 1):
+                start = jnp.where(spot >= n * depth, n * depth, start)
+            reach = spot - start - sub
+            here = [(n, start == n * depth) for n in range(first, last + 1)]
+            is_low = (start >= 9 * depth) & (start < 18 * depth)
+            width = min(LANES, 27 * depth - half * LANES)
+            lanes = slice(half * LANES, half * LANES + width)
+            for c in range(3):
+                for i in range(3):
+                    rows_of = []
+                    for b in range(3):
+                        full = zero
+                        for n, mask in here:
+                            a, j = divmod(n % 9, 3)
+                            entry = stencil_ref[i, j, 9 * a + 3 * b + c]
+                            full = jnp.where(mask, entry, full)
+                        full = scale * full
+                        high = full.astype(jnp.bfloat16).astype(jnp.float32)
+                        rows_of.append(jnp.where(is_low, full - high, high))
+                    for ref, offset, step in users:
+                        for r in range(ref.shape[1] // SUB):
+                            value = zero
+                            for b in range(3):
+                                at = r * SUB + offset + step * (b - 1)
+                                value = jnp.where(reach == at, rows_of[b], value)
+                            ref[c * 3 + i, r * SUB : (r + 1) * SUB, lanes] = value[:, :width]
 
 
 def pack_kernel(
@@ -362,45 +361,42 @@
         high = v.astype(jnp.bfloat16).astype(jnp.float32)
         return high, v - high
 
-    blank = jnp.zeros((DEPTH - PIECE, 2 * LANES), jnp.float32)
-
     def product(band_of, high, low):
-        width = high.shape[1]
         return jnp.dot(
             band_of(),
-            jnp.concatenate(
-                [high, blank[:, :width], high, blank[:, :width], low, blank[:, :width]]
-            ),
+            jnp.concatenate([high, high, low]),
             preferred_element_type=jnp.float32,
             precision=lax.Precision.DEFAULT,
         )
 
-    def apply(base, count, band_ref, first, rows, scale, emit, with_strips=True):
+    def apply(base, count, band_ref, window, rows, scale, emit, with_strips=True):
         height = rows * SUB
         half = -(-count // 2)
+        depth = band_ref.shape[2] // 27
+        inputs = [window + r * SUB for r in range(depth // SUB)]
 
         def band_of():
-            return band_ref[:, first : first + height, :].reshape(9 * height, 3 * DEPTH)
+            return band_ref[:, :height, :].reshape(9 * height, 27 * depth)
 
         for n in range(half + 2 * scale):
             for side in range(2):
                 for j in range(3):
-                    for r in range(3):
+                    for r, row in enumerate(inputs):
                         spot = LEAD + base - scale + side * half + n
-                        high, low = parts_of(work[j, spot, r * SUB : (r + 1) * SUB, :])
-                        at = ((n * 3 + j) * 3 + r) * SUB
+                        high, low = parts_of(work[j, spot, row : row + SUB, :])
+                        at = (n * 3 + j) * depth + r * SUB
                         lanes = slice(side * LANES, (side + 1) * LANES)
                         split[0, at : at + SUB, lanes] = high
                         split[1, at : at + SUB, lanes] = low
-        size = 9 * SUB
+        size = 3 * depth
         for q in range(0, blocks, 2):
             width = min(2, blocks - q)
             pieces = []
             for a in range(3):
                 for j in range(3):
-                    for r in range(3):
+                    for row in inputs:
                         tiles_of = [
-                            work[j, strips + p, r * SUB : (r + 1) * SUB, :] for p in range(blocks)
+                            work[j, strips + p, row : row + SUB, :] for p in range(blocks)
                         ]
                         if a != 1:
                             tiles_of = strip_shift(tiles_of, (a - 1) * scale)
@@ -517,7 +513,7 @@
         value = jnp.where(inside(t, ROWS_START + r * SUB), value - weight * total_of, 0.0)
         work[i, w, at, :] = value
 
-    apply(*span(2), coarse_ref, 0, 2, 2, emit_start)
+    apply(*span(2), coarse_ref, WINDOW_COARSE, 2, 2, emit_start)
 
     def emit_middle(t, w, k, r, i, total_of):
         at = slice(ROWS_MIDDLE + r * SUB, ROWS_MIDDLE + (r + 1) * SUB)
@@ -525,15 +521,9 @@
         work[i, w, at, :] = work[i, w, at, :] + step
         second_x[i, t, at, :] = step
 
-    apply(*span(1), middle_ref, 0, 2, 1, emit_middle)
+    apply(*span(1), middle_ref, WINDOW_MIDDLE, 2, 1, emit_middle)
 
     own = slice(OWN, OWN + SUB)
-
-    def emit_last(t, w, k, r, i, total_of):
-        value = work[i, w, own, :] + carry * second_x[i, t, own, :]
-        vel_ref[i, k] = value + weight * (fields[i, t, own, :] - total_of)
-
-    apply(*span(0), smooth_ref, OWN, 1, 1, emit_last, with_strips=False)
 
     def strip_sides(row):
         return [press[strips + q, row : row + SUB, :] for q in range(blocks)]
@@ -544,12 +534,12 @@
         v = v + press[LEAD + k - 1, row : row + SUB, :] + press[LEAD + k + 1, row : row + SUB, :]
         q, p = place(k)
         here = press[LEAD + k, row : row + SUB, :]
-        return v + z_shifts(here, here, edge[q, at : at + SUB, :], p, 1)
+        return v + z_shifts(here, here, edge[q, 9 * SUB + at : 10 * SUB + at, :], p, 1)
 
     def set_edges(row, at):
         for q in range(blocks):
             v = press[strips + q, row : row + SUB, :]
-            edge[q, at : at + SUB, :] = edge_source(v, v, 1)
+            edge[q, 9 * SUB + at : 10 * SUB + at, :] = edge_source(v, v, 1)
 
     starts = (OWN - 1, OWN + 1)
     base, count = span(1)
@@ -576,6 +566,12 @@
         v = press[LEAD + base + k, own, :] * (1.0 / 3.0) + fields[4, base + k, own, :]
         press_ref[k] = v + beside(base + k, OWN, 0) * (1.0 / 9.0)
 
+    def emit_last(t, w, k, r, i, total_of):
+        value = work[i, w, own, :] + carry * second_x[i, t, own, :]
+        vel_ref[i, k] = value + weight * (fields[i, t, own, :] - total_of)
+
+    apply(*span(0), middle_ref, WINDOW_LAST, 1, 1, emit_last, with_strips=False)
+
 
 def on_device(rhs_velocity, rhs_pressure, layer_ids, visc_table, stencil):
     planes, rows, depth = rhs_pressure.shape
@@ -589,7 +585,8 @@
     bands = pl.pallas_call(
         band_kernel,
         out_shape=tuple(
-            jax.ShapeDtypeStruct((9, r * SUB, 3 * DEPTH), jnp.float32) for r in (3, 2, 2, 2)
+            jax.ShapeDtypeStruct((9, r * SUB, 27 * depth), jnp.float32)
+            for r, depth in ((3, ROWS), (2, ROWS), (2, WINDOW), (2, WINDOW))
         ),
         in_specs=[smem],
         out_specs=(vmem,) * 4,
@@ -667,7 +664,7 @@
             pltpu.VMEM((3, tiles + 2 * LEAD, ROWS, LANES), f32),
             pltpu.VMEM((2, (total // 2 + 2 * LEAD) * 9 * SUB, 2 * LANES), f32),
             pltpu.VMEM((tiles + 2, 9 * ROWS, LANES), f32),
-            pltpu.VMEM((blocks, 3 * ROWS, LANES), f32),
+            pltpu.VMEM((blocks, 3 * ROWS + 2 * SUB, LANES), f32),
             pltpu.VMEM((3, tiles, ROWS, LANES), f32),
             pltpu.VMEM((3, 2 * tiles, 2 * SUB, LANES), f32),
             pltpu.VMEM((tiles + 2 * LEAD, ROWS, LANES), f32),

time: 22.6 us -> 22.3 us (0.987)
  waiting for transfers between devices: 7.83 us -> 7.21 us
  Pallas kernels: 5.98 us -> 6.28 us
    pallas_call x1, Pallas kernels: 1.06 us -> 1.68 us  [on_device(): pl.pallas_call(band_kernel, out_shape=tuple((jax.ShapeDtypeStruct((9, r *...]
    ppermute x4, waiting for transfers between devices: 4.69 us -> 4.07 us  [matched(): return lax.ppermute(block, axis, pairs)]
    pallas_call x1, Pallas kernels: 3.89 us -> 3.56 us  [on_device(): pl.pallas_call(functools.partial(cycle_kernel, planes, blocks, paired), o...]
  transfers between devices with their start and end apart: 5 -> 5, of which waited for: 4 -> 4; matrix products, arithmetic and copies ran while one was open for 0% -> 0% of each run, Pallas kernels for 5% -> 8%
where the time goes in v7:
time: 22.3 us; the launch traced here: 22.1 us
  starting transfers between devices  7.88 us (35%)
  waiting for transfers between devices  7.21 us (32%)
  Pallas kernels  6.28 us (28%)
  between operations  0.68 us (3%)
    ppermute x4, starting transfers between devices, matched(): return lax.ppermute(block, axis, pairs)  6.29 us
    ppermute x4, waiting for transfers between devices, matched(): return lax.ppermute(block, axis, pairs)  4.07 us
    pallas_call x1, Pallas kernels, on_device(): pl.pallas_call(functools.partial(cycle_kernel, planes, blocks, paired), o...  3.56 us
    ppermute x1, waiting for transfers between devices, on_device(): parts = [block, lax.ppermute(block, 'gx', [(0, 1), (1, 0)])]  3.14 us
    pallas_call x1, Pallas kernels, on_device(): pl.pallas_call(band_kernel, out_shape=tuple((jax.ShapeDtypeStruct((9, r *...  1.68 us
    ppermute x1, starting transfers between devices, on_device(): parts = [block, lax.ppermute(block, 'gx', [(0, 1), (1, 0)])]  1.58 us
    pallas_call x1, Pallas kernels, on_device(): pl.pallas_call(functools.partial(pack_kernel, planes), out_shape=(jax.Sha...  0.99 us
  transfers between devices with their start and end apart: 5, of which 4 were waited for; matrix products, arithmetic and copies ran while one was open for 0% of the time, Pallas kernels for 8%

profile of v7, /device:TPU:0, one launch (start us, length us, event | category | flops | bytes accessed | tf_op | source)
XLA Modules:
  0.0 22.1 jit_solution(4614700293879409887)
XLA Ops:
  0.6 1.0 %pack.1 = (f32[25,8,128]{2,1,0:T(8,128)S(1)}, f32[5,8,128]{2,1,0:T(8,128)S(1)}, f32[5,8,128]{2,1,0:T(8,128)S(1)}) custom-call(f32[8]{0:T(128)} %visc_hbm.1, f32[3,3,27]{2,1,0:T(4,128)} %bitcast.5, f32[3,4,8,128]{3,2,1,0:T(8,128)} %rhs_hbm.1, f32[4,8,128]{2,1,0:T(8,128)} %press_hbm.1, s32[4,8,128]{2,1,0:T(8,128)} %ids_hbm.1), custom_call_target="tpu_custom_call" | custom-call | tf_op jit(solution)/shard_map/pack/pallas_call | solution.py:596
  1.6 3.1 %collective-permute-start = (f32[5,8,128]{2,1,0:T(8,128)S(1)}, f32[5,8,128]{2,1,0:T(8,128)S(1)}, u32[]{:S(2)}, u32[]{:S(2)}) collective-permute-start(f32[5,8,128]{2,1,0:T(8,128)S(1)} %get-tuple-element.12), channel_id=1, source_target_pairs={{0,1},{1,0},{2,3},{3,2},{4,5},{5,4},{6,7},{7,6},{8,9},{9,8},{10,11... | collective-permute-start | bytes 61448 | tf_op jit(solution)/shard_map/ppermute | solution.py:67
  4.7 1.5 %collective-permute-start.1 = (f32[5,8,128]{2,1,0:T(8,128)S(1)}, f32[5,8,128]{2,1,0:T(8,128)S(1)}, u32[]{:S(2)}, u32[]{:S(2)}) collective-permute-start(f32[5,8,128]{2,1,0:T(8,128)S(1)} %get-tuple-element.13), channel_id=1, source_target_pairs={{1,2},{2,1},{17,18},{18,17},{0,16},{3,19},{16,0},{19,3},{5,6},{6,5... | collective-permute-start | bytes 61448 | tf_op jit(solution)/shard_map/ppermute | solution.py:67
  6.3 0.2 %collective-permute-done = f32[5,8,128]{2,1,0:T(8,128)S(1)} collective-permute-done((f32[5,8,128]{2,1,0:T(8,128)S(1)}, f32[5,8,128]{2,1,0:T(8,128)S(1)}, u32[]{:S(2)}, u32[]{:S(2)}) %collective-permute-start) | collective-permute-done | bytes 20512 | tf_op jit(solution)/shard_map/ppermute | solution.py:67
  6.5 2.0 %collective-permute-done.1 = f32[5,8,128]{2,1,0:T(8,128)S(1)} collective-permute-done((f32[5,8,128]{2,1,0:T(8,128)S(1)}, f32[5,8,128]{2,1,0:T(8,128)S(1)}, u32[]{:S(2)}, u32[]{:S(2)}) %collective-permute-start.1) | collective-permute-done | bytes 20512 | tf_op jit(solution)/shard_map/ppermute | solution.py:67
  8.5 1.6 %collective-permute-start.2 = (f32[25,8,128]{2,1,0:T(8,128)S(1)}, f32[25,8,128]{2,1,0:T(8,128)S(1)}, u32[]{:S(2)}, u32[]{:S(2)}) collective-permute-start(f32[25,8,128]{2,1,0:T(8,128)S(1)} %get-tuple-element.21.refs_0_), channel_id=1, source_target_pairs={{0,16},{16,0},{1,17},{17,1},{2,18},{18,2},{3,19},{19,3},{4,20},{20... | collective-permute-start | bytes 307208 | tf_op jit(solution)/shard_map/ppermute | solution.py:629
  10.1 3.1 %collective-permute-done.2.refs_1_ = f32[25,8,128]{2,1,0:T(8,128)S(1)} collective-permute-done((f32[25,8,128]{2,1,0:T(8,128)S(1)}, f32[25,8,128]{2,1,0:T(8,128)S(1)}, u32[]{:S(2)}, u32[]{:S(2)}) %collective-permute-start.2) | collective-permute-done | bytes 102432 | tf_op jit(solution)/shard_map/ppermute | solution.py:629
  13.3 0.1 collective-permute-start.3
  13.4 1.6 %collective-permute-start.4 = (f32[2,136,128]{2,1,0:T(8,128)S(1)}, f32[2,136,128]{2,1,0:T(8,128)S(1)}, u32[]{:S(2)}, u32[]{:S(2)}) collective-permute-start(f32[2,136,128]{2,1,0:T(8,128)S(1)} %get-tuple-element.15), channel_id=1, source_target_pairs={{4,8},{8,4},{20,24},{24,20},{0,16},{12,28},{16,0},{28,12},{5,9},{9... | collective-permute-start | bytes 417800 | tf_op jit(solution)/shard_map/ppermute | solution.py:67
  15.0 1.7 %bands.1 = (f32[9,24,648]{2,1,0:T(8,128)S(1)}, f32[9,16,648]{2,1,0:T(8,128)S(1)}, f32[9,16,432]{2,1,0:T(8,128)S(1)}, f32[9,16,432]{2,1,0:T(8,128)S(1)}) custom-call(f32[3,3,27]{2,1,0:T(4,128)} %bitcast.6), custom_call_target="tpu_custom_call" | custom-call | tf_op jit(solution)/shard_map/bands/pallas_call | solution.py:585
  16.7 0.0 collective-permute-done.3.a_ref
  16.7 1.8 %collective-permute-done.4.b_ref = f32[2,136,128]{2,1,0:T(8,128)S(1)} collective-permute-done((f32[2,136,128]{2,1,0:T(8,128)S(1)}, f32[2,136,128]{2,1,0:T(8,128)S(1)}, u32[]{:S(2)}, u32[]{:S(2)}) %collective-permute-start.4) | collective-permute-done | bytes 139296 | tf_op jit(solution)/shard_map/ppermute | solution.py:67
  18.5 3.6 %cycle.1 = (f32[3,4,8,128]{3,2,1,0:T(8,128)}, f32[4,8,128]{2,1,0:T(8,128)}) custom-call(f32[2,25,8,128]{3,2,1,0:T(8,128)S(1)} %pad_maximum_fusion.own_ref, f32[2,136,128]{2,1,0:T(8,128)S(1)} %collective-permute-done.3.a_ref, f32[2,136,128]{2,1,0:T(8,128)S(1)} %collective-permute-done.4.b_ref, f32[9,24,648]{2,1,0:T(8,128)S(1)} %get-tuple-element.16.smooth_ref, ...), custom_call_target="tpu_custom_call" | custom-call | tf_op jit(solution)/shard_map/cycle/pallas_call | solution.py:654
  (5 shorter events, 0.1 us)
Async XLA Ops:
  1.6 4.9 %collective-permute-start = (f32[5,8,128]{2,1,0:T(8,128)S(1)}, f32[5,8,128]{2,1,0:T(8,128)S(1)}, u32[]{:S(2)}, u32[]{:S(2)}) collective-permute-start(f32[5,8,128]{2,1,0:T(8,128)S(1)} %get-tuple-element.12), channel_id=1, source_target_pairs={{0,1},{1,0},{2,3},{3,2},{4,5},{5,4},{6,7},{7,6},{8,9},{9,8},{10,11... | collective-permute-start | bytes 61448 | tf_op jit(solution)/shard_map/ppermute | solution.py:67
  4.7 3.8 %collective-permute-start.1 = (f32[5,8,128]{2,1,0:T(8,128)S(1)}, f32[5,8,128]{2,1,0:T(8,128)S(1)}, u32[]{:S(2)}, u32[]{:S(2)}) collective-permute-start(f32[5,8,128]{2,1,0:T(8,128)S(1)} %get-tuple-element.13), channel_id=1, source_target_pairs={{1,2},{2,1},{17,18},{18,17},{0,16},{3,19},{16,0},{19,3},{5,6},{6,5... | collective-permute-start | bytes 61448 | tf_op jit(solution)/shard_map/ppermute | solution.py:67
  8.5 4.7 %collective-permute-start.2 = (f32[25,8,128]{2,1,0:T(8,128)S(1)}, f32[25,8,128]{2,1,0:T(8,128)S(1)}, u32[]{:S(2)}, u32[]{:S(2)}) collective-permute-start(f32[25,8,128]{2,1,0:T(8,128)S(1)} %get-tuple-element.21.refs_0_), channel_id=1, source_target_pairs={{0,16},{16,0},{1,17},{17,1},{2,18},{18,2},{3,19},{19,3},{4,20},{20... | collective-permute-start | bytes 307208 | tf_op jit(solution)/shard_map/ppermute | solution.py:629
  13.3 3.4 %collective-permute-start.3 = (f32[2,136,128]{2,1,0:T(8,128)S(1)}, f32[2,136,128]{2,1,0:T(8,128)S(1)}, u32[]{:S(2)}, u32[]{:S(2)}) collective-permute-start(f32[2,136,128]{2,1,0:T(8,128)S(1)} %get-tuple-element.14), channel_id=1, source_target_pairs={{0,4},{4,0},{8,12},{12,8},{1,5},{5,1},{9,13},{13,9},{2,6},{6,2},{1... | collective-permute-start | bytes 417800 | tf_op jit(solution)/shard_map/ppermute | solution.py:67
  13.4 5.1 %collective-permute-start.4 = (f32[2,136,128]{2,1,0:T(8,128)S(1)}, f32[2,136,128]{2,1,0:T(8,128)S(1)}, u32[]{:S(2)}, u32[]{:S(2)}) collective-permute-start(f32[2,136,128]{2,1,0:T(8,128)S(1)} %get-tuple-element.15), channel_id=1, source_target_pairs={{4,8},{8,4},{20,24},{24,20},{0,16},{12,28},{16,0},{28,12},{5,9},{9... | collective-permute-start | bytes 417800 | tf_op jit(solution)/shard_map/ppermute | solution.py:67
